TPU v7x, 128 devices: a whole 4x4x4 slice. The times are simulated.
128 devices in a mesh: mix: 4 (over z), span: 32 (over x, y, core).
Axes of the slice: x: 4, y: 4, z: 4, core: 2. Of those that a mesh axis runs over, the one named last changes fastest.
Arguments:
- mixture: bfloat16 [2048, 256, 256], P(('mix', 'span')), parts along dimension 0, may hold values from -16 to 16, as said below
- w_query: bfloat16 [2, 256, 256], replicated, may hold values from -4 to 4
- w_key: bfloat16 [2, 256, 256], replicated, may hold values from -4 to 4
- w_value: bfloat16 [2, 256, 256], replicated, may hold values from -0.375 to 0.375
- w_out: bfloat16 [2, 256, 256], replicated, may hold values from -0.375 to 0.375
- w_up: bfloat16 [2, 256, 1024], replicated, may hold values from -0.375 to 0.375
- w_down: bfloat16 [2, 1024, 256], replicated, may hold values from -0.1875 to 0.1875
- ln_gain: float32 [2, 2, 256], replicated, may hold values from 0.25 to 1.75
- gln_gain: float32 [2, 256], replicated, may hold values from 0.25 to 1.75
- gln_bias: float32 [2, 256], replicated, may hold values from -3 to 3
Outputs:
- block_out: bfloat16 [2048, 256, 256], P(('mix', 'span')), parts along dimension 0
There are 4 independent parts, one for each index of `mix`. A program takes and returns all parts, laid end to end along the dimension named above; an argument that names none is the same for every part. Nothing has to cross between parts.
Inputs may be any that keep to these rules, and one draw needn't show every extreme that they name: `mixture`: entries of order one, scaled by a factor per segment.
All inputs are finite; a program needn't handle non-finite values.
Results may differ from a plain program's by a relative error of at most 0.0057.
Values may be sent and summed in bfloat16 or wider, within the bound.
No kernel may reach another device: no remote copies, remote signals or barrier semaphores. Data moves between devices by JAX's collectives and lax.ppermute only.
A program may use at most 128 MiB of HBM per device.

v0:
```python
import math

import jax
import jax.numpy as jnp
from jax import lax
from jax.sharding import PartitionSpec as P

D = 256
HEADS = 8


norm_eps = 1e-05


def sent_to_all(array, axis):
    copies = jnp.broadcast_to(array, (lax.axis_size(axis), *array.shape))
    return lax.all_to_all(copies, axis, split_axis=0, concat_axis=0, tiled=True)


def taken_together(array, axis):
    return sent_to_all(array, axis).sum(axis=0)


def together(arrays, axis):
    flat, at, gathered = (jnp.concatenate([a.reshape(-1) for a in arrays]), 0, [])
    total = taken_together(flat, axis)
    for a in arrays:
        gathered.append(total[at : at + a.size].reshape(a.shape))
        at += a.size
    return tuple(gathered)


def pos_table(length, width):
    places = jnp.arange(length, dtype=jnp.float32)[:, None]
    column = jnp.arange(width)
    rates = jnp.exp(-(2 * (column // 2)).astype(jnp.float32) / width * math.log(10000.0))
    angles = places * rates[None, :]
    return jnp.where((column % 2 == 0)[None, :], jnp.sin(angles), jnp.cos(angles))


def norm_rows(rows, gain):
    center = jnp.mean(rows, axis=-1, keepdims=True)
    shifted = rows - center
    spread = jnp.mean(shifted * shifted, axis=-1, keepdims=True)
    return shifted * lax.rsqrt(spread + norm_eps) * gain


def group_width(count, length):
    best = 1
    for option in range(1, count + 1):
        if count % option == 0 and option * length <= max(512, length):
            best = option
    return best


def attend_block(queries, key_rows, values):
    head_dim = D // HEADS
    scores = jnp.einsum(
        "qbhd,kbhd->bhqk", queries, key_rows, preferred_element_type=jnp.float32
    ) / math.sqrt(head_dim)
    weights = jax.nn.softmax(scores, axis=-1).astype(jnp.bfloat16)
    context = jnp.einsum("bhqk,kbhd->qbhd", weights, values, preferred_element_type=jnp.float32)
    return context.astype(jnp.bfloat16)


def attend_along(queries, key_rows, values):
    length, count = (queries.shape[0], queries.shape[1])
    width = group_width(count, length)
    split_q = queries.reshape(length, count, HEADS, D // HEADS)
    split_k = key_rows.reshape(length, count, HEADS, D // HEADS)
    split_v = values.reshape(length, count, HEADS, D // HEADS)
    result = jnp.zeros(split_q.shape, jnp.bfloat16)

    def one_group(step, current):
        start = step * width
        block_q = lax.dynamic_slice_in_dim(split_q, start, width, 1)
        block_k = lax.dynamic_slice_in_dim(split_k, start, width, 1)
        block_v = lax.dynamic_slice_in_dim(split_v, start, width, 1)
        return lax.dynamic_update_slice_in_dim(
            current, attend_block(block_q, block_k, block_v), start, 1
        )

    result = lax.fori_loop(0, count // width, one_group, result)
    return result.reshape(length, count, D)


def encoder_layer(sequences, level, w_query, w_key, w_value, w_out, w_up, w_down, ln_gain):
    length, count = (sequences.shape[0], sequences.shape[1])
    inputs = sequences.astype(jnp.float32) + pos_table(length, D)[:, None, :]
    flat = inputs.reshape(length * count, D)
    normed = norm_rows(flat, ln_gain[level, 0]).astype(jnp.bfloat16)
    queries = jnp.dot(normed, w_query[level], preferred_element_type=jnp.float32).astype(
        jnp.bfloat16
    )
    key_rows = jnp.dot(normed, w_key[level], preferred_element_type=jnp.float32).astype(
        jnp.bfloat16
    )
    values = jnp.dot(normed, w_value[level], preferred_element_type=jnp.float32).astype(
        jnp.bfloat16
    )
    context = attend_along(
        queries.reshape(length, count, D),
        key_rows.reshape(length, count, D),
        values.reshape(length, count, D),
    )
    after_attn = flat + jnp.dot(
        context.reshape(length * count, D), w_out[level], preferred_element_type=jnp.float32
    )
    normed_two = norm_rows(after_attn, ln_gain[level, 1]).astype(jnp.bfloat16)
    hidden = jax.nn.relu(
        jnp.dot(normed_two, w_up[level], preferred_element_type=jnp.float32)
    ).astype(jnp.bfloat16)
    output = after_attn + jnp.dot(hidden, w_down[level], preferred_element_type=jnp.float32)
    return output.reshape(length, count, D)


def global_norm(rows, gain, bias, shards):
    cells_all = float(rows.size * shards)
    sums, squares = together((jnp.sum(rows), jnp.sum(rows * rows)), "span")
    center = sums / cells_all
    spread = squares / cells_all - center * center
    shifted = rows - center
    return gain * shifted * lax.rsqrt(spread + norm_eps) + bias


def body(mixture, w_query, w_key, w_value, w_out, w_up, w_down, ln_gain, gln_gain, gln_bias):
    shards = lax.axis_size("span")
    frames_first = jnp.swapaxes(mixture, 0, 1)
    intra_frames = encoder_layer(
        frames_first, 0, w_query, w_key, w_value, w_out, w_up, w_down, ln_gain
    )
    intra = jnp.swapaxes(intra_frames, 0, 1)
    intra_out = (
        global_norm(intra, gln_gain[0], gln_bias[0], shards) + mixture.astype(jnp.float32)
    ).astype(jnp.bfloat16)
    moved = lax.all_to_all(intra_out, "span", split_axis=1, concat_axis=0, tiled=True)
    inter = encoder_layer(moved, 1, w_query, w_key, w_value, w_out, w_up, w_down, ln_gain)
    final = (
        global_norm(inter, gln_gain[1], gln_bias[1], shards) + moved.astype(jnp.float32)
    ).astype(jnp.bfloat16)
    return lax.all_to_all(final, "span", split_axis=0, concat_axis=1, tiled=True)


def solution(mesh):
    in_specs = (P(("mix", "span"), None, None), P(), P(), P(), P(), P(), P(), P(), P(), P())
    out_specs = P(("mix", "span"), None, None)
    return jax.shard_map(body, mesh=mesh, in_specs=in_specs, out_specs=out_specs, check_vma=False)
```

profile of v0, /device:TPU:1, one launch (start us, length us, event | category | flops | bytes accessed | tf_op | source)
XLA Modules:
  0.0 493.9 jit_solution(6720231771606946138)
XLA Ops:
  7.4 5.4 %multiply_reduce_fusion.7 = f32[256,16]{1,0:T(8,128)S(1)} fusion(f32[256,16]{1,0:T(8,128)S(1)} %broadcast_multiply_fusion.1, f32[256,256]{1,0:T(8,128)S(1)} %cosine_select_fusion.1, bf16[16,256,256]{2,1,0:T(8,128)(2,1)S(1)} %copy-done.1), kind=kLoop, calls=%fused_computation.84 | loop fusion | flops 5238784 | bytes 2392064 | tf_op jit(solution)/shard_map/reduce_sum | solution.py:44
  19.2 10.0 %reshape_reshape.24 = bf16[256,16,8,32]{3,2,1,0:T(8,128)(2,1)} reshape(bf16[4096,256]{1,0:T(8,128)(2,1)} %convolution_convert_fusion.5) | data formatting | bytes 4194304 | tf_op jit(solution)/shard_map/reshape;reshape | solution.py:71
  29.2 10.0 %copy.52 = bf16[256,16,8,32]{0,3,2,1:T(8,128)(2,1)} copy(bf16[256,16,8,32]{3,2,1,0:T(8,128)(2,1)} %reshape_reshape.24) | data formatting | bytes 4194304 | tf_op jit(solution)/shard_map/while | solution.py:83
  41.2 10.0 %reshape_reshape.25 = bf16[256,16,8,32]{3,2,1,0:T(8,128)(2,1)} reshape(bf16[4096,256]{1,0:T(8,128)(2,1)} %convolution_convert_fusion.4) | data formatting | bytes 4194304 | tf_op jit(solution)/shard_map/reshape;reshape | solution.py:69
  51.2 10.0 %copy.53 = bf16[256,16,8,32]{0,3,2,1:T(8,128)(2,1)} copy(bf16[256,16,8,32]{3,2,1,0:T(8,128)(2,1)} %reshape_reshape.25) | data formatting | bytes 4194304 | tf_op jit(solution)/shard_map/while | solution.py:83
  63.3 10.0 %reshape_reshape.26 = bf16[256,16,8,32]{3,2,1,0:T(8,128)(2,1)} reshape(bf16[4096,256]{1,0:T(8,128)(2,1)} %convolution_convert_fusion.3) | data formatting | bytes 4194304 | tf_op jit(solution)/shard_map/reshape;reshape | solution.py:70
  73.3 10.0 %copy.54 = bf16[256,16,8,32]{0,3,2,1:T(8,128)(2,1)} copy(bf16[256,16,8,32]{3,2,1,0:T(8,128)(2,1)} %reshape_reshape.26) | data formatting | bytes 4194304 | tf_op jit(solution)/shard_map/while | solution.py:83
  83.5 58.2 %while.26 = (s32[]{:T(128)}, bf16[256,16,8,32]{0,3,2,1:T(8,128)(2,1)S(1)}, bf16[256,16,8,32]{0,3,2,1:T(8,128)(2,1)}, bf16[256,16,8,32]{0,3,2,1:T(8,128)(2,1)}, b...) while((s32[]{:T(128)}, bf16[256,16,8,32]{0,3,2,1:T(8,128)(2,1)S(1)}, ...), condition=%wide.region_5.6_spmd, body=%wide.region_2.5_spmd.sunk | while | flops 139591936 | bytes 9472139 | solution.py:83
  83.7 4.5 fusion.178
  91.0 4.5 fusion.178
  98.2 4.5 fusion.178
  105.5 4.5 fusion.178
  112.7 4.5 fusion.178
  120.0 4.5 fusion.178
  127.2 4.5 fusion.178
  134.5 4.5 fusion.178
  141.7 12.0 %copy.55 = bf16[256,16,8,32]{3,2,1,0:T(8,128)(2,1)} copy(bf16[256,16,8,32]{0,3,2,1:T(8,128)(2,1)S(1)} %get-tuple-element.193) | data formatting | bytes 4194304 | tf_op jit(solution)/shard_map/while | solution.py:83
  153.7 9.8 %reshape_reshape.27 = bf16[4096,256]{1,0:T(8,128)(2,1)S(1)} reshape(bf16[256,16,8,32]{3,2,1,0:T(8,128)(2,1)} %copy.55) | data formatting | bytes 4194304 | tf_op jit(solution)/shard_map/reshape;reshape | solution.py:107
  170.0 10.3 %fusion.130 = (f32[]{:T(128)}, f32[]{:T(128)}, f32[4096,256]{1,0:T(8,128)}) fusion(f32[4096,256]{1,0:T(8,128)} %copy-done.4, bf16[2,1024,256]{2,1,0:T(8,128)(2,1)S(1)} %copy-done.17, f32[256]{0:T(256)S(1)} %bitcast.202, f32[4096]{0:T(1024)S(1)} %add_rsqrt_fusion.3, f32[4096]{0:T(1024)S(1)} %broadcast_multiply_fusion.3, bf16[2,256,1024]{2,1,0:T(8,128)(2,1)S(1)} %copy-done.19), kind=kOutput, calls=%fused_computation.152 | convolution fusion | flops 4311744512 | bytes 13665288 | tf_op jit(solution)/shard_map/dot_general | solution.py:113
  182.1 8.6 %all-to-all-start = ((f32[32,1,2]{2,1,0:T(1,128)}), f32[32,1,2]{2,1,0:T(1,128)S(1)}, u32[]{:S(2)}, u32[]{:S(2)}) async-start(f32[32,1,2]{2,1,0:T(1,128)} %broadcast_in_dim.62), calls=%async_computation | async-start | bytes 32768 | tf_op jit(solution)/shard_map/all_to_all | solution.py:17
  190.8 6.9 %all-to-all-done = f32[32,1,2]{2,1,0:T(1,128)S(1)} async-done(((f32[32,1,2]{2,1,0:T(1,128)}), f32[32,1,2]{2,1,0:T(1,128)S(1)}, u32[]{:S(2)}, u32[]{:S(2)}) %all-to-all-start) | async-done | bytes 288 | tf_op jit(solution)/shard_map/all_to_all | solution.py:17
  206.7 4.6 all-to-all-start.1
  215.2 24.4 %all-to-all-done.1 = bf16[16,256,256]{2,0,1:T(8,128)(2,1)S(1)} async-done(((bf16[16,256,256]{2,0,1:T(8,128)(2,1)}), bf16[16,256,256]{2,0,1:T(8,128)(2,1)S(1)}, u32[]{:S(2)}, u32[]{:S(2)}) %all-to-all-start.1) | async-done | bytes 2097184 | tf_op jit(solution)/shard_map/all_to_all | solution.py:136
  257.5 10.0 %reshape_reshape.28 = bf16[512,8,8,32]{3,2,1,0:T(8,128)(2,1)} reshape(bf16[4096,256]{1,0:T(8,128)(2,1)} %convolution_convert_fusion.2) | data formatting | bytes 4194304 | tf_op jit(solution)/shard_map/reshape;reshape | solution.py:71
  267.5 9.3 %copy.58 = bf16[512,8,8,32]{0,3,2,1:T(8,128)(2,1)} copy(bf16[512,8,8,32]{3,2,1,0:T(8,128)(2,1)} %reshape_reshape.28) | data formatting | bytes 4194304 | tf_op jit(solution)/shard_map/while | solution.py:83
  276.8 10.0 %reshape_reshape.29 = bf16[512,8,8,32]{3,2,1,0:T(8,128)(2,1)} reshape(bf16[4096,256]{1,0:T(8,128)(2,1)} %convolution_convert_fusion.1) | data formatting | bytes 4194304 | tf_op jit(solution)/shard_map/reshape;reshape | solution.py:69
  286.8 9.3 %copy.59 = bf16[512,8,8,32]{0,3,2,1:T(8,128)(2,1)} copy(bf16[512,8,8,32]{3,2,1,0:T(8,128)(2,1)} %reshape_reshape.29) | data formatting | bytes 4194304 | tf_op jit(solution)/shard_map/while | solution.py:83
  296.1 6.2 %reshape_reshape.30 = bf16[512,8,8,32]{3,2,1,0:T(8,128)(2,1)} reshape(bf16[4096,256]{1,0:T(8,128)(2,1)S(1)} %convolution_convert_fusion) | data formatting | bytes 4194304 | tf_op jit(solution)/shard_map/reshape;reshape | solution.py:70
  302.3 9.5 %copy.60 = bf16[512,8,8,32]{0,3,2,1:T(8,128)(2,1)} copy(bf16[512,8,8,32]{3,2,1,0:T(8,128)(2,1)} %reshape_reshape.30) | data formatting | bytes 4194304 | tf_op jit(solution)/shard_map/while | solution.py:83
  311.8 90.4 %while.27 = (s32[]{:T(128)}, bf16[512,8,8,32]{0,3,2,1:T(8,128)(2,1)S(1)}, bf16[512,8,8,32]{0,3,2,1:T(8,128)(2,1)}, bf16[512,8,8,32]{0,3,2,1:T(8,128)(2,1)}, bf16[512,8,8,32]{0,3,2,1:T(8,128)(2,1)}, /*index=5*/s32[]{:T(128)}) while((s32[]{:T(128)}, bf16[512,8,8,32]{0,3,2,1:T(8,128)(2,1)S(1)}, bf16[512,8,8,32]{0,3,2,1:T(8,128)(2,1)}, ...), condition=%wide.region_16.17_spmd, body=%wide.region_13.16_spmd.sunk | while | flops 279052800 | bytes 17860676 | solution.py:83
  311.8 7.0 %fusion.183 = (f32[8,512]{1,0:T(8,128)S(1)}, f32[8,512,512]{1,2,0:T(8,128)}) fusion(bf16[512,8,8,32]{0,3,2,1:T(8,128)(2,1)} %get-tuple-element.394, s32[]{:T(128)} %get-tuple-element.384, bf16[512,8,8,32]{0,3,2,1:T(8,128)(2,1)} %get-tuple-element.393), kind=kOutput, calls=%fused_computation.154.clone.1 | convolution fusion | flops 140509696 | bytes 8930304 | tf_op jit(solution)/shard_map/while/body/eval_jaxpr/sub | solution.py:61
  318.8 4.3 fusion.184
  323.1 7.0 %fusion.183 = (f32[8,512]{1,0:T(8,128)S(1)}, f32[8,512,512]{1,2,0:T(8,128)}) fusion(bf16[512,8,8,32]{0,3,2,1:T(8,128)(2,1)} %get-tuple-element.394, s32[]{:T(128)} %get-tuple-element.384, bf16[512,8,8,32]{0,3,2,1:T(8,128)(2,1)} %get-tuple-element.393), kind=kOutput, calls=%fused_computation.154.clone.1 | convolution fusion | flops 140509696 | bytes 8930304 | tf_op jit(solution)/shard_map/while/body/eval_jaxpr/sub | solution.py:61
  330.1 4.3 fusion.184
  334.4 7.0 %fusion.183 = (f32[8,512]{1,0:T(8,128)S(1)}, f32[8,512,512]{1,2,0:T(8,128)}) fusion(bf16[512,8,8,32]{0,3,2,1:T(8,128)(2,1)} %get-tuple-element.394, s32[]{:T(128)} %get-tuple-element.384, bf16[512,8,8,32]{0,3,2,1:T(8,128)(2,1)} %get-tuple-element.393), kind=kOutput, calls=%fused_computation.154.clone.1 | convolution fusion | flops 140509696 | bytes 8930304 | tf_op jit(solution)/shard_map/while/body/eval_jaxpr/sub | solution.py:61
  341.4 4.3 fusion.184
  345.7 7.0 %fusion.183 = (f32[8,512]{1,0:T(8,128)S(1)}, f32[8,512,512]{1,2,0:T(8,128)}) fusion(bf16[512,8,8,32]{0,3,2,1:T(8,128)(2,1)} %get-tuple-element.394, s32[]{:T(128)} %get-tuple-element.384, bf16[512,8,8,32]{0,3,2,1:T(8,128)(2,1)} %get-tuple-element.393), kind=kOutput, calls=%fused_computation.154.clone.1 | convolution fusion | flops 140509696 | bytes 8930304 | tf_op jit(solution)/shard_map/while/body/eval_jaxpr/sub | solution.py:61
  352.7 4.3 fusion.184
  357.0 7.0 %fusion.183 = (f32[8,512]{1,0:T(8,128)S(1)}, f32[8,512,512]{1,2,0:T(8,128)}) fusion(bf16[512,8,8,32]{0,3,2,1:T(8,128)(2,1)} %get-tuple-element.394, s32[]{:T(128)} %get-tuple-element.384, bf16[512,8,8,32]{0,3,2,1:T(8,128)(2,1)} %get-tuple-element.393), kind=kOutput, calls=%fused_computation.154.clone.1 | convolution fusion | flops 140509696 | bytes 8930304 | tf_op jit(solution)/shard_map/while/body/eval_jaxpr/sub | solution.py:61
  364.0 4.3 fusion.184
  368.3 7.0 %fusion.183 = (f32[8,512]{1,0:T(8,128)S(1)}, f32[8,512,512]{1,2,0:T(8,128)}) fusion(bf16[512,8,8,32]{0,3,2,1:T(8,128)(2,1)} %get-tuple-element.394, s32[]{:T(128)} %get-tuple-element.384, bf16[512,8,8,32]{0,3,2,1:T(8,128)(2,1)} %get-tuple-element.393), kind=kOutput, calls=%fused_computation.154.clone.1 | convolution fusion | flops 140509696 | bytes 8930304 | tf_op jit(solution)/shard_map/while/body/eval_jaxpr/sub | solution.py:61
  379.6 7.0 %fusion.183 = (f32[8,512]{1,0:T(8,128)S(1)}, f32[8,512,512]{1,2,0:T(8,128)}) fusion(bf16[512,8,8,32]{0,3,2,1:T(8,128)(2,1)} %get-tuple-element.394, s32[]{:T(128)} %get-tuple-element.384, bf16[512,8,8,32]{0,3,2,1:T(8,128)(2,1)} %get-tuple-element.393), kind=kOutput, calls=%fused_computation.154.clone.1 | convolution fusion | flops 140509696 | bytes 8930304 | tf_op jit(solution)/shard_map/while/body/eval_jaxpr/sub | solution.py:61
  390.9 7.0 %fusion.183 = (f32[8,512]{1,0:T(8,128)S(1)}, f32[8,512,512]{1,2,0:T(8,128)}) fusion(bf16[512,8,8,32]{0,3,2,1:T(8,128)(2,1)} %get-tuple-element.394, s32[]{:T(128)} %get-tuple-element.384, bf16[512,8,8,32]{0,3,2,1:T(8,128)(2,1)} %get-tuple-element.393), kind=kOutput, calls=%fused_computation.154.clone.1 | convolution fusion | flops 140509696 | bytes 8930304 | tf_op jit(solution)/shard_map/while/body/eval_jaxpr/sub | solution.py:61
  402.2 12.0 %copy.61 = bf16[512,8,8,32]{3,2,1,0:T(8,128)(2,1)} copy(bf16[512,8,8,32]{0,3,2,1:T(8,128)(2,1)S(1)} %get-tuple-element.194) | data formatting | bytes 4194304 | tf_op jit(solution)/shard_map/while | solution.py:83
  414.2 9.9 %reshape_reshape.31 = bf16[4096,256]{1,0:T(8,128)(2,1)S(1)} reshape(bf16[512,8,8,32]{3,2,1,0:T(8,128)(2,1)} %copy.61) | data formatting | bytes 4194304 | tf_op jit(solution)/shard_map/reshape;reshape | solution.py:107
  430.6 10.3 %fusion.129 = (f32[]{:T(128)}, f32[]{:T(128)}, f32[4096,256]{1,0:T(8,128)}) fusion(f32[4096,256]{1,0:T(8,128)} %copy-done.3, bf16[2,1024,256]{2,1,0:T(8,128)(2,1)S(1)} %copy-done.18, f32[256]{0:T(256)S(1)} %bitcast.201, f32[4096]{0:T(1024)S(1)} %add_rsqrt_fusion.2, f32[4096]{0:T(1024)S(1)} %broadcast_multiply_fusion.2, bf16[2,256,1024]{2,1,0:T(8,128)(2,1)S(1)} %copy-done.20), kind=kOutput, calls=%fused_computation.151 | convolution fusion | flops 4311744512 | bytes 13665288 | tf_op jit(solution)/shard_map/dot_general | solution.py:113
  442.2 10.6 %all_to_all.39 = f32[32,1,2]{2,1,0:T(1,128)S(1)} all-to-all(f32[32,1,2]{2,1,0:T(1,128)S(1)} %broadcast_in_dim.66), channel_id=1, replica_groups=mesh['mix'=4,'span'=32] {'span'}, dimensions={0} | all-to-all | bytes 512 | tf_op jit(solution)/shard_map/all_to_all | solution.py:17
  460.3 31.9 %all_to_all.40 = bf16[512,8,256]{2,1,0:T(8,128)(2,1)S(1)} all-to-all(bf16[512,8,256]{2,1,0:T(8,128)(2,1)S(1)} %fusion.72), channel_id=1, replica_groups=mesh['mix'=4,'span'=32] {'span'}, dimensions={0} | all-to-all | bytes 4194304 | tf_op jit(solution)/shard_map/all_to_all | solution.py:141
  (103 shorter events, 103.6 us)
Async XLA Ops:
  0.0 4.0 copy-start.1
  4.0 8.9 %copy-start.13 = (f32[2,2,256]{2,1,0:T(2,128)S(1)}, f32[2,2,256]{2,1,0:T(2,128)}, u32[]{:S(2)}) copy-start(f32[2,2,256]{2,1,0:T(2,128)} %param.21) | copy-start | bytes 12292
  7.4 9.7 %copy-start.6 = (bf16[2,256,256]{2,1,0:T(8,128)(2,1)S(1)}, bf16[2,256,256]{2,1,0:T(8,128)(2,1)}, u32[]{:S(2)}) copy-start(bf16[2,256,256]{2,1,0:T(8,128)(2,1)} %param.17) | copy-start | bytes 786436
  29.1 10.0 %copy-start.7 = (bf16[2,256,256]{2,1,0:T(8,128)(2,1)S(1)}, bf16[2,256,256]{2,1,0:T(8,128)(2,1)}, u32[]{:S(2)}) copy-start(bf16[2,256,256]{2,1,0:T(8,128)(2,1)} %param.15) | copy-start | bytes 786436
  51.2 10.0 %copy-start.9 = (bf16[2,256,256]{2,1,0:T(8,128)(2,1)S(1)}, bf16[2,256,256]{2,1,0:T(8,128)(2,1)}, u32[]{:S(2)}) copy-start(bf16[2,256,256]{2,1,0:T(8,128)(2,1)} %param.16) | copy-start | bytes 786436
  153.7 9.8 %copy-start.11 = (bf16[2,256,256]{2,1,0:T(8,128)(2,1)S(1)}, bf16[2,256,256]{2,1,0:T(8,128)(2,1)}, u32[]{:S(2)}) copy-start(bf16[2,256,256]{2,1,0:T(8,128)(2,1)} %param.18) | copy-start | bytes 786436
  166.5 2.1 copy-start.4
  166.5 3.5 copy-start.17
  166.5 3.5 copy-start.19
  170.0 20.8 %copy-start.14 = (f32[2,256]{1,0:T(2,128)S(1)}, f32[2,256]{1,0:T(2,128)}, u32[]{:S(2)}) copy-start(f32[2,256]{1,0:T(2,128)} %param.23) | copy-start | bytes 6148
  170.0 20.8 %copy-start.15 = (f32[2,256]{1,0:T(2,128)S(1)}, f32[2,256]{1,0:T(2,128)}, u32[]{:S(2)}) copy-start(f32[2,256]{1,0:T(2,128)} %param.22) | copy-start | bytes 6148
  182.1 15.5 %all-to-all-start = ((f32[32,1,2]{2,1,0:T(1,128)}), f32[32,1,2]{2,1,0:T(1,128)S(1)}, u32[]{:S(2)}, u32[]{:S(2)}) async-start(f32[32,1,2]{2,1,0:T(1,128)} %broadcast_in_dim.62), calls=%async_computation | async-start | bytes 32768 | tf_op jit(solution)/shard_map/all_to_all | solution.py:17
  200.8 2.9 copy-start.2
  206.7 32.9 %all-to-all-start.1 = ((bf16[16,256,256]{2,0,1:T(8,128)(2,1)}), bf16[16,256,256]{2,0,1:T(8,128)(2,1)S(1)}, u32[]{:S(2)}, u32[]{:S(2)}) async-start(bf16[16,256,256]{2,0,1:T(8,128)(2,1)} %fusion.67), calls=%async_computation.1 | async-start | bytes 4194304 | tf_op jit(solution)/shard_map/all_to_all | solution.py:136
  247.3 7.5 %copy-start = (f32[16,32,8,256]{3,2,0,1:T(8,128)}, f32[16,32,8,256]{3,2,0,1:T(8,128)S(1)}, u32[]{:S(2)}) copy-start(f32[16,32,8,256]{3,2,0,1:T(8,128)S(1)} %copy.57) | copy-start | bytes 12582916
  250.0 2.0 copy-start.8
  252.0 2.1 copy-start.10
  302.3 9.5 %copy-start.5 = (bf16[512,8,8,32]{0,3,2,1:T(8,128)(2,1)S(1)}, bf16[512,8,8,32]{0,3,2,1:T(8,128)(2,1)}, u32[]{:S(2)}) copy-start(bf16[512,8,8,32]{0,3,2,1:T(8,128)(2,1)} %custom-call) | copy-start | bytes 6291460
  414.2 9.9 %copy-start.12 = (bf16[2,256,256]{2,1,0:T(8,128)(2,1)S(1)}, bf16[2,256,256]{2,1,0:T(8,128)(2,1)}, u32[]{:S(2)}) copy-start(bf16[2,256,256]{2,1,0:T(8,128)(2,1)} %param.18) | copy-start | bytes 786436
  427.1 2.1 copy-start.3
  427.1 3.5 copy-start.16
  427.1 3.5 copy-start.18
  427.1 3.5 copy-start.20
where the time goes:
time: 501 us; the launch traced here: 494 us
  matrix products  186 us (37%)
  local copies, waits for them, and re-layouts  168 us (34%)
  other arithmetic  47.5 us (9%)
  blocking collectives  42.5 us (8%)
  waiting for transfers between devices  31.3 us (6%)
  starting transfers between devices  13.2 us (3%)
  between operations  5.78 us (1%)
    sub x16, matrix products, attend_block(): weights = jax.nn.softmax(scores, axis=-1).astype(jnp.bfloat16)  91.8 us
    while x8, local copies, waits for them, and re-layouts, attend_along(): result = lax.fori_loop(0, count // width, one_group, result)  82.1 us
    dot_general x16, matrix products, attend_block(): jnp.einsum('bhqk,kbhd->qbhd', weights, values, preferred_element_type=jnp...  56.4 us
    all_to_all x1, blocking collectives, body(): lax.all_to_all(final, 'span', split_axis=0, concat_axis=1, tiled=True)  31.9 us
    all_to_all x1, waiting for transfers between devices, body(): lax.all_to_all(intra_out, 'span', split_axis=1, concat_axis=0, tiled=True)  24.4 us
    dot_general x2, matrix products, encoder_layer(): jnp.dot(hidden, w_down[level], preferred_element_type=jnp.float32)  20.5 us
    another operation x2, local copies, waits for them, and re-layouts, attend_along(): split_v = values.reshape(length, count, HEADS, D // HEADS)  20 us
    another operation x2, local copies, waits for them, and re-layouts, attend_along(): split_q = queries.reshape(length, count, HEADS, D // HEADS)  20 us
  transfers between devices with their start and end apart: 2, of which 2 were waited for; matrix products, arithmetic and copies ran while one was open for 1% of the time, Pallas kernels for 0%

commit v1 on v0

v1 whole, which is shorter than its diff:
```python
import functools
import math

import jax
import jax.numpy as jnp
from jax import lax
from jax.experimental import pallas as pl
from jax.experimental.pallas import tpu as pltpu
from jax.sharding import PartitionSpec as P

D = 256
HEADS = 8
HD = D // HEADS
FF = 1024
EPS = 1e-05
AUG = HD + 16
F32 = jnp.float32
BF16 = jnp.bfloat16


def pos_table_t(length):
    places = jnp.arange(length, dtype=F32)[None, :]
    column = jnp.arange(D)
    rates = jnp.exp(-(2 * (column // 2)).astype(F32) / D * math.log(10000.0))
    angles = places * rates[:, None]
    return jnp.where((column % 2 == 0)[:, None], jnp.sin(angles), jnp.cos(angles))


def dot(a, b):
    return lax.dot_general(a, b, (((1,), (0,)), ((), ())), preferred_element_type=F32)


def norm_cols(x, gain):
    center = jnp.mean(x, axis=0, keepdims=True)
    shifted = x - center
    spread = jnp.mean(shifted * shifted, axis=0, keepdims=True)
    return shifted * lax.rsqrt(spread + EPS) * gain


def layer_body(xt, g1, g2, wq_t, w_k, wv_t, wo_t, wup_t, wdn_t, vaug, ctx):
    length = xt.shape[1]
    chunk = 256
    normed = norm_cols(xt, g1).astype(BF16)
    scale = math.log2(math.e) / math.sqrt(HD)
    q_t = (dot(wq_t, normed) * scale).astype(BF16)
    v_t = dot(wv_t, normed).astype(BF16)
    keys = dot(normed.T, w_k).astype(BF16)
    for h in range(HEADS):
        vaug[h * AUG : h * AUG + HD, :] = v_t[h * HD : (h + 1) * HD, :]
    for c in range(length // chunk):
        lanes = slice(c * chunk, (c + 1) * chunk)
        for h in range(HEADS):
            block, at = divmod(h * HD, 128)
            parts = []
            if at:
                parts.append(jnp.zeros((at, chunk), BF16))
            parts.append(q_t[h * HD : (h + 1) * HD, lanes])
            if at + HD < 128:
                parts.append(jnp.zeros((128 - at - HD, chunk), BF16))
            q_pad = jnp.concatenate(parts, axis=0)
            scores = dot(keys[:, block * 128 : (block + 1) * 128], q_pad)
            top = jnp.max(scores, axis=0, keepdims=True)
            weights = jnp.exp2(scores - top).astype(BF16)
            mixed = dot(vaug[h * AUG : (h + 1) * AUG, :], weights)
            ctx[h * HD : (h + 1) * HD, lanes] = (
                mixed[:HD, :] * (1.0 / mixed[HD : HD + 1, :])
            ).astype(BF16)
    after = xt + dot(wo_t, ctx[...])
    normed_two = norm_cols(after, g2).astype(BF16)
    hidden = jnp.maximum(dot(wup_t, normed_two), 0.0).astype(BF16)
    return after + dot(wdn_t, hidden)


def layer_kernel(x_ref, pos_ref, g1_ref, g2_ref, wq_ref, wk_ref, wv_ref, wo_ref, wup_ref, wdn_ref,
                 y_ref, stat_ref, wq_t, wv_t, wo_t, wup_t, wdn_t, vaug, ctx):
    length = pos_ref.shape[1]

    @pl.when(pl.program_id(0) == 0)
    def _():
        wq_t[...] = wq_ref[...].T
        wv_t[...] = wv_ref[...].T
        wo_t[...] = wo_ref[...].T
        wup_t[...] = wup_ref[...].T
        wdn_t[...] = wdn_ref[...].T
        vaug[...] = jnp.ones_like(vaug)
        stat_ref[...] = jnp.zeros_like(stat_ref)

    x = x_ref[...].reshape(length, D)
    xt = x.T.astype(F32) + pos_ref[...]
    y_t = layer_body(xt, g1_ref[...], g2_ref[...], wq_t[...], wk_ref[...], wv_t[...], wo_t[...],
                     wup_t[...], wdn_t[...], vaug, ctx)
    part = y_t.reshape(D // 8, 8, length)
    stat_ref[0] += jnp.sum(part, axis=0)
    stat_ref[1] += jnp.sum(part * part, axis=0)
    y_ref[...] = y_t.astype(BF16).T.reshape(y_ref.shape)


def layer(x, steps, x_block, x_map, length, pos, g1, g2, w_q, w_k, w_v, w_o, w_u, w_d, name):
    whole = lambda a: pl.BlockSpec(a.shape, lambda i: (0,) * a.ndim)
    consts = (pos, g1, g2, w_q, w_k, w_v, w_o, w_u, w_d)
    return pl.pallas_call(
        layer_kernel,
        grid=(steps,),
        in_specs=[pl.BlockSpec(x_block, x_map)] + [whole(a) for a in consts],
        out_specs=[pl.BlockSpec(x_block, x_map), pl.BlockSpec((2, 8, length), lambda i: (0, 0, 0))],
        out_shape=[jax.ShapeDtypeStruct(x.shape, BF16), jax.ShapeDtypeStruct((2, 8, length), F32)],
        scratch_shapes=[
            pltpu.VMEM((D, D), BF16), pltpu.VMEM((D, D), BF16), pltpu.VMEM((D, D), BF16),
            pltpu.VMEM((FF, D), BF16), pltpu.VMEM((D, FF), BF16),
            pltpu.VMEM((HEADS * AUG, length), BF16), pltpu.VMEM((D, length), BF16),
        ],
        compiler_params=pltpu.CompilerParams(dimension_semantics=("arbitrary",)),
        name=name,
    )(x, *consts)


def shared_stats(stat, cells):
    mine = jnp.sum(stat, axis=(1, 2))
    copies = jnp.broadcast_to(mine[None, None, :], (lax.axis_size("span"), 1, 2))
    total = lax.all_to_all(copies, "span", split_axis=0, concat_axis=0, tiled=True).sum(axis=(0, 1))
    center = total[0] / cells
    spread = total[1] / cells - center * center
    return center, lax.rsqrt(spread + EPS)


def body(mixture, w_query, w_key, w_value, w_out, w_up, w_down, ln_gain, gln_gain, gln_bias):
    shards = lax.axis_size("span")
    segs, frames, _ = mixture.shape
    own = frames // shards
    total = segs * shards
    cells = float(total * frames * D)
    weights = lambda l: (w_query[l], w_key[l], w_value[l], w_out[l], w_up[l], w_down[l])
    gains = lambda l: (ln_gain[l, 0][:, None], ln_gain[l, 1][:, None])

    intra, stat = layer(mixture, segs, (1, frames, D), lambda i: (i, 0, 0), frames,
                        pos_table_t(frames), *gains(0), *weights(0), name="intra")
    center, inv = shared_stats(stat, cells)
    intra_out = (gln_gain[0] * (intra.astype(F32) - center) * inv + gln_bias[0]
                 + mixture.astype(F32)).astype(BF16)
    by_frame = jnp.swapaxes(intra_out, 0, 1).reshape(shards, own, segs, D)
    moved = lax.all_to_all(by_frame, "span", split_axis=0, concat_axis=0, tiled=True)

    inter, stat = layer(moved, own, (shards, 1, segs, D), lambda i: (0, i, 0, 0), total,
                        pos_table_t(total), *gains(1), *weights(1), name="inter")
    center, inv = shared_stats(stat, cells)
    back = lax.all_to_all(inter, "span", split_axis=0, concat_axis=0, tiled=True)
    back = back.reshape(frames, segs, D)
    final = (gln_gain[1] * (back.astype(F32) - center) * inv + gln_bias[1]
             + jnp.swapaxes(intra_out, 0, 1).astype(F32)).astype(BF16)
    return jnp.swapaxes(final, 0, 1)


def solution(mesh):
    in_specs = (P(("mix", "span"), None, None), P(), P(), P(), P(), P(), P(), P(), P(), P())
    out_specs = P(("mix", "span"), None, None)
    return jax.shard_map(body, mesh=mesh, in_specs=in_specs, out_specs=out_specs, check_vma=False)
```

time: 501 us -> 244 us (0.49); the launches traced: 494 us -> 244 us
  matrix products: 186 us -> 0 us
  local copies, waits for them, and re-layouts: 168 us -> 14.4 us
  Pallas kernels: 0 us -> 123 us
  blocking collectives: 42.5 us -> 10.6 us
  other arithmetic: 47.5 us -> 15.9 us
  waiting for transfers between devices: 31.3 us -> 56.2 us
  starting transfers between devices: 13.2 us -> 18.6 us
    pallas_call x0 -> x2, Pallas kernels: none -> 123 us  [layer(): pl.pallas_call(layer_kernel, grid=(steps,), in_specs=[pl.BlockSpec(x_bloc...]
    dot_general x26 -> x0, matrix products: 93.9 us -> none  [the longest x16 56.4 us: attend_block(): jnp.einsum('bhqk,kbhd->qbhd', weights, values, preferred_element_type=jnp...]
    sub x16 -> x0, matrix products: 91.8 us -> none  [attend_block(): weights = jax.nn.softmax(scores, axis=-1).astype(jnp.bfloat16)]
    while x8 -> x0, local copies, waits for them, and re-layouts: 82.1 us -> none  [attend_along(): result = lax.fori_loop(0, count // width, one_group, result)]
    another operation x8 -> x5, local copies, waits for them, and re-layouts: 75.8 us -> 4 us  [body(): gains = lambda l: (ln_gain[l, 0][:, None], ln_gain[l, 1][:, None])]
    all_to_all x2 -> x1, blocking collectives: 42.5 us -> 10.6 us  [shared_stats(): lax.all_to_all(copies, 'span', split_axis=0, concat_axis=0, tiled=True)]
    all_to_all x2 -> x3, waiting for transfers between devices: 31.3 us -> 56.2 us  [the longest x1 25.4 us: body(): lax.all_to_all(inter, 'span', split_axis=0, concat_axis=0, tiled=True)]
    reduce_sum x8 -> x4, other arithmetic: 17.1 us -> 1.77 us  [the longest x2 1.67 us: shared_stats(): mine = jnp.sum(stat, axis=(1, 2))]
  transfers between devices with their start and end apart: 2 -> 3, of which waited for: 2 -> 3; matrix products, arithmetic and copies ran while one was open for 1% -> 2% of each run, Pallas kernels for 0% -> 0%
where the time goes in v1:
time: 244 us
  Pallas kernels  123 us (50%)
  waiting for transfers between devices  56.2 us (23%)
  starting transfers between devices  18.6 us (8%)
  other arithmetic  15.9 us (7%)
  local copies, waits for them, and re-layouts  14.4 us (6%)
  blocking collectives  10.6 us (4%)
  between operations  5.16 us (2%)
    pallas_call x2, Pallas kernels, layer(): pl.pallas_call(layer_kernel, grid=(steps,), in_specs=[pl.BlockSpec(x_bloc...  123 us
    all_to_all x1, waiting for transfers between devices, body(): lax.all_to_all(inter, 'span', split_axis=0, concat_axis=0, tiled=True)  25.4 us
    all_to_all x1, waiting for transfers between devices, body(): lax.all_to_all(by_frame, 'span', split_axis=0, concat_axis=0, tiled=True)  23.9 us
    all_to_all x1, blocking collectives, shared_stats(): lax.all_to_all(copies, 'span', split_axis=0, concat_axis=0, tiled=True)  10.6 us
    all_to_all x1, starting transfers between devices, shared_stats(): lax.all_to_all(copies, 'span', split_axis=0, concat_axis=0, tiled=True)  8.58 us
    all_to_all x1, waiting for transfers between devices, shared_stats(): lax.all_to_all(copies, 'span', split_axis=0, concat_axis=0, tiled=True)  6.93 us
    all_to_all x1, starting transfers between devices, body(): lax.all_to_all(by_frame, 'span', split_axis=0, concat_axis=0, tiled=True)  5.01 us
    all_to_all x1, starting transfers between devices, body(): lax.all_to_all(inter, 'span', split_axis=0, concat_axis=0, tiled=True)  5 us
  transfers between devices with their start and end apart: 3, of which 3 were waited for; matrix products, arithmetic and copies ran while one was open for 2% of the time, Pallas kernels for 0%

profile of v1, /device:TPU:1, one launch (start us, length us, event | category | flops | bytes accessed | tf_op | source)
XLA Modules:
  0.0 243.7 jit_solution(1627020205297679724)
XLA Ops:
  0.0 0.0 copy-start
  0.0 0.0 copy-start.1
  0.0 0.0 copy-start.2
  0.0 0.0 copy-start.3
  0.0 0.8 slice_bitcast_fusion.12
  0.9 0.8 copy.26.g2_ref
  1.7 0.8 copy.25.g1_ref
  2.4 2.3 slice_bitcast_fusion.1
  4.7 0.0 copy-start.4
  4.7 0.0 copy-start.5
  4.7 2.3 slice_bitcast_fusion
  7.0 1.8 cosine_select_fusion.1.pos_ref
  8.7 0.0 copy-done
  8.7 0.0 copy-done.1
  8.8 0.8 slice_bitcast_fusion.6
  9.6 0.0 copy-done.2
  9.6 0.0 copy-done.3
  9.6 0.8 slice_bitcast_fusion.4
  10.4 59.8 %intra.1 = (bf16[16,256,256]{2,1,0:T(8,128)(2,1)}, f32[2,8,256]{2,1,0:T(8,128)}) custom-call(bf16[16,256,256]{2,1,0:T(8,128)(2,1)} %x_ref.1, f32[256,256]{1,0:T(8,128)} %cosine_select_fusion.1.pos_ref, f32[256,1]{1,0:T(8,128)} %copy.25.g1_ref, f32[256,1]{1,0:T(8,128)} %copy.26.g2_ref, bf16[256,256]{1,0:T(8,128)(2,1)} %get-tuple-element.39.wq_ref, ...), custom_call_target="tpu_custom_call" | custom-call | tf_op jit(solution)/shard_map/intra/pallas_call | solution.py:101
  70.2 0.8 reduce_sum.36
  71.0 0.6 broadcast_in_dim.18
  71.7 8.6 %all-to-all-start = ((f32[32,1,2]{2,1,0:T(1,128)}), f32[32,1,2]{2,1,0:T(1,128)S(1)}, u32[]{:S(2)}, u32[]{:S(2)}) async-start(f32[32,1,2]{2,1,0:T(1,128)} %broadcast_in_dim.18), calls=%async_computation | async-start | bytes 32768 | tf_op jit(solution)/shard_map/all_to_all | solution.py:120
  80.2 0.0 copy-done.4
  80.3 0.0 copy-done.5
  80.3 6.9 %all-to-all-done = f32[32,1,2]{2,1,0:T(1,128)S(1)} async-done(((f32[32,1,2]{2,1,0:T(1,128)}), f32[32,1,2]{2,1,0:T(1,128)S(1)}, u32[]{:S(2)}, u32[]{:S(2)}) %all-to-all-start) | async-done | bytes 288 | tf_op jit(solution)/shard_map/all_to_all | solution.py:120
  87.2 0.1 reduce_sum.37
  87.3 0.6 fusion.16
  90.4 3.2 %fusion.4 = bf16[256,16,256]{2,0,1:T(8,128)(2,1)S(1)} fusion(bf16[16,256,256]{2,1,0:T(8,128)(2,1)} %x_ref.1, bf16[16,256,256]{2,1,0:T(8,128)(2,1)} %get-tuple-element.9, f32[256]{0:T(256)S(1)} %bitcast.51, f32[]{:T(128)} %bitcast.11, f32[]{:T(128)} %bitcast.10, f32[256]{0:T(256)S(1)} %bitcast.50), kind=kLoop, calls=%fused_computation.7 | loop fusion | flops 8388608 | bytes 6293512 | tf_op jit(solution)/shard_map/transpose | solution.py:140
  93.7 2.5 %copy.28 = bf16[256,16,256]{2,1,0:T(8,128)(2,1)} copy(bf16[256,16,256]{2,0,1:T(8,128)(2,1)S(1)} %fusion.4) | data formatting | bytes 4194304 | tf_op jit(solution)/shard_map/transpose | solution.py:140
  96.2 5.0 %all-to-all-start.1 = ((bf16[32,8,16,256]{3,2,1,0:T(8,128)(2,1)}), bf16[32,8,16,256]{3,2,1,0:T(8,128)(2,1)}, u32[]{:S(2)}, u32[]{:S(2)}) async-start(bf16[32,8,16,256]{3,2,1,0:T(8,128)(2,1)} %bitcast.47), calls=%async_computation.1 | async-start | bytes 4194304 | tf_op jit(solution)/shard_map/all_to_all | solution.py:141
  101.2 0.8 copy.30.g2_ref
  102.0 0.8 copy.29.g1_ref
  102.8 3.0 %cosine_select_fusion.pos_ref = f32[256,512]{1,0:T(8,128)} fusion(f32[256]{0:T(256)S(1)} %fusion.10, pred[256]{0:T(512)(128)(4,1)S(1)} %fusion.12), kind=kLoop, calls=%fused_computation.11 | loop fusion | flops 262144 | bytes 525568 | tf_op jit(solution)/shard_map/jit(_where)/select_n | solution.py:26
  105.8 23.9 %all-to-all-done.1.x_ref = bf16[32,8,16,256]{3,2,1,0:T(8,128)(2,1)} async-done(((bf16[32,8,16,256]{3,2,1,0:T(8,128)(2,1)}), bf16[32,8,16,256]{3,2,1,0:T(8,128)(2,1)}, u32[]{:S(2)}, u32[]{:S(2)}) %all-to-all-start.1) | async-done | bytes 2097184 | tf_op jit(solution)/shard_map/all_to_all | solution.py:141
  129.7 63.0 %inter.1 = (bf16[32,8,16,256]{3,2,1,0:T(8,128)(2,1)}, f32[2,8,512]{2,1,0:T(8,128)}) custom-call(bf16[32,8,16,256]{3,2,1,0:T(8,128)(2,1)} %all-to-all-done.1.x_ref, f32[256,512]{1,0:T(8,128)} %cosine_select_fusion.pos_ref, f32[256,1]{1,0:T(8,128)} %copy.29.g1_ref, f32[256,1]{1,0:T(8,128)} %copy.30.g2_ref, bf16[256,256]{1,0:T(8,128)(2,1)} %get-tuple-element.40.wq_ref, ...), custom_call_target="tpu_custom_call" | custom-call | tf_op jit(solution)/shard_map/inter/pallas_call | solution.py:101
  192.7 0.9 reduce_sum.38
  193.6 10.6 %all_to_all.20 = f32[32,1,2]{2,1,0:T(1,128)S(1)} all-to-all(f32[32,1,2]{2,1,0:T(1,128)S(1)} %broadcast_in_dim.23), channel_id=1, replica_groups=mesh['mix'=4,'span'=32] {'span'}, dimensions={0} | all-to-all | bytes 512 | tf_op jit(solution)/shard_map/all_to_all | solution.py:120
  204.1 5.0 %all-to-all-start.2 = ((bf16[32,8,16,256]{3,2,1,0:T(8,128)(2,1)}), bf16[32,8,16,256]{3,2,1,0:T(8,128)(2,1)}, u32[]{:S(2)}, u32[]{:S(2)}) async-start(bf16[32,8,16,256]{3,2,1,0:T(8,128)(2,1)} %get-tuple-element.11), calls=%async_computation.2 | async-start | bytes 4194304 | tf_op jit(solution)/shard_map/all_to_all | solution.py:146
  209.2 0.1 reduce_sum.39
  209.2 0.6 fusion.15
  212.3 25.4 %all-to-all-done.2 = bf16[32,8,16,256]{3,2,1,0:T(8,128)(2,1)} async-done(((bf16[32,8,16,256]{3,2,1,0:T(8,128)(2,1)}), bf16[32,8,16,256]{3,2,1,0:T(8,128)(2,1)}, u32[]{:S(2)}, u32[]{:S(2)}) %all-to-all-start.2) | async-done | bytes 2097184 | tf_op jit(solution)/shard_map/all_to_all | solution.py:146
  237.6 2.2 convert_subtract_fusion
  239.8 3.9 %fusion.5 = bf16[16,256,256]{2,1,0:T(8,128)(2,1)} fusion(bf16[256,16,256]{2,0,1:T(8,128)(2,1)S(1)} %fusion.4, f32[256,16,256]{2,1,0:T(8,128)S(1)} %bitcast.46, f32[256]{0:T(256)S(1)} %bitcast.49, f32[]{:T(128)} %bitcast.25, f32[256]{0:T(256)S(1)} %bitcast.48), kind=kLoop, calls=%fused_computation.8 | loop fusion | flops 6291456 | bytes 8390660 | tf_op jit(solution)/shard_map/transpose | solution.py:150
  (5 shorter events, 0.0 us)
Async XLA Ops:
  0.0 8.7 %copy-start = (bf16[2,256,256]{2,1,0:T(8,128)(2,1)S(1)}, bf16[2,256,256]{2,1,0:T(8,128)(2,1)}, u32[]{:S(2)}) copy-start(bf16[2,256,256]{2,1,0:T(8,128)(2,1)} %param.12) | copy-start | bytes 786436
  0.0 8.7 %copy-start.1 = (bf16[2,256,256]{2,1,0:T(8,128)(2,1)S(1)}, bf16[2,256,256]{2,1,0:T(8,128)(2,1)}, u32[]{:S(2)}) copy-start(bf16[2,256,256]{2,1,0:T(8,128)(2,1)} %param.11) | copy-start | bytes 786436
  0.0 9.6 %copy-start.2 = (bf16[2,256,256]{2,1,0:T(8,128)(2,1)S(1)}, bf16[2,256,256]{2,1,0:T(8,128)(2,1)}, u32[]{:S(2)}) copy-start(bf16[2,256,256]{2,1,0:T(8,128)(2,1)} %param.14) | copy-start | bytes 786436
  0.0 9.6 %copy-start.3 = (bf16[2,256,256]{2,1,0:T(8,128)(2,1)S(1)}, bf16[2,256,256]{2,1,0:T(8,128)(2,1)}, u32[]{:S(2)}) copy-start(bf16[2,256,256]{2,1,0:T(8,128)(2,1)} %param.13) | copy-start | bytes 786436
  4.7 75.5 %copy-start.4 = (f32[2,256]{1,0:T(2,128)S(1)}, f32[2,256]{1,0:T(2,128)}, u32[]{:S(2)}) copy-start(f32[2,256]{1,0:T(2,128)} %param.18) | copy-start | bytes 6148
  4.7 75.6 %copy-start.5 = (f32[2,256]{1,0:T(2,128)S(1)}, f32[2,256]{1,0:T(2,128)}, u32[]{:S(2)}) copy-start(f32[2,256]{1,0:T(2,128)} %param.19) | copy-start | bytes 6148
  71.7 15.6 %all-to-all-start = ((f32[32,1,2]{2,1,0:T(1,128)}), f32[32,1,2]{2,1,0:T(1,128)S(1)}, u32[]{:S(2)}, u32[]{:S(2)}) async-start(f32[32,1,2]{2,1,0:T(1,128)} %broadcast_in_dim.18), calls=%async_computation | async-start | bytes 32768 | tf_op jit(solution)/shard_map/all_to_all | solution.py:120
  96.2 33.5 %all-to-all-start.1 = ((bf16[32,8,16,256]{3,2,1,0:T(8,128)(2,1)}), bf16[32,8,16,256]{3,2,1,0:T(8,128)(2,1)}, u32[]{:S(2)}, u32[]{:S(2)}) async-start(bf16[32,8,16,256]{3,2,1,0:T(8,128)(2,1)} %bitcast.47), calls=%async_computation.1 | async-start | bytes 4194304 | tf_op jit(solution)/shard_map/all_to_all | solution.py:141
  204.1 33.5 %all-to-all-start.2 = ((bf16[32,8,16,256]{3,2,1,0:T(8,128)(2,1)}), bf16[32,8,16,256]{3,2,1,0:T(8,128)(2,1)}, u32[]{:S(2)}, u32[]{:S(2)}) async-start(bf16[32,8,16,256]{3,2,1,0:T(8,128)(2,1)} %get-tuple-element.11), calls=%async_computation.2 | async-start | bytes 4194304 | tf_op jit(solution)/shard_map/all_to_all | solution.py:146

commit v2 on v1

v2 whole, which is shorter than its diff:
```python
import functools
import math

import jax
import jax.numpy as jnp
from jax import lax
from jax.experimental import pallas as pl
from jax.experimental.pallas import tpu as pltpu
from jax.sharding import PartitionSpec as P

D = 256
HEADS = 8
HD = D // HEADS
FF = 1024
EPS = 1e-05
AUG = HD + 16
F32 = jnp.float32
BF16 = jnp.bfloat16


def pos_table_t(length):
    places = jnp.arange(length, dtype=F32)[None, :]
    column = jnp.arange(D)
    rates = jnp.exp(-(2 * (column // 2)).astype(F32) / D * math.log(10000.0))
    angles = places * rates[:, None]
    return jnp.where((column % 2 == 0)[:, None], jnp.sin(angles), jnp.cos(angles))


def dot(a, b):
    return lax.dot_general(a, b, (((1,), (0,)), ((), ())), preferred_element_type=F32)


def norm_cols(x, gain):
    center = jnp.mean(x, axis=0, keepdims=True)
    shifted = x - center
    spread = jnp.mean(shifted * shifted, axis=0, keepdims=True)
    return shifted * lax.rsqrt(spread + EPS) * gain


CHUNK = 256


def phase_a(x, pos, g1, wq_t, wv_t, w_k, x_res, q_t, keys, vaug):
    xt = x.T.astype(F32) + pos
    x_res[...] = xt
    normed = norm_cols(xt, g1).astype(BF16)
    keys[...] = dot(normed.T, w_k).astype(BF16)
    scale = math.log2(math.e) / math.sqrt(HD)
    q_t[...] = (dot(wq_t, normed) * scale).astype(BF16)
    v_t = dot(wv_t, normed).astype(BF16)
    for h in range(HEADS):
        vaug[h * AUG : h * AUG + HD, :] = v_t[h * HD : (h + 1) * HD, :]


def phase_b(x_res, q_t, keys, vaug, wo_t, after, scores, weights, ctx):
    units = [(c, h) for c in range(q_t.shape[1] // CHUNK) for h in range(HEADS)]
    tops = {}

    def score(u):
        c, h = units[u]
        block, at = divmod(h * HD, 128)
        parts = []
        if at:
            parts.append(jnp.zeros((at, CHUNK), BF16))
        parts.append(q_t[h * HD : (h + 1) * HD, c * CHUNK : (c + 1) * CHUNK])
        if at + HD < 128:
            parts.append(jnp.zeros((128 - at - HD, CHUNK), BF16))
        s = dot(keys[:, block * 128 : (block + 1) * 128], jnp.concatenate(parts, axis=0))
        tops[u] = jnp.max(s, axis=0, keepdims=True)
        scores[u % len(scores)][...] = s

    def soften(u):
        s = scores[u % len(scores)][...]
        weights[u % len(weights)][...] = jnp.exp2(s - tops.pop(u)).astype(BF16)

    def mix(u):
        c, h = units[u]
        mixed = dot(vaug[h * AUG : (h + 1) * AUG, :], weights[u % len(weights)][...])
        ctx[h * HD : (h + 1) * HD, c * CHUNK : (c + 1) * CHUNK] = (
            mixed[:HD, :] * (1.0 / mixed[HD : HD + 1, :])
        ).astype(BF16)

    n = len(units)
    for u in range(n + 2):
        if u < n:
            score(u)
        if 0 <= u - 1 < n:
            soften(u - 1)
        if 0 <= u - 2 < n:
            mix(u - 2)
    after[...] = x_res[...] + dot(wo_t, ctx[...])


def phase_c(after, g2, wup_t, wdn_t, y_ref, stat_ref):
    aft = after[...]
    normed_two = norm_cols(aft, g2).astype(BF16)
    hidden = jnp.maximum(dot(wup_t, normed_two), 0.0).astype(BF16)
    y_t = aft + dot(wdn_t, hidden)
    part = y_t.reshape(D // 8, 8, y_t.shape[1])
    stat_ref[0] += jnp.sum(part, axis=0)
    stat_ref[1] += jnp.sum(part * part, axis=0)
    y_ref[...] = y_t.astype(BF16).T.reshape(y_ref.shape)


def layer_kernel(pair, x_ref, pos_ref, g1_ref, g2_ref, wq_ref, wk_ref, wv_ref, wo_ref, wup_ref, wdn_ref,
                 y_ref, stat_ref, wq_t, wv_t, wo_t, wup_t, wdn_t, *bufs):
    length = pos_ref.shape[1]
    slots = (bufs[0:5], bufs[5:10])
    ctx, scores, weights = bufs[10], bufs[11:14], bufs[14:17]
    step, last = pl.program_id(0), pl.num_programs(0) - 1

    def run(sub, a, b, c):
        here, other = slots[sub], slots[1 - sub]
        if c:
            phase_c(here[4], g2_ref[...], wup_t[...], wdn_t[...], pair(y_ref, sub), stat_ref)
        if a:
            phase_a(pair(x_ref, sub)[...].reshape(length, D), pos_ref[...], g1_ref[...], wq_t[...], wv_t[...],
                    wk_ref[...], *here[:4])
        if b:
            phase_b(*other[:4], wo_t[...], other[4], scores, weights, ctx)

    @pl.when(step == 0)
    def _():
        wq_t[...] = wq_ref[...].T
        wv_t[...] = wv_ref[...].T
        wo_t[...] = wo_ref[...].T
        wup_t[...] = wup_ref[...].T
        wdn_t[...] = wdn_ref[...].T
        for slot in slots:
            slot[3][...] = jnp.ones_like(slot[3])
        stat_ref[...] = jnp.zeros_like(stat_ref)
        run(0, True, False, False)
        run(1, True, True, False)

    @pl.when((step > 0) & (step < last))
    def _():
        run(0, True, True, True)
        run(1, True, True, True)

    @pl.when(step == last)
    def _():
        run(0, False, True, True)
        run(1, False, False, True)


def layer(x, count, x_block, x_map, pair, length, pos, g1, g2, w_q, w_k, w_v, w_o, w_u, w_d, name):
    whole = lambda a: pl.BlockSpec(a.shape, lambda i: (0,) * a.ndim)
    consts = (pos, g1, g2, w_q, w_k, w_v, w_o, w_u, w_d)
    pairs = count // 2
    slot = [
        pltpu.VMEM((D, length), F32), pltpu.VMEM((D, length), BF16), pltpu.VMEM((length, D), BF16),
        pltpu.VMEM((HEADS * AUG, length), BF16), pltpu.VMEM((D, length), F32),
    ]
    return pl.pallas_call(
        functools.partial(layer_kernel, pair),
        grid=(pairs + 1,),
        in_specs=[pl.BlockSpec(x_block, lambda i: x_map(jnp.minimum(i, pairs - 1)))] + [whole(a) for a in consts],
        out_specs=[pl.BlockSpec(x_block, lambda i: x_map(jnp.maximum(i - 1, 0))),
                   pl.BlockSpec((2, 8, length), lambda i: (0, 0, 0))],
        out_shape=[jax.ShapeDtypeStruct(x.shape, BF16), jax.ShapeDtypeStruct((2, 8, length), F32)],
        scratch_shapes=[
            pltpu.VMEM((D, D), BF16), pltpu.VMEM((D, D), BF16), pltpu.VMEM((D, D), BF16),
            pltpu.VMEM((FF, D), BF16), pltpu.VMEM((D, FF), BF16), *slot, *slot,
            pltpu.VMEM((D, length), BF16),
            *[pltpu.VMEM((length, CHUNK), F32)] * 3, *[pltpu.VMEM((length, CHUNK), BF16)] * 3,
        ],
        compiler_params=pltpu.CompilerParams(dimension_semantics=("arbitrary",)),
        name=name,
    )(x, *consts)


def shared_stats(stat, cells):
    mine = jnp.sum(stat, axis=(1, 2))
    copies = jnp.broadcast_to(mine[None, None, :], (lax.axis_size("span"), 1, 2))
    total = lax.all_to_all(copies, "span", split_axis=0, concat_axis=0, tiled=True).sum(axis=(0, 1))
    center = total[0] / cells
    spread = total[1] / cells - center * center
    return center, lax.rsqrt(spread + EPS)


def body(mixture, w_query, w_key, w_value, w_out, w_up, w_down, ln_gain, gln_gain, gln_bias):
    shards = lax.axis_size("span")
    segs, frames, _ = mixture.shape
    own = frames // shards
    total = segs * shards
    cells = float(total * frames * D)
    weights = lambda l: (w_query[l], w_key[l], w_value[l], w_out[l], w_up[l], w_down[l])
    gains = lambda l: (ln_gain[l, 0][:, None], ln_gain[l, 1][:, None])

    intra, stat = layer(mixture, segs, (2, frames, D), lambda i: (i, 0, 0), lambda r, k: r.at[k], frames,
                        pos_table_t(frames), *gains(0), *weights(0), name="intra")
    center, inv = shared_stats(stat, cells)
    intra_out = (gln_gain[0] * (intra.astype(F32) - center) * inv + gln_bias[0]
                 + mixture.astype(F32)).astype(BF16)
    by_frame = jnp.swapaxes(intra_out, 0, 1).reshape(shards, own, segs, D)
    moved = lax.all_to_all(by_frame, "span", split_axis=0, concat_axis=0, tiled=True)

    inter, stat = layer(moved, own, (shards, 2, segs, D), lambda i: (0, i, 0, 0), lambda r, k: r.at[:, k], total,
                        pos_table_t(total), *gains(1), *weights(1), name="inter")
    center, inv = shared_stats(stat, cells)
    back = lax.all_to_all(inter, "span", split_axis=0, concat_axis=0, tiled=True)
    back = back.reshape(frames, segs, D)
    final = (gln_gain[1] * (back.astype(F32) - center) * inv + gln_bias[1]
             + jnp.swapaxes(intra_out, 0, 1).astype(F32)).astype(BF16)
    return jnp.swapaxes(final, 0, 1)


def solution(mesh):
    in_specs = (P(("mix", "span"), None, None), P(), P(), P(), P(), P(), P(), P(), P(), P())
    out_specs = P(("mix", "span"), None, None)
    return jax.shard_map(body, mesh=mesh, in_specs=in_specs, out_specs=out_specs, check_vma=False)
```

time: 244 us -> 188 us (0.77)
  Pallas kernels: 123 us -> 66 us
    pallas_call x2, Pallas kernels: 123 us -> 66 us  [layer(): pl.pallas_call(functools.partial(layer_kernel, pair), grid=(pairs + 1,),...]
  transfers between devices with their start and end apart: 3 -> 3, of which waited for: 3 -> 3; matrix products, arithmetic and copies ran while one was open for 2% -> 3% of each run, Pallas kernels for 0% -> 0%
where the time goes in v2:
time: 188 us; the launch traced here: 187 us
  Pallas kernels  66 us (35%)
  waiting for transfers between devices  56.2 us (30%)
  starting transfers between devices  18.6 us (10%)
  other arithmetic  15.9 us (8%)
  local copies, waits for them, and re-layouts  14.4 us (8%)
  blocking collectives  10.6 us (6%)
  between operations  5.16 us (3%)
    pallas_call x2, Pallas kernels, layer(): pl.pallas_call(functools.partial(layer_kernel, pair), grid=(pairs + 1,),...  66 us
    all_to_all x1, waiting for transfers between devices, body(): lax.all_to_all(inter, 'span', split_axis=0, concat_axis=0, tiled=True)  25.4 us
    all_to_all x1, waiting for transfers between devices, body(): lax.all_to_all(by_frame, 'span', split_axis=0, concat_axis=0, tiled=True)  23.9 us
    all_to_all x1, blocking collectives, shared_stats(): lax.all_to_all(copies, 'span', split_axis=0, concat_axis=0, tiled=True)  10.6 us
    all_to_all x1, starting transfers between devices, shared_stats(): lax.all_to_all(copies, 'span', split_axis=0, concat_axis=0, tiled=True)  8.57 us
    all_to_all x1, waiting for transfers between devices, shared_stats(): lax.all_to_all(copies, 'span', split_axis=0, concat_axis=0, tiled=True)  6.93 us
    all_to_all x1, starting transfers between devices, body(): lax.all_to_all(by_frame, 'span', split_axis=0, concat_axis=0, tiled=True)  5 us
    all_to_all x1, starting transfers between devices, body(): lax.all_to_all(inter, 'span', split_axis=0, concat_axis=0, tiled=True)  5 us
  transfers between devices with their start and end apart: 3, of which 3 were waited for; matrix products, arithmetic and copies ran while one was open for 3% of the time, Pallas kernels for 0%

profile of v2, /device:TPU:1, one launch (start us, length us, event | category | flops | bytes accessed | tf_op | source)
XLA Modules:
  0.0 186.8 jit_solution(11551139620284654821)
XLA Ops:
  0.0 0.0 copy-start
  0.0 0.0 copy-start.1
  0.0 0.0 copy-start.2
  0.0 0.0 copy-start.3
  0.0 0.8 slice_bitcast_fusion.12
  0.9 0.8 copy.26.g2_ref
  1.7 0.8 copy.25.g1_ref
  2.4 2.3 %slice_bitcast_fusion.1 = (bf16[256,1024]{1,0:T(8,128)(2,1)}, bf16[256,1024]{1,0:T(8,128)(2,1)}) fusion(bf16[2,256,1024]{2,1,0:T(8,128)(2,1)} %param.15), kind=kLoop, calls=%fused_computation.10 | loop fusion | bytes 2097152 | tf_op jit(solution)/shard_map/squeeze | solution.py:187
  4.7 0.0 copy-start.4
  4.7 0.0 copy-start.5
  4.7 2.3 %slice_bitcast_fusion = (bf16[1024,256]{1,0:T(8,128)(2,1)}, bf16[1024,256]{1,0:T(8,128)(2,1)}) fusion(bf16[2,1024,256]{2,1,0:T(8,128)(2,1)} %param.16), kind=kLoop, calls=%fused_computation.9 | loop fusion | bytes 2097152 | tf_op jit(solution)/shard_map/squeeze | solution.py:187
  7.0 1.8 cosine_select_fusion.1.pos_ref
  8.7 0.0 copy-done
  8.7 0.0 copy-done.1
  8.8 0.8 slice_bitcast_fusion.6
  9.6 0.0 copy-done.2
  9.6 0.0 copy-done.3
  9.6 0.8 slice_bitcast_fusion.4
  10.4 31.9 %intra.1 = (bf16[16,256,256]{2,1,0:T(8,128)(2,1)}, f32[2,8,256]{2,1,0:T(8,128)}) custom-call(bf16[16,256,256]{2,1,0:T(8,128)(2,1)} %x_ref.1, f32[256,256]{1,0:T(8,128)} %cosine_select_fusion.1.pos_ref, f32[256,1]{1,0:T(8,128)} %copy.25.g1_ref, f32[256,1]{1,0:T(8,128)} %copy.26.g2_ref, bf16[256,256]{1,0:T(8,128)(2,1)} %get-tuple-element.39.wq_ref, ...), custom_call_target="tpu_custom_call" | custom-call | tf_op jit(solution)/shard_map/intra/pallas_call | solution.py:154
  42.3 0.8 reduce_sum.36
  43.1 0.6 broadcast_in_dim.18
  43.7 8.6 %all-to-all-start = ((f32[32,1,2]{2,1,0:T(1,128)}), f32[32,1,2]{2,1,0:T(1,128)S(1)}, u32[]{:S(2)}, u32[]{:S(2)}) async-start(f32[32,1,2]{2,1,0:T(1,128)} %broadcast_in_dim.18), calls=%async_computation | async-start | bytes 32768 | tf_op jit(solution)/shard_map/all_to_all | solution.py:175
  52.3 0.0 copy-done.4
  52.3 0.0 copy-done.5
  52.3 6.9 %all-to-all-done = f32[32,1,2]{2,1,0:T(1,128)S(1)} async-done(((f32[32,1,2]{2,1,0:T(1,128)}), f32[32,1,2]{2,1,0:T(1,128)S(1)}, u32[]{:S(2)}, u32[]{:S(2)}) %all-to-all-start) | async-done | bytes 288 | tf_op jit(solution)/shard_map/all_to_all | solution.py:175
  59.2 0.1 reduce_sum.37
  59.3 0.6 fusion.16
  62.5 3.2 %fusion.4 = bf16[256,16,256]{2,0,1:T(8,128)(2,1)S(1)} fusion(bf16[16,256,256]{2,1,0:T(8,128)(2,1)} %x_ref.1, bf16[16,256,256]{2,1,0:T(8,128)(2,1)} %get-tuple-element.9, f32[256]{0:T(256)S(1)} %bitcast.51, f32[]{:T(128)} %bitcast.11, f32[]{:T(128)} %bitcast.10, f32[256]{0:T(256)S(1)} %bitcast.50), kind=kLoop, calls=%fused_computation.7 | loop fusion | flops 8388608 | bytes 6293512 | tf_op jit(solution)/shard_map/transpose | solution.py:195
  65.7 2.5 %copy.28 = bf16[256,16,256]{2,1,0:T(8,128)(2,1)} copy(bf16[256,16,256]{2,0,1:T(8,128)(2,1)S(1)} %fusion.4) | data formatting | bytes 4194304 | tf_op jit(solution)/shard_map/transpose | solution.py:195
  68.2 5.0 %all-to-all-start.1 = ((bf16[32,8,16,256]{3,2,1,0:T(8,128)(2,1)}), bf16[32,8,16,256]{3,2,1,0:T(8,128)(2,1)}, u32[]{:S(2)}, u32[]{:S(2)}) async-start(bf16[32,8,16,256]{3,2,1,0:T(8,128)(2,1)} %bitcast.47), calls=%async_computation.1 | async-start | bytes 4194304 | tf_op jit(solution)/shard_map/all_to_all | solution.py:196
  73.2 0.8 copy.30.g2_ref
  74.0 0.8 copy.29.g1_ref
  74.8 3.0 %cosine_select_fusion.pos_ref = f32[256,512]{1,0:T(8,128)} fusion(f32[256]{0:T(256)S(1)} %fusion.10, pred[256]{0:T(512)(128)(4,1)S(1)} %fusion.12), kind=kLoop, calls=%fused_computation.11 | loop fusion | flops 262144 | bytes 525568 | tf_op jit(solution)/shard_map/jit(_where)/select_n | solution.py:26
  77.8 23.9 %all-to-all-done.1.x_ref = bf16[32,8,16,256]{3,2,1,0:T(8,128)(2,1)} async-done(((bf16[32,8,16,256]{3,2,1,0:T(8,128)(2,1)}), bf16[32,8,16,256]{3,2,1,0:T(8,128)(2,1)}, u32[]{:S(2)}, u32[]{:S(2)}) %all-to-all-start.1) | async-done | bytes 2097184 | tf_op jit(solution)/shard_map/all_to_all | solution.py:196
  101.7 34.1 %inter.1 = (bf16[32,8,16,256]{3,2,1,0:T(8,128)(2,1)}, f32[2,8,512]{2,1,0:T(8,128)}) custom-call(bf16[32,8,16,256]{3,2,1,0:T(8,128)(2,1)} %all-to-all-done.1.x_ref, f32[256,512]{1,0:T(8,128)} %cosine_select_fusion.pos_ref, f32[256,1]{1,0:T(8,128)} %copy.29.g1_ref, f32[256,1]{1,0:T(8,128)} %copy.30.g2_ref, bf16[256,256]{1,0:T(8,128)(2,1)} %get-tuple-element.40.wq_ref, ...), custom_call_target="tpu_custom_call" | custom-call | tf_op jit(solution)/shard_map/inter/pallas_call | solution.py:154
  135.8 0.9 reduce_sum.38
  136.7 10.6 %all_to_all.20 = f32[32,1,2]{2,1,0:T(1,128)S(1)} all-to-all(f32[32,1,2]{2,1,0:T(1,128)S(1)} %broadcast_in_dim.23), channel_id=1, replica_groups=mesh['mix'=4,'span'=32] {'span'}, dimensions={0} | all-to-all | bytes 512 | tf_op jit(solution)/shard_map/all_to_all | solution.py:175
  147.2 5.0 %all-to-all-start.2 = ((bf16[32,8,16,256]{3,2,1,0:T(8,128)(2,1)}), bf16[32,8,16,256]{3,2,1,0:T(8,128)(2,1)}, u32[]{:S(2)}, u32[]{:S(2)}) async-start(bf16[32,8,16,256]{3,2,1,0:T(8,128)(2,1)} %get-tuple-element.11), calls=%async_computation.2 | async-start | bytes 4194304 | tf_op jit(solution)/shard_map/all_to_all | solution.py:201
  152.2 0.1 reduce_sum.39
  152.3 0.6 fusion.15
  155.3 25.4 %all-to-all-done.2 = bf16[32,8,16,256]{3,2,1,0:T(8,128)(2,1)} async-done(((bf16[32,8,16,256]{3,2,1,0:T(8,128)(2,1)}), bf16[32,8,16,256]{3,2,1,0:T(8,128)(2,1)}, u32[]{:S(2)}, u32[]{:S(2)}) %all-to-all-start.2) | async-done | bytes 2097184 | tf_op jit(solution)/shard_map/all_to_all | solution.py:201
  180.7 2.2 %convert_subtract_fusion = f32[32,8,16,256]{3,2,1,0:T(8,128)S(1)} fusion(bf16[32,8,16,256]{3,2,1,0:T(8,128)(2,1)} %all-to-all-done.2, f32[]{:T(128)} %bitcast.23), kind=kLoop, calls=%fused_computation.5 | loop fusion | flops 2097152 | bytes 6291460 | tf_op jit(solution)/shard_map/sub | solution.py:203
  182.9 3.9 %fusion.5 = bf16[16,256,256]{2,1,0:T(8,128)(2,1)} fusion(bf16[256,16,256]{2,0,1:T(8,128)(2,1)S(1)} %fusion.4, f32[256,16,256]{2,1,0:T(8,128)S(1)} %bitcast.46, f32[256]{0:T(256)S(1)} %bitcast.49, f32[]{:T(128)} %bitcast.25, f32[256]{0:T(256)S(1)} %bitcast.48), kind=kLoop, calls=%fused_computation.8 | loop fusion | flops 6291456 | bytes 8390660 | tf_op jit(solution)/shard_map/transpose | solution.py:205
  (5 shorter events, 0.0 us)
Async XLA Ops:
  0.0 8.7 %copy-start = (bf16[2,256,256]{2,1,0:T(8,128)(2,1)S(1)}, bf16[2,256,256]{2,1,0:T(8,128)(2,1)}, u32[]{:S(2)}) copy-start(bf16[2,256,256]{2,1,0:T(8,128)(2,1)} %param.12) | copy-start | bytes 786436
  0.0 8.7 %copy-start.1 = (bf16[2,256,256]{2,1,0:T(8,128)(2,1)S(1)}, bf16[2,256,256]{2,1,0:T(8,128)(2,1)}, u32[]{:S(2)}) copy-start(bf16[2,256,256]{2,1,0:T(8,128)(2,1)} %param.11) | copy-start | bytes 786436
  0.0 9.6 %copy-start.2 = (bf16[2,256,256]{2,1,0:T(8,128)(2,1)S(1)}, bf16[2,256,256]{2,1,0:T(8,128)(2,1)}, u32[]{:S(2)}) copy-start(bf16[2,256,256]{2,1,0:T(8,128)(2,1)} %param.14) | copy-start | bytes 786436
  0.0 9.6 %copy-start.3 = (bf16[2,256,256]{2,1,0:T(8,128)(2,1)S(1)}, bf16[2,256,256]{2,1,0:T(8,128)(2,1)}, u32[]{:S(2)}) copy-start(bf16[2,256,256]{2,1,0:T(8,128)(2,1)} %param.13) | copy-start | bytes 786436
  4.7 47.6 %copy-start.4 = (f32[2,256]{1,0:T(2,128)S(1)}, f32[2,256]{1,0:T(2,128)}, u32[]{:S(2)}) copy-start(f32[2,256]{1,0:T(2,128)} %param.18) | copy-start | bytes 6148
  4.7 47.6 %copy-start.5 = (f32[2,256]{1,0:T(2,128)S(1)}, f32[2,256]{1,0:T(2,128)}, u32[]{:S(2)}) copy-start(f32[2,256]{1,0:T(2,128)} %param.19) | copy-start | bytes 6148
  43.7 15.6 %all-to-all-start = ((f32[32,1,2]{2,1,0:T(1,128)}), f32[32,1,2]{2,1,0:T(1,128)S(1)}, u32[]{:S(2)}, u32[]{:S(2)}) async-start(f32[32,1,2]{2,1,0:T(1,128)} %broadcast_in_dim.18), calls=%async_computation | async-start | bytes 32768 | tf_op jit(solution)/shard_map/all_to_all | solution.py:175
  68.2 33.5 %all-to-all-start.1 = ((bf16[32,8,16,256]{3,2,1,0:T(8,128)(2,1)}), bf16[32,8,16,256]{3,2,1,0:T(8,128)(2,1)}, u32[]{:S(2)}, u32[]{:S(2)}) async-start(bf16[32,8,16,256]{3,2,1,0:T(8,128)(2,1)} %bitcast.47), calls=%async_computation.1 | async-start | bytes 4194304 | tf_op jit(solution)/shard_map/all_to_all | solution.py:196
  147.2 33.5 %all-to-all-start.2 = ((bf16[32,8,16,256]{3,2,1,0:T(8,128)(2,1)}), bf16[32,8,16,256]{3,2,1,0:T(8,128)(2,1)}, u32[]{:S(2)}, u32[]{:S(2)}) async-start(bf16[32,8,16,256]{3,2,1,0:T(8,128)(2,1)} %get-tuple-element.11), calls=%async_computation.2 | async-start | bytes 4194304 | tf_op jit(solution)/shard_map/all_to_all | solution.py:201

commit v3 on v2

v3 whole, which is shorter than its diff:
```python
import functools
import math

import jax
import numpy as np
import jax.numpy as jnp
from jax import lax
from jax.experimental import pallas as pl
from jax.experimental.pallas import tpu as pltpu
from jax.sharding import PartitionSpec as P

D = 256
HEADS = 8
HD = D // HEADS
FF = 1024
EPS = 1e-05
AUG = HD + 16
F32 = jnp.float32
BF16 = jnp.bfloat16


def pos_parts(length):
    column = np.arange(D)
    rates = np.exp(-(2 * (column // 2)) / D * math.log(10000.0))[:, None]
    near = np.arange(128)[None, :] * rates
    far = 128 * np.arange(length // 128)[None, :] * rates
    even = (column % 2 == 0)[:, None]
    outer = np.where(even, np.sin(far), np.cos(far))
    swap = np.where(even, np.cos(far), -np.sin(far))
    far_two = np.zeros((2 * D, 128))
    far_two[:, : length // 128] = np.concatenate([outer, swap], axis=0)
    return np.stack([np.cos(near), np.sin(near)]).astype(np.float32), far_two.astype(np.float32)


def dot(a, b):
    return lax.dot_general(a, b, (((1,), (0,)), ((), ())), preferred_element_type=F32)


def norm_cols(x, gain):
    center = jnp.mean(x, axis=0, keepdims=True)
    shifted = x - center
    spread = jnp.mean(shifted * shifted, axis=0, keepdims=True)
    return shifted * lax.rsqrt(spread + EPS) * gain


CHUNK = 256
LEAD = 2
TRAIL = 1


def score_unit(q_t, keys, c, h):
    block, at = divmod(h * HD, 128)
    parts = []
    if at:
        parts.append(jnp.zeros((at, CHUNK), BF16))
    parts.append(q_t[h * HD : (h + 1) * HD, c * CHUNK : (c + 1) * CHUNK])
    if at + HD < 128:
        parts.append(jnp.zeros((128 - at - HD, CHUNK), BF16))
    return dot(keys[:, block * 128 : (block + 1) * 128], jnp.concatenate(parts, axis=0))


def run_step(fills, b, scores, weights, ctx):
    if b is None:
        for piece in fills:
            piece()
        return
    x_res, q_t, keys, vaug, after, wo_t = b
    units = [(c, h) for c in range(q_t.shape[1] // CHUNK) for h in range(HEADS)]
    tops = {}
    n = len(units)
    slots = n + LEAD + TRAIL
    done = 0
    for u in range(slots):
        if u < n:
            s = score_unit(q_t, keys, *units[u])
            tops[u] = jnp.max(s, axis=0, keepdims=True)
            scores[u % len(scores)][...] = s
        v = u - LEAD
        if 0 <= v < n:
            s = scores[v % len(scores)][...]
            weights[v % len(weights)][...] = jnp.exp2(s - tops.pop(v)).astype(BF16)
        w = v - TRAIL
        if 0 <= w < n:
            c, h = units[w]
            mixed = dot(vaug[h * AUG : (h + 1) * AUG, :], weights[w % len(weights)][...])
            ctx[h * HD : (h + 1) * HD, c * CHUNK : (c + 1) * CHUNK] = (
                mixed[:HD, :] * (1.0 / mixed[HD : HD + 1, :])
            ).astype(BF16)
        upto = len(fills) * (u + 1) // slots
        for piece in fills[done:upto]:
            piece()
        done = upto
    after[...] = x_res[...] + dot(wo_t[...], ctx[...])


def pieces_a(x, pos, g1, wq_t, wv_t, w_k, x_res, q_t, keys, vaug, n1):
    def first():
        xt = x().T.astype(F32) + pos[...]
        x_res[...] = xt
        n1[...] = norm_cols(xt, g1).astype(BF16)

    def get_keys():
        keys[...] = dot(n1[...].T, w_k[...]).astype(BF16)

    def get_queries():
        scale = math.log2(math.e) / math.sqrt(HD)
        q_t[...] = (dot(wq_t[...], n1[...]) * scale).astype(BF16)

    def get_values():
        v_t = dot(wv_t[...], n1[...]).astype(BF16)
        for h in range(HEADS):
            vaug[h * AUG : h * AUG + HD, :] = v_t[h * HD : (h + 1) * HD, :]

    return [first, get_keys, get_queries, get_values]


def pieces_c(after, g2, wup_t, wdn_t, y_ref, sums, n2, hidden):
    def first():
        n2[...] = norm_cols(after[...], g2).astype(BF16)

    def up(j):
        rows = slice(j * D, (j + 1) * D)
        hidden[rows, :] = jnp.maximum(dot(wup_t[rows, :], n2[...]), 0.0).astype(BF16)

    def down():
        y_t = after[...] + dot(wdn_t[...], hidden[...])
        part = y_t.reshape(D // 8, 8, y_t.shape[1])
        for k in range(y_t.shape[1] // 128):
            lanes = slice(k * 128, (k + 1) * 128)
            sums[0] += jnp.sum(part[:, :, lanes], axis=0)
            sums[1] += jnp.sum(part[:, :, lanes] * part[:, :, lanes], axis=0)
        y_ref[...] = y_t.astype(BF16).T.reshape(y_ref.shape)

    return [first] + [functools.partial(up, j) for j in range(FF // D)] + [down]


def layer_kernel(pair, x_ref, near_ref, far_ref, gain_ref, wq_ref, wk_ref, wv_ref, wo_ref, wup_ref, wdn_ref,
                 y_ref, stat_ref, wq_t, wv_t, wo_t, wup_t, wdn_t, pos, g1, g2, n1, n2, hidden, sums, *bufs):
    length = pos.shape[1]
    slots = (bufs[0:5], bufs[5:10])
    ctx, scores, weights = bufs[10], bufs[11 : 12 + LEAD], bufs[12 + LEAD :]
    step, last = pl.program_id(0), pl.num_programs(0) - 1

    def run(sub, a, b, c):
        here, other = slots[sub], slots[1 - sub]
        left, right = [], []
        if c:
            left = pieces_c(here[4], g2[:, :1], wup_t, wdn_t, pair(y_ref, sub), sums, n2, hidden)
        if a:
            get = lambda: pair(x_ref, sub)[...].reshape(length, D)
            right = pieces_a(get, pos, g1[:, :1], wq_t, wv_t, wk_ref, *here[:4], n1)
        fills = []
        while left or right:
            fills += left[:1] + right[:1]
            left, right = left[1:], right[1:]
        run_step(fills, (*other, wo_t) if b else None, scores, weights, ctx)

    @pl.when(step == 0)
    def _():
        wq_t[...] = wq_ref[...].T
        wv_t[...] = wv_ref[...].T
        wo_t[...] = wo_ref[...].T
        wup_t[...] = wup_ref[...].T
        wdn_t[...] = wdn_ref[...].T
        g1[...] = jnp.broadcast_to(gain_ref[0:1, :], (128, D)).T
        g2[...] = jnp.broadcast_to(gain_ref[1:2, :], (128, D)).T
        for a in range(length // 128):
            pos[:, a * 128 : (a + 1) * 128] = (
                far_ref[:D, a : a + 1] * near_ref[0] + far_ref[D:, a : a + 1] * near_ref[1])
        for slot in slots:
            slot[3][...] = jnp.ones_like(slot[3])
        sums[...] = jnp.zeros_like(sums)
        run(0, True, False, False)
        run(1, True, True, False)

    @pl.when((step > 0) & (step < last))
    def _():
        run(0, True, True, True)
        run(1, True, True, True)

    @pl.when(step == last)
    def _():
        run(0, False, True, True)
        run(1, False, False, True)
        rows = [jnp.sum(sums[k], axis=0, keepdims=True) for k in range(2)]
        tile = jnp.concatenate(rows + [jnp.zeros((6, 128), F32)], axis=0)
        stat_ref[...] = jnp.broadcast_to(tile[None], stat_ref.shape)


def layer(x, count, x_block, x_map, pair, length, level, gain, weights, peers, name):
    near, far = pos_parts(length)
    pick = lambda a: pl.BlockSpec((None, *a.shape[1:]), lambda i: (level,) + (0,) * (a.ndim - 1))
    whole = lambda a: pl.BlockSpec(a.shape, lambda i: (0,) * a.ndim)
    pairs = count // 2
    slot = [
        pltpu.VMEM((D, length), F32), pltpu.VMEM((D, length), BF16), pltpu.VMEM((length, D), BF16),
        pltpu.VMEM((HEADS * AUG, length), BF16), pltpu.VMEM((D, length), F32),
    ]
    return pl.pallas_call(
        functools.partial(layer_kernel, pair),
        grid=(pairs + 1,),
        in_specs=[pl.BlockSpec(x_block, lambda i: x_map(jnp.minimum(i, pairs - 1))),
                  whole(near), whole(far), pick(gain)] + [pick(w) for w in weights],
        out_specs=[pl.BlockSpec(x_block, lambda i: x_map(jnp.maximum(i - 1, 0))),
                   pl.BlockSpec((peers, 8, 128), lambda i: (0, 0, 0))],
        out_shape=[jax.ShapeDtypeStruct(x.shape, BF16), jax.ShapeDtypeStruct((peers, 8, 128), F32)],
        scratch_shapes=[
            pltpu.VMEM((D, D), BF16), pltpu.VMEM((D, D), BF16), pltpu.VMEM((D, D), BF16),
            pltpu.VMEM((FF, D), BF16), pltpu.VMEM((D, FF), BF16),
            pltpu.VMEM((D, length), F32), pltpu.VMEM((D, 128), F32), pltpu.VMEM((D, 128), F32),
            pltpu.VMEM((D, length), BF16), pltpu.VMEM((D, length), BF16), pltpu.VMEM((FF, length), BF16),
            pltpu.VMEM((2, 8, 128), F32), *slot, *slot, pltpu.VMEM((D, length), BF16),
            *[pltpu.VMEM((length, CHUNK), F32)] * (LEAD + 1), *[pltpu.VMEM((length, CHUNK), BF16)] * (TRAIL + 1),
        ],
        compiler_params=pltpu.CompilerParams(dimension_semantics=("arbitrary",)),
        name=name,
    )(x, jnp.asarray(near), jnp.asarray(far), gain, *weights)


def blend_kernel(cells, stat_ref, out_ref, res_ref, gain_ref, bias_ref, final_ref):
    parts = jnp.sum(stat_ref[...], axis=0)
    center = jnp.sum(parts[0:1, :], axis=1, keepdims=True) / cells
    spread = jnp.sum(parts[1:2, :], axis=1, keepdims=True) / cells - center * center
    slope = gain_ref[...] * lax.rsqrt(spread + EPS)
    shifted = out_ref[...].astype(F32) - center[None]
    final = slope[None] * shifted + bias_ref[...][None] + res_ref[...].astype(F32)
    final_ref[...] = jnp.swapaxes(final, 0, 1).astype(BF16)


def blend(stat, out, residual, gain, bias, cells, in_block, in_map, steps, name):
    first, second, _ = out.shape
    block = pl.BlockSpec(in_block, in_map)
    whole = lambda a: pl.BlockSpec(a.shape, lambda i: (0,) * a.ndim)
    def out_map(i):
        one, two, _ = in_map(i)
        return two, one, 0
    return pl.pallas_call(
        functools.partial(blend_kernel, cells),
        grid=(steps,),
        in_specs=[whole(stat), block, block, whole(gain), whole(bias)],
        out_specs=pl.BlockSpec((in_block[1], in_block[0], D), out_map),
        out_shape=jax.ShapeDtypeStruct((second, first, D), BF16),
        compiler_params=pltpu.CompilerParams(dimension_semantics=("arbitrary",)),
        name=name,
    )(stat, out, residual, gain, bias)


def body(mixture, w_query, w_key, w_value, w_out, w_up, w_down, ln_gain, gln_gain, gln_bias):
    shards = lax.axis_size("span")
    segs, frames, _ = mixture.shape
    own = frames // shards
    total = segs * shards
    cells = float(total * frames * D)
    weights = (w_query, w_key, w_value, w_out, w_up, w_down)
    steps = 4

    intra, stat = layer(mixture, segs, (2, frames, D), lambda i: (i, 0, 0), lambda r, k: r.at[k], frames,
                        0, ln_gain, weights, shards, name="intra")
    stat = lax.all_to_all(stat, "span", split_axis=0, concat_axis=0, tiled=True)
    across = blend(stat, intra, mixture, gln_gain[0:1], gln_bias[0:1], cells,
                   (segs, frames // steps, D), lambda i: (0, i, 0), steps, "blend_intra")
    moved = lax.all_to_all(across.reshape(shards, own, segs, D), "span", split_axis=0, concat_axis=0, tiled=True)

    inter, stat = layer(moved, own, (shards, 2, segs, D), lambda i: (0, i, 0, 0), lambda r, k: r.at[:, k], total,
                        1, ln_gain, weights, 1, name="inter")
    back = lax.all_to_all(inter, "span", split_axis=0, concat_axis=0, tiled=True)
    stat = stat[0]
    for bit in range(shards.bit_length() - 1):
        stat = stat + lax.ppermute(stat, "span", [(i, i ^ (1 << bit)) for i in range(shards)])
    return blend(stat[None], back.reshape(frames, segs, D), across, gln_gain[1:2], gln_bias[1:2], cells,
                 (frames // steps, segs, D), lambda i: (i, 0, 0), steps, "blend_inter")


def solution(mesh):
    in_specs = (P(("mix", "span"), None, None), P(), P(), P(), P(), P(), P(), P(), P(), P())
    out_specs = P(("mix", "span"), None, None)
    return jax.shard_map(body, mesh=mesh, in_specs=in_specs, out_specs=out_specs, check_vma=False)
```

time: 188 us -> 159 us (0.85)
  the two profiles are of different devices: /device:TPU:1 before, /device:TPU:70 now
where the time goes in v3:
time: 159 us; the launch traced here: 158 us
  Pallas kernels  64.4 us (41%)
  waiting for transfers between devices  37.8 us (24%)
  blocking collectives  33.1 us (21%)
  starting transfers between devices  19.7 us (12%)
  local copies, waits for them, and re-layouts  2.59 us (2%)
    pallas_call x2, Pallas kernels, layer(): pl.pallas_call(functools.partial(layer_kernel, pair), grid=(pairs + 1,),...  53.3 us
    all_to_all x1, blocking collectives, body(): lax.all_to_all(across.reshape(shards, own, segs, D), 'span', split_axis=0...  33.1 us
    ppermute x5, waiting for transfers between devices, body(): lax.ppermute(stat, 'span', [(i, i ^ 1 << bit) for i in range(shards)])  32.5 us
    pallas_call x2, Pallas kernels, blend(): pl.pallas_call(functools.partial(blend_kernel, cells), grid=(steps,), in_...  11.1 us
    all_to_all x1, starting transfers between devices, body(): stat = lax.all_to_all(stat, 'span', split_axis=0, concat_axis=0, tiled=True)  7.62 us
    ppermute x5, starting transfers between devices, body(): lax.ppermute(stat, 'span', [(i, i ^ 1 << bit) for i in range(shards)])  6.39 us
    all_to_all x1, starting transfers between devices, body(): lax.all_to_all(inter, 'span', split_axis=0, concat_axis=0, tiled=True)  5.73 us
    all_to_all x1, waiting for transfers between devices, body(): stat = lax.all_to_all(stat, 'span', split_axis=0, concat_axis=0, tiled=True)  5.28 us
  transfers between devices with their start and end apart: 7, of which 6 were waited for; matrix products, arithmetic and copies ran while one was open for 1% of the time, Pallas kernels for 0%

profile of v3, /device:TPU:70, one launch (start us, length us, event | category | flops | bytes accessed | tf_op | source)
XLA Modules:
  0.0 158.2 jit_solution(3651552302972551513)
XLA Ops:
  0.0 0.0 copy-start.3
  0.0 0.0 copy-start.4
  0.0 23.5 %intra.1 = (bf16[16,256,256]{2,1,0:T(8,128)(2,1)}, f32[32,8,128]{2,1,0:T(8,128)}) custom-call(bf16[16,256,256]{2,1,0:T(8,128)(2,1)} %res_ref.1, f32[2,256,128]{2,1,0:T(8,128)} %constant.6.clone.near_ref, f32[512,128]{1,0:T(8,128)} %constant.7.clone.far_ref, f32[2,2,256]{2,1,0:T(2,128)} %gain_ref.3, bf16[2,256,256]{2,1,0:T(8,128)(2,1)} %wq_ref.3, ...), custom_call_target="tpu_custom_call" | custom-call | tf_op jit(solution)/shard_map/intra/pallas_call | solution.py:199
  23.6 7.6 %all-to-all-start = ((f32[32,8,128]{2,1,0:T(8,128)}), f32[32,8,128]{2,1,0:T(8,128)S(1)}, u32[]{:S(2)}, u32[]{:S(2)}) async-start(f32[32,8,128]{2,1,0:T(8,128)} %get-tuple-element.9), calls=%async_computation | async-start | bytes 262144 | tf_op jit(solution)/shard_map/all_to_all | solution.py:259
  31.2 0.0 copy-done.3
  31.2 0.0 copy-done.4
  31.2 0.6 fusion
  31.8 5.3 %all-to-all-done.stat_ref = f32[32,8,128]{2,1,0:T(8,128)S(1)} async-done(((f32[32,8,128]{2,1,0:T(8,128)}), f32[32,8,128]{2,1,0:T(8,128)S(1)}, u32[]{:S(2)}, u32[]{:S(2)}) %all-to-all-start) | async-done | bytes 131104 | tf_op jit(solution)/shard_map/all_to_all | solution.py:259
  37.1 0.0 copy-start.1
  37.1 0.6 copy-done.1
  37.7 5.6 %blend_intra.1.res_ref = bf16[256,16,256]{2,1,0:T(8,128)(2,1)} custom-call(f32[32,8,128]{2,1,0:T(8,128)} %copy-done.1, bf16[16,256,256]{2,1,0:T(8,128)(2,1)} %get-tuple-element.10.out_ref, bf16[16,256,256]{2,1,0:T(8,128)(2,1)} %res_ref.1, f32[1,256]{1,0:T(1,128)} %get-tuple-element.17.gain_ref, f32[1,256]{1,0:T(1,128)} %get-tuple-element.14.bias_ref), custom_call_target="tpu_custom_call" | custom-call | tf_op jit(solution)/shard_map/blend_intra/pallas_call | solution.py:237
  43.3 33.1 %all_to_all.15.x_ref = bf16[32,8,16,256]{3,2,1,0:T(8,128)(2,1)} all-to-all(bf16[32,8,16,256]{3,2,1,0:T(8,128)(2,1)} %bitcast.6), channel_id=1, replica_groups=mesh['mix'=4,'span'=32] {'span'}, dimensions={0} | all-to-all | bytes 4194304 | tf_op jit(solution)/shard_map/all_to_all | solution.py:262
  76.4 29.8 %inter.1 = (bf16[32,8,16,256]{3,2,1,0:T(8,128)(2,1)}, f32[1,8,128]{2,1,0:T(8,128)}) custom-call(bf16[32,8,16,256]{3,2,1,0:T(8,128)(2,1)} %all_to_all.15.x_ref, f32[2,256,128]{2,1,0:T(8,128)} %constant.6.clone.near_ref, f32[512,128]{1,0:T(8,128)} %constant.8.clone.far_ref, f32[2,2,256]{2,1,0:T(2,128)} %gain_ref.3, bf16[2,256,256]{2,1,0:T(8,128)(2,1)} %wq_ref.3, ...), custom_call_target="tpu_custom_call" | custom-call | tf_op jit(solution)/shard_map/inter/pallas_call | solution.py:199
  106.2 0.0 copy-start.2
  106.2 5.7 %all-to-all-start.2 = ((bf16[32,8,16,256]{3,2,1,0:T(8,128)(2,1)}), bf16[32,8,16,256]{3,2,1,0:T(8,128)(2,1)S(1)}, u32[]{:S(2)}, u32[]{:S(2)}) async-start(bf16[32,8,16,256]{3,2,1,0:T(8,128)(2,1)} %get-tuple-element.12), calls=%async_computation.2 | async-start | bytes 4194304 | tf_op jit(solution)/shard_map/all_to_all | solution.py:266
  111.9 0.0 copy-done.2
  111.9 0.2 collective-permute-start
  112.1 1.0 collective-permute-done
  113.2 1.5 collective-permute-start.1
  114.6 22.4 %collective-permute-done.1 = f32[8,128]{1,0:T(8,128)S(1)} collective-permute-done((f32[8,128]{1,0:T(8,128)S(1)}, f32[8,128]{1,0:T(8,128)S(1)}, u32[]{:S(2)}, u32[]{:S(2)}) %collective-permute-start.1) | collective-permute-done | bytes 4128 | tf_op jit(solution)/shard_map/ppermute | solution.py:269
  137.0 2.7 %collective-permute-start.2 = (f32[8,128]{1,0:T(8,128)S(1)}, f32[8,128]{1,0:T(8,128)S(1)}, u32[]{:S(2)}, u32[]{:S(2)}) collective-permute-start(f32[8,128]{1,0:T(8,128)S(1)} %add.16), channel_id=1, source_target_pairs={{0,4},{1,5},{2,6},{3,7},{4,0},{5,1},{6,2},{7,3},{8,12},{9,13},{10,... | collective-permute-start | bytes 12296 | tf_op jit(solution)/shard_map/ppermute | solution.py:269
  139.7 2.4 %collective-permute-done.2 = f32[8,128]{1,0:T(8,128)S(1)} collective-permute-done((f32[8,128]{1,0:T(8,128)S(1)}, f32[8,128]{1,0:T(8,128)S(1)}, u32[]{:S(2)}, u32[]{:S(2)}) %collective-permute-start.2) | collective-permute-done | bytes 4128 | tf_op jit(solution)/shard_map/ppermute | solution.py:269
  142.1 0.8 collective-permute-start.3
  142.9 2.8 %collective-permute-done.3 = f32[8,128]{1,0:T(8,128)S(1)} collective-permute-done((f32[8,128]{1,0:T(8,128)S(1)}, f32[8,128]{1,0:T(8,128)S(1)}, u32[]{:S(2)}, u32[]{:S(2)}) %collective-permute-start.3) | collective-permute-done | bytes 4128 | tf_op jit(solution)/shard_map/ppermute | solution.py:269
  145.7 1.2 collective-permute-start.4
  146.9 3.9 %collective-permute-done.4 = f32[8,128]{1,0:T(8,128)S(1)} collective-permute-done((f32[8,128]{1,0:T(8,128)S(1)}, f32[8,128]{1,0:T(8,128)S(1)}, u32[]{:S(2)}, u32[]{:S(2)}) %collective-permute-start.4) | collective-permute-done | bytes 4128 | tf_op jit(solution)/shard_map/ppermute | solution.py:269
  150.8 0.6 add_bitcast_fusion.stat_ref
  151.4 0.0 all-to-all-done.2
  151.4 0.0 copy-start
  151.4 1.3 copy-done
  152.8 5.5 %blend_inter.1 = bf16[16,256,256]{2,1,0:T(8,128)(2,1)} custom-call(f32[1,8,128]{2,1,0:T(8,128)} %add_bitcast_fusion.stat_ref, bf16[256,16,256]{2,1,0:T(8,128)(2,1)} %bitcast.7, bf16[256,16,256]{2,1,0:T(8,128)(2,1)} %blend_intra.1.res_ref, f32[1,256]{1,0:T(1,128)} %get-tuple-element.18.gain_ref, f32[1,256]{1,0:T(1,128)} %get-tuple-element.13.bias_ref), custom_call_target="tpu_custom_call" | custom-call | tf_op jit(solution)/shard_map/blend_inter/pallas_call | solution.py:237
  (4 shorter events, 0.0 us)
Async XLA Ops:
  0.0 31.2 %copy-start.3 = (f32[2,256]{1,0:T(2,128)S(1)}, f32[2,256]{1,0:T(2,128)}, u32[]{:S(2)}) copy-start(f32[2,256]{1,0:T(2,128)} %param.23) | copy-start | bytes 6148
  0.0 31.2 %copy-start.4 = (f32[2,256]{1,0:T(2,128)S(1)}, f32[2,256]{1,0:T(2,128)}, u32[]{:S(2)}) copy-start(f32[2,256]{1,0:T(2,128)} %param.22) | copy-start | bytes 6148
  23.6 13.5 %all-to-all-start = ((f32[32,8,128]{2,1,0:T(8,128)}), f32[32,8,128]{2,1,0:T(8,128)S(1)}, u32[]{:S(2)}, u32[]{:S(2)}) async-start(f32[32,8,128]{2,1,0:T(8,128)} %get-tuple-element.9), calls=%async_computation | async-start | bytes 262144 | tf_op jit(solution)/shard_map/all_to_all | solution.py:259
  37.1 0.7 copy-start.1
  106.2 5.7 %copy-start.2 = (f32[1,8,128]{2,1,0:T(8,128)S(1)}, f32[1,8,128]{2,1,0:T(8,128)}, u32[]{:S(2)}) copy-start(f32[1,8,128]{2,1,0:T(8,128)} %get-tuple-element.11) | copy-start | bytes 12292
  106.2 45.3 %all-to-all-start.2 = ((bf16[32,8,16,256]{3,2,1,0:T(8,128)(2,1)}), bf16[32,8,16,256]{3,2,1,0:T(8,128)(2,1)S(1)}, u32[]{:S(2)}, u32[]{:S(2)}) async-start(bf16[32,8,16,256]{3,2,1,0:T(8,128)(2,1)} %get-tuple-element.12), calls=%async_computation.2 | async-start | bytes 4194304 | tf_op jit(solution)/shard_map/all_to_all | solution.py:266
  111.9 1.2 collective-permute-start
  113.2 23.8 %collective-permute-start.1 = (f32[8,128]{1,0:T(8,128)S(1)}, f32[8,128]{1,0:T(8,128)S(1)}, u32[]{:S(2)}, u32[]{:S(2)}) collective-permute-start(f32[8,128]{1,0:T(8,128)S(1)} %bitcast_add_fusion), channel_id=1, source_target_pairs={{0,2},{1,3},{2,0},{3,1},{4,6},{5,7},{6,4},{7,5},{8,10},{9,11},{10,... | collective-permute-start | bytes 12296 | tf_op jit(solution)/shard_map/ppermute | solution.py:269
  137.0 5.1 %collective-permute-start.2 = (f32[8,128]{1,0:T(8,128)S(1)}, f32[8,128]{1,0:T(8,128)S(1)}, u32[]{:S(2)}, u32[]{:S(2)}) collective-permute-start(f32[8,128]{1,0:T(8,128)S(1)} %add.16), channel_id=1, source_target_pairs={{0,4},{1,5},{2,6},{3,7},{4,0},{5,1},{6,2},{7,3},{8,12},{9,13},{10,... | collective-permute-start | bytes 12296 | tf_op jit(solution)/shard_map/ppermute | solution.py:269
  142.1 3.6 %collective-permute-start.3 = (f32[8,128]{1,0:T(8,128)S(1)}, f32[8,128]{1,0:T(8,128)S(1)}, u32[]{:S(2)}, u32[]{:S(2)}) collective-permute-start(f32[8,128]{1,0:T(8,128)S(1)} %add.17), channel_id=1, source_target_pairs={{0,8},{1,9},{2,10},{3,11},{4,12},{5,13},{6,14},{7,15},{8,0},{9,1},... | collective-permute-start | bytes 12296 | tf_op jit(solution)/shard_map/ppermute | solution.py:269
  145.7 5.1 %collective-permute-start.4 = (f32[8,128]{1,0:T(8,128)S(1)}, f32[8,128]{1,0:T(8,128)S(1)}, u32[]{:S(2)}, u32[]{:S(2)}) collective-permute-start(f32[8,128]{1,0:T(8,128)S(1)} %add.18), channel_id=1, source_target_pairs={{0,16},{1,17},{2,18},{3,19},{4,20},{5,21},{6,22},{7,23},{8,24},{9,... | collective-permute-start | bytes 12296 | tf_op jit(solution)/shard_map/ppermute | solution.py:269
  151.4 1.3 copy-start

commit v4 on v3

--- a/solution.py
+++ b/solution.py
@@ -134,18 +134,34 @@
     return [first] + [functools.partial(up, j) for j in range(FF // D)] + [down]
 
 
-def layer_kernel(pair, x_ref, near_ref, far_ref, gain_ref, wq_ref, wk_ref, wv_ref, wo_ref, wup_ref, wdn_ref,
-                 y_ref, stat_ref, wq_t, wv_t, wo_t, wup_t, wdn_t, pos, g1, g2, n1, n2, hidden, sums, *bufs):
+def layer_kernel(pair, pairs, joined, x_ref, near_ref, far_ref, gain_ref, wq_ref, wk_ref, wv_ref, wo_ref, wup_ref, wdn_ref,
+                 y_ref, *refs):
+    if joined:
+        stat_ref = None
+    else:
+        stat_ref, refs = refs[0], refs[1:]
+    layer_steps(pair, pairs, x_ref, near_ref, far_ref, gain_ref, wq_ref, wk_ref, wv_ref, wo_ref, wup_ref, wdn_ref,
+                y_ref, stat_ref, *refs)
+
+
+def layer_steps(pair, pairs, x_ref, near_ref, far_ref, gain_ref, wq_ref, wk_ref, wv_ref, wo_ref, wup_ref, wdn_ref,
+                y_ref, stat_ref, wq_t, wv_t, wo_t, wup_t, wdn_t, pos, g1, g2, n1, n2, hidden, sums, *bufs):
     length = pos.shape[1]
     slots = (bufs[0:5], bufs[5:10])
     ctx, scores, weights = bufs[10], bufs[11 : 12 + LEAD], bufs[12 + LEAD :]
-    step, last = pl.program_id(0), pl.num_programs(0) - 1
+    step, last = pl.program_id(0), pairs
+
+    def out_part(sub):
+        if stat_ref is not None:
+            return pair(y_ref, sub)
+        half = y_ref.shape[1] // 2
+        return y_ref.at[:, sub * half : (sub + 1) * half]
 
     def run(sub, a, b, c):
         here, other = slots[sub], slots[1 - sub]
         left, right = [], []
         if c:
-            left = pieces_c(here[4], g2[:, :1], wup_t, wdn_t, pair(y_ref, sub), sums, n2, hidden)
+            left = pieces_c(here[4], g2[:, :1], wup_t, wdn_t, out_part(sub), sums, n2, hidden)
         if a:
             get = lambda: pair(x_ref, sub)[...].reshape(length, D)
             right = pieces_a(get, pos, g1[:, :1], wq_t, wv_t, wk_ref, *here[:4], n1)
@@ -182,12 +198,22 @@
     def _():
         run(0, False, True, True)
         run(1, False, False, True)
-        rows = [jnp.sum(sums[k], axis=0, keepdims=True) for k in range(2)]
-        tile = jnp.concatenate(rows + [jnp.zeros((6, 128), F32)], axis=0)
-        stat_ref[...] = jnp.broadcast_to(tile[None], stat_ref.shape)
-
-
-def layer(x, count, x_block, x_map, pair, length, level, gain, weights, peers, name):
+        if stat_ref is not None:
+            rows = [jnp.sum(sums[k], axis=0, keepdims=True) for k in range(2)]
+            tile = jnp.concatenate(rows + [jnp.zeros((6, 128), F32)], axis=0)
+            stat_ref[...] = jnp.broadcast_to(tile[None], stat_ref.shape)
+
+    if stat_ref is None:
+        @pl.when(step == last + 1)
+        def _():
+            rows = [jnp.sum(sums[k], axis=0, keepdims=True) for k in range(2)]
+            terms = [t.astype(F32) for r in rows for t in split_three(r)]
+            tile = jnp.concatenate(terms + [jnp.zeros((y_ref.shape[1] - 6, 128), F32)], axis=0)
+            tile = jnp.concatenate([tile, jnp.zeros_like(tile)], axis=1).astype(BF16)
+            y_ref[...] = jnp.broadcast_to(tile[None], y_ref.shape)
+
+
+def layer(x, count, x_block, x_map, pair, length, level, gain, weights, joined, peers, name):
     near, far = pos_parts(length)
     pick = lambda a: pl.BlockSpec((None, *a.shape[1:]), lambda i: (level,) + (0,) * (a.ndim - 1))
     whole = lambda a: pl.BlockSpec(a.shape, lambda i: (0,) * a.ndim)
@@ -196,14 +222,22 @@
         pltpu.VMEM((D, length), F32), pltpu.VMEM((D, length), BF16), pltpu.VMEM((length, D), BF16),
         pltpu.VMEM((HEADS * AUG, length), BF16), pltpu.VMEM((D, length), F32),
     ]
+    if joined is None:
+        steps = pairs + 1
+        out_specs = [pl.BlockSpec(x_block, lambda i: x_map(jnp.maximum(i - 1, 0))),
+                     pl.BlockSpec((peers, 8, 128), lambda i: (0, 0, 0))]
+        out_shape = [jax.ShapeDtypeStruct(x.shape, BF16), jax.ShapeDtypeStruct((peers, 8, 128), F32)]
+    else:
+        steps = pairs + 2
+        out_specs = pl.BlockSpec((peers, (joined[1] - 8) // pairs, D), lambda i: (0, jnp.maximum(i - 1, 0), 0))
+        out_shape = jax.ShapeDtypeStruct(joined, BF16)
     return pl.pallas_call(
-        functools.partial(layer_kernel, pair),
-        grid=(pairs + 1,),
+        functools.partial(layer_kernel, pair, pairs, joined is not None),
+        grid=(steps,),
         in_specs=[pl.BlockSpec(x_block, lambda i: x_map(jnp.minimum(i, pairs - 1))),
                   whole(near), whole(far), pick(gain)] + [pick(w) for w in weights],
-        out_specs=[pl.BlockSpec(x_block, lambda i: x_map(jnp.maximum(i - 1, 0))),
-                   pl.BlockSpec((peers, 8, 128), lambda i: (0, 0, 0))],
-        out_shape=[jax.ShapeDtypeStruct(x.shape, BF16), jax.ShapeDtypeStruct((peers, 8, 128), F32)],
+        out_specs=out_specs,
+        out_shape=out_shape,
         scratch_shapes=[
             pltpu.VMEM((D, D), BF16), pltpu.VMEM((D, D), BF16), pltpu.VMEM((D, D), BF16),
             pltpu.VMEM((FF, D), BF16), pltpu.VMEM((D, FF), BF16),
@@ -217,29 +251,62 @@
     )(x, jnp.asarray(near), jnp.asarray(far), gain, *weights)
 
 
-def blend_kernel(cells, stat_ref, out_ref, res_ref, gain_ref, bias_ref, final_ref):
-    parts = jnp.sum(stat_ref[...], axis=0)
-    center = jnp.sum(parts[0:1, :], axis=1, keepdims=True) / cells
-    spread = jnp.sum(parts[1:2, :], axis=1, keepdims=True) / cells - center * center
-    slope = gain_ref[...] * lax.rsqrt(spread + EPS)
-    shifted = out_ref[...].astype(F32) - center[None]
-    final = slope[None] * shifted + bias_ref[...][None] + res_ref[...].astype(F32)
-    final_ref[...] = jnp.swapaxes(final, 0, 1).astype(BF16)
-
-
-def blend(stat, out, residual, gain, bias, cells, in_block, in_map, steps, name):
-    first, second, _ = out.shape
-    block = pl.BlockSpec(in_block, in_map)
+def split_three(x):
+    high = x.astype(BF16)
+    rest = x - high.astype(F32)
+    mid = rest.astype(BF16)
+    return high, mid, (rest - mid.astype(F32)).astype(BF16)
+
+
+class ByFrame:
+    def __init__(self, ref, own, segs):
+        self.ref, self.own, self.segs = ref, own, segs
+
+    def __getitem__(self, i):
+        peer, frame = divmod(i, self.own)
+        return self.ref[peer, frame * self.segs : (frame + 1) * self.segs, :]
+
+
+def blend_kernel(cells, level, stat_ref, out_ref, res_ref, gain_ref, bias_ref, final_ref, *halves):
+    if stat_ref.dtype == BF16:
+        rows = jnp.sum(stat_ref[...].astype(F32), axis=0)
+        sums = [jnp.sum(rows[3 * k : 3 * k + 3, :], axis=(0, 1), keepdims=True) for k in range(2)]
+    else:
+        rows = jnp.sum(stat_ref[...], axis=0)
+        sums = [jnp.sum(rows[k : k + 1, :], axis=(0, 1), keepdims=True) for k in range(2)]
+    center = sums[0] / cells
+    spread = sums[1] / cells - center * center
+    slope = gain_ref[level : level + 1, :] * lax.rsqrt(spread + EPS)
+    one, two, _ = res_ref.shape
+    pitch = two + 8
+    for i in range(one):
+        data = out_ref[i].astype(F32) - center
+        final = slope * data + bias_ref[level : level + 1, :] + res_ref[i].astype(F32)
+        for k, half in enumerate(halves):
+            half[i * pitch : i * pitch + two, :] = final[:, k * 128 : (k + 1) * 128]
+    for j in range(two):
+        for k, half in enumerate(halves):
+            final_ref[j, :, k * 128 : (k + 1) * 128] = half[pl.ds(j, one, stride=pitch), :].astype(BF16)
+
+
+def blend(stat, stat_spec, out, out_spec, out_view, residual, res_block, res_map, gain, bias, level, cells, steps, name):
+    first, second, _ = residual.shape
     whole = lambda a: pl.BlockSpec(a.shape, lambda i: (0,) * a.ndim)
-    def out_map(i):
-        one, two, _ = in_map(i)
+
+    def final_map(i):
+        one, two, _ = res_map(i)
         return two, one, 0
+
+    def kernel(stat_ref, out_ref, *rest):
+        blend_kernel(cells, level, stat_ref, out_view(out_ref), *rest)
+
     return pl.pallas_call(
-        functools.partial(blend_kernel, cells),
+        kernel,
         grid=(steps,),
-        in_specs=[whole(stat), block, block, whole(gain), whole(bias)],
-        out_specs=pl.BlockSpec((in_block[1], in_block[0], D), out_map),
+        in_specs=[stat_spec, out_spec, pl.BlockSpec(res_block, res_map), whole(gain), whole(bias)],
+        out_specs=pl.BlockSpec((res_block[1], res_block[0], D), final_map),
         out_shape=jax.ShapeDtypeStruct((second, first, D), BF16),
+        scratch_shapes=[pltpu.VMEM((res_block[0] * (res_block[1] + 8), 128), F32)] * 2,
         compiler_params=pltpu.CompilerParams(dimension_semantics=("arbitrary",)),
         name=name,
     )(stat, out, residual, gain, bias)
@@ -255,20 +322,22 @@
     steps = 4
 
     intra, stat = layer(mixture, segs, (2, frames, D), lambda i: (i, 0, 0), lambda r, k: r.at[k], frames,
-                        0, ln_gain, weights, shards, name="intra")
+                        0, ln_gain, weights, None, shards, name="intra")
     stat = lax.all_to_all(stat, "span", split_axis=0, concat_axis=0, tiled=True)
-    across = blend(stat, intra, mixture, gln_gain[0:1], gln_bias[0:1], cells,
-                   (segs, frames // steps, D), lambda i: (0, i, 0), steps, "blend_intra")
+    block = (segs, frames // steps, D)
+    spread = lambda i: (0, i, 0)
+    across = blend(stat, pl.BlockSpec(stat.shape, lambda i: (0, 0, 0)), intra, pl.BlockSpec(block, spread), lambda r: r,
+                   mixture, block, spread, gln_gain, gln_bias, 0, cells, steps, "blend_intra")
     moved = lax.all_to_all(across.reshape(shards, own, segs, D), "span", split_axis=0, concat_axis=0, tiled=True)
 
-    inter, stat = layer(moved, own, (shards, 2, segs, D), lambda i: (0, i, 0, 0), lambda r, k: r.at[:, k], total,
-                        1, ln_gain, weights, 1, name="inter")
+    rows = own * segs
+    inter = layer(moved, own, (shards, 2, segs, D), lambda i: (0, i, 0, 0), lambda r, k: r.at[:, k], total,
+                  1, ln_gain, weights, (shards, rows + 8, D), shards, name="inter")
     back = lax.all_to_all(inter, "span", split_axis=0, concat_axis=0, tiled=True)
-    stat = stat[0]
-    for bit in range(shards.bit_length() - 1):
-        stat = stat + lax.ppermute(stat, "span", [(i, i ^ (1 << bit)) for i in range(shards)])
-    return blend(stat[None], back.reshape(frames, segs, D), across, gln_gain[1:2], gln_bias[1:2], cells,
-                 (frames // steps, segs, D), lambda i: (i, 0, 0), steps, "blend_inter")
+    peers = shards // steps
+    return blend(back, pl.BlockSpec((shards, 8, D), lambda i: (0, rows // 8, 0)),
+                 back, pl.BlockSpec((peers, rows, D), lambda i: (i, 0, 0)), lambda r: ByFrame(r, own, segs),
+                 across, (frames // steps, segs, D), lambda i: (i, 0, 0), gln_gain, gln_bias, 1, cells, steps, "blend_inter")
 
 
 def solution(mesh):

time: 159 us -> 149 us (0.937)
  the two profiles are of different devices: /device:TPU:70 before, /device:TPU:1 now
where the time goes in v4:
time: 149 us; the launch traced here: 148 us
  blocking collectives  84.2 us (57%)
  Pallas kernels  63.8 us (43%)
    pallas_call x2, Pallas kernels, layer(): pl.pallas_call(functools.partial(layer_kernel, pair, pairs, joined is not...  53.3 us
    all_to_all x1, blocking collectives, body(): lax.all_to_all(inter, 'span', split_axis=0, concat_axis=0, tiled=True)  34.8 us
    all_to_all x1, blocking collectives, body(): lax.all_to_all(across.reshape(shards, own, segs, D), 'span', split_axis=0...  33 us
    all_to_all x1, blocking collectives, body(): stat = lax.all_to_all(stat, 'span', split_axis=0, concat_axis=0, tiled=True)  16.4 us
    pallas_call x2, Pallas kernels, blend(): pl.pallas_call(kernel, grid=(steps,), in_specs=[stat_spec, out_spec, pl.B...  10.5 us

profile of v4, /device:TPU:1, one launch (start us, length us, event | category | flops | bytes accessed | tf_op | source)
XLA Modules:
  0.0 148.0 jit_solution(17459124930440888745)
XLA Ops:
  0.0 23.5 %intra.1 = (bf16[16,256,256]{2,1,0:T(8,128)(2,1)}, f32[32,8,128]{2,1,0:T(8,128)}) custom-call(bf16[16,256,256]{2,1,0:T(8,128)(2,1)} %rest_0_.1, f32[2,256,128]{2,1,0:T(8,128)} %constant.6.clone.near_ref, f32[512,128]{1,0:T(8,128)} %constant.7.clone.far_ref, f32[2,2,256]{2,1,0:T(2,128)} %gain_ref.3, bf16[2,256,256]{2,1,0:T(8,128)(2,1)} %wq_ref.3, ...), custom_call_target="tpu_custom_call" | custom-call | tf_op jit(solution)/shard_map/intra/pallas_call | solution.py:234
  23.5 16.4 %all_to_all.15.stat_ref = f32[32,8,128]{2,1,0:T(8,128)} all-to-all(f32[32,8,128]{2,1,0:T(8,128)} %get-tuple-element.7), channel_id=1, replica_groups=mesh['mix'=4,'span'=32] {'span'}, dimensions={0} | all-to-all | bytes 262144 | tf_op jit(solution)/shard_map/all_to_all | solution.py:326
  39.9 5.3 %blend_intra.1.rest_0_ = bf16[256,16,256]{2,1,0:T(8,128)(2,1)} custom-call(f32[32,8,128]{2,1,0:T(8,128)} %all_to_all.15.stat_ref, bf16[16,256,256]{2,1,0:T(8,128)(2,1)} %get-tuple-element.8.out_ref, bf16[16,256,256]{2,1,0:T(8,128)(2,1)} %rest_0_.1, f32[2,256]{1,0:T(2,128)} %rest_1_.3, f32[2,256]{1,0:T(2,128)} %rest_2_.3), custom_call_target="tpu_custom_call" | custom-call | tf_op jit(solution)/shard_map/blend_intra/pallas_call | solution.py:303
  45.2 33.0 %all_to_all.16.x_ref = bf16[32,8,16,256]{3,2,1,0:T(8,128)(2,1)} all-to-all(bf16[32,8,16,256]{3,2,1,0:T(8,128)(2,1)} %bitcast.1), channel_id=1, replica_groups=mesh['mix'=4,'span'=32] {'span'}, dimensions={0} | all-to-all | bytes 4194304 | tf_op jit(solution)/shard_map/all_to_all | solution.py:331
  78.2 29.8 %inter.1 = bf16[32,136,256]{2,1,0:T(8,128)(2,1)} custom-call(bf16[32,8,16,256]{3,2,1,0:T(8,128)(2,1)} %all_to_all.16.x_ref, f32[2,256,128]{2,1,0:T(8,128)} %constant.6.clone.near_ref, f32[512,128]{1,0:T(8,128)} %constant.8.clone.far_ref, f32[2,2,256]{2,1,0:T(2,128)} %gain_ref.3, bf16[2,256,256]{2,1,0:T(8,128)(2,1)} %wq_ref.3, bf16[2,256,256]{2,1,0:T(8,128)(2,1)} %wk_ref.3, ...), custom_call_target="tpu_custom_call" | custom-call | tf_op jit(solution)/shard_map/inter/pallas_call | solution.py:234
  108.0 34.8 %all_to_all.17.stat_ref.out_ref = bf16[32,136,256]{2,1,0:T(8,128)(2,1)} all-to-all(bf16[32,136,256]{2,1,0:T(8,128)(2,1)} %inter.1), channel_id=1, replica_groups=mesh['mix'=4,'span'=32] {'span'}, dimensions={0} | all-to-all | bytes 4456448 | tf_op jit(solution)/shard_map/all_to_all | solution.py:336
  142.8 5.2 %blend_inter.1 = bf16[16,256,256]{2,1,0:T(8,128)(2,1)} custom-call(bf16[32,136,256]{2,1,0:T(8,128)(2,1)} %all_to_all.17.stat_ref.out_ref, bf16[32,136,256]{2,1,0:T(8,128)(2,1)} %all_to_all.17.stat_ref.out_ref, bf16[256,16,256]{2,1,0:T(8,128)(2,1)} %blend_intra.1.rest_0_, f32[2,256]{1,0:T(2,128)} %rest_1_.3, f32[2,256]{1,0:T(2,128)} %rest_2_.3), custom_call_target="tpu_custom_call" | custom-call | tf_op jit(solution)/shard_map/blend_inter/pallas_call | solution.py:303

commit v5 on v3

v5 whole, which is shorter than its diff:
```python
import functools
import math

import jax
import numpy as np
import jax.numpy as jnp
from jax import lax
from jax.experimental import pallas as pl
from jax.experimental.pallas import tpu as pltpu
from jax.sharding import PartitionSpec as P


D = 256
HEADS = 8
HD = D // HEADS
FF = 1024
EPS = 1e-05
AUG = HD + 16
F32 = jnp.float32
BF16 = jnp.bfloat16


def pos_parts():
    column = np.arange(D)
    rates = np.exp(-(2 * (column // 2)) / D * math.log(10000.0))[:, None]
    near = np.arange(128)[None, :] * rates
    far = 128 * np.arange(8)[None, :] * rates
    even = (column % 2 == 0)[:, None]
    outer = np.where(even, np.sin(far), np.cos(far))
    swap = np.where(even, np.cos(far), -np.sin(far))
    return (np.stack([np.cos(near), np.sin(near)]).astype(np.float32),
            np.concatenate([outer, swap], axis=0).T.astype(np.float32))


def dot(a, b):
    return lax.dot_general(a, b, (((1,), (0,)), ((), ())), preferred_element_type=F32)


def norm_cols(x, gain):
    center = jnp.mean(x, axis=0, keepdims=True)
    shifted = x - center
    spread = jnp.mean(shifted * shifted, axis=0, keepdims=True)
    return shifted * lax.rsqrt(spread + EPS) * gain


CHUNK = 256
LEAD = 2
TRAIL = 1


def score_unit(q_t, keys, c, h):
    block, at = divmod(h * HD, 128)
    parts = []
    if at:
        parts.append(jnp.zeros((at, CHUNK), BF16))
    parts.append(q_t[h * HD : (h + 1) * HD, c * CHUNK : (c + 1) * CHUNK])
    if at + HD < 128:
        parts.append(jnp.zeros((128 - at - HD, CHUNK), BF16))
    return dot(keys[:, block * 128 : (block + 1) * 128], jnp.concatenate(parts, axis=0))


def run_step(fills, b, scores, weights, ctx):
    if b is None:
        for piece in fills:
            piece()
        return
    x_res, q_t, keys, vaug, after, wo_t = b
    units = [(c, h) for c in range(q_t.shape[1] // CHUNK) for h in range(HEADS)]
    tops = {}
    n = len(units)
    slots = n + LEAD + TRAIL
    done = 0
    for u in range(slots):
        if u < n:
            s = score_unit(q_t, keys, *units[u])
            tops[u] = jnp.max(s, axis=0, keepdims=True)
            scores[u % len(scores)][...] = s
        v = u - LEAD
        if 0 <= v < n:
            s = scores[v % len(scores)][...]
            weights[v % len(weights)][...] = jnp.exp2(s - tops.pop(v)).astype(BF16)
        w = v - TRAIL
        if 0 <= w < n:
            c, h = units[w]
            mixed = dot(vaug[h * AUG : (h + 1) * AUG, :], weights[w % len(weights)][...])
            ctx[h * HD : (h + 1) * HD, c * CHUNK : (c + 1) * CHUNK] = (
                mixed[:HD, :] * (1.0 / mixed[HD : HD + 1, :])
            ).astype(BF16)
        upto = len(fills) * (u + 1) // slots
        for piece in fills[done:upto]:
            piece()
        done = upto
    after[...] = x_res[...] + dot(wo_t[...], ctx[...])


def pieces_a(x, pos, g1, wq_t, wv_t, w_k, x_res, q_t, keys, vaug, n1):
    def first():
        xt = x().T.astype(F32) + pos[...]
        x_res[...] = xt
        n1[...] = norm_cols(xt, g1).astype(BF16)

    def get_keys():
        keys[...] = dot(n1[...].T, w_k[...]).astype(BF16)

    def get_queries():
        scale = math.log2(math.e) / math.sqrt(HD)
        q_t[...] = (dot(wq_t[...], n1[...]) * scale).astype(BF16)

    def get_values():
        v_t = dot(wv_t[...], n1[...]).astype(BF16)
        for h in range(HEADS):
            vaug[h * AUG : h * AUG + HD, :] = v_t[h * HD : (h + 1) * HD, :]

    return [first, get_keys, get_queries, get_values]


def global_norm(rows, gain, bias, cells):
    total = [jnp.sum(rows[3 * k : 3 * k + 3, :], axis=(0, 1), keepdims=True) for k in range(2)]
    center = total[0] / cells
    spread = total[1] / cells - center * center
    slope = gain * lax.rsqrt(spread + EPS)
    return slope, bias - slope * center


def split_three(x):
    high = x.astype(BF16)
    rest = x - high.astype(F32)
    mid = rest.astype(BF16)
    return high, mid, (rest - mid.astype(F32)).astype(BF16)


def stat_rows(sums, count):
    terms = [t.astype(F32) for k in range(2) for t in split_three(jnp.sum(sums[k], axis=0, keepdims=True))]
    tile = jnp.concatenate(terms + [jnp.zeros((count - 6, 128), F32)], axis=0)
    return jnp.concatenate([tile, jnp.zeros_like(tile)], axis=1).astype(BF16)


def pieces_c(after, g2, wup_t, wdn_t, emit, sums, valid, n2, hidden):
    def first():
        n2[...] = norm_cols(after[...], g2).astype(BF16)

    def up(j):
        rows = slice(j * D, (j + 1) * D)
        hidden[rows, :] = jnp.maximum(dot(wup_t[rows, :], n2[...]), 0.0).astype(BF16)

    def down():
        y_t = after[...] + dot(wdn_t[...], hidden[...])
        part = y_t.reshape(D // 8, 8, y_t.shape[1])
        for k in range(y_t.shape[1] // 128):
            lanes = slice(k * 128, (k + 1) * 128)
            sums[0] += jnp.where(valid, jnp.sum(part[:, :, lanes], axis=0), 0.0)
            sums[1] += jnp.where(valid, jnp.sum(part[:, :, lanes] * part[:, :, lanes], axis=0), 0.0)
        emit(y_t.astype(BF16).T)

    return [first] + [functools.partial(up, j) for j in range(FF // D)] + [down]


def layer_steps(pairs, prepare, get, emit, near_ref, far_ref, gain_ref, wq_ref, wk_ref, wv_ref, wo_ref, wup_ref, wdn_ref,
                wq_t, wv_t, wo_t, wup_t, wdn_t, pos, g1, g2, n1, n2, hidden, sums, *bufs):
    length = pos.shape[1]
    slots = (bufs[0:5], bufs[5:10])
    ctx, scores, weights = bufs[10], bufs[11 : 12 + LEAD], bufs[12 + LEAD :]
    step = pl.program_id(0)

    def run(sub, a, b, c):
        here, other = slots[sub], slots[1 - sub]
        left, right = [], []
        if c:
            left = pieces_c(here[4], g2[:, :1], wup_t, wdn_t, functools.partial(emit, sub), sums, step > 0, n2, hidden)
        if a:
            right = pieces_a(lambda: get(sub), pos, g1[:, :1], wq_t, wv_t, wk_ref, *here[:4], n1)
        fills = []
        while left or right:
            fills += left[:1] + right[:1]
            left, right = left[1:], right[1:]
        run_step(fills, (*other, wo_t) if b else None, scores, weights, ctx)

    @pl.when(step == 0)
    def _():
        wq_t[...] = wq_ref[...].T
        wv_t[...] = wv_ref[...].T
        wo_t[...] = wo_ref[...].T
        wup_t[...] = wup_ref[...].T
        wdn_t[...] = wdn_ref[...].T
        g1[...] = jnp.broadcast_to(gain_ref[0:1, :], (128, D)).T
        g2[...] = jnp.broadcast_to(gain_ref[1:2, :], (128, D)).T
        far = far_ref[...].T
        for a in range(length // 128):
            pos[:, a * 128 : (a + 1) * 128] = far[:D, a : a + 1] * near_ref[0] + far[D:, a : a + 1] * near_ref[1]
        for slot in slots:
            slot[3][...] = jnp.ones_like(slot[3])
        sums[...] = jnp.zeros_like(sums)
        prepare()
        run(0, True, False, False)

    @pl.when((step > 0) & (step <= pairs))
    def _():
        run(0, True, True, True)

    @pl.when(step < pairs)
    def _():
        run(1, True, True, True)

    @pl.when(step == pairs)
    def _():
        run(1, False, False, True)


def layer_consts(length, level, gain, weights):
    near, far = pos_parts()
    pick = lambda a: pl.BlockSpec((None, *a.shape[1:]), lambda i: (level,) + (0,) * (a.ndim - 1))
    whole = lambda a: pl.BlockSpec(a.shape, lambda i: (0,) * a.ndim)
    slot = [
        pltpu.VMEM((D, length), F32), pltpu.VMEM((D, length), BF16), pltpu.VMEM((length, D), BF16),
        pltpu.VMEM((HEADS * AUG, length), BF16), pltpu.VMEM((D, length), F32),
    ]
    scratch = [
        pltpu.VMEM((D, D), BF16), pltpu.VMEM((D, D), BF16), pltpu.VMEM((D, D), BF16),
        pltpu.VMEM((FF, D), BF16), pltpu.VMEM((D, FF), BF16),
        pltpu.VMEM((D, length), F32), pltpu.VMEM((D, 128), F32), pltpu.VMEM((D, 128), F32),
        pltpu.VMEM((D, length), BF16), pltpu.VMEM((D, length), BF16), pltpu.VMEM((FF, length), BF16),
        pltpu.VMEM((2, 8, 128), F32), *slot, *slot, pltpu.VMEM((D, length), BF16),
        *[pltpu.VMEM((length, CHUNK), F32)] * (LEAD + 1), *[pltpu.VMEM((length, CHUNK), BF16)] * (TRAIL + 1),
    ]
    values = (jnp.asarray(near), jnp.asarray(far), gain, *weights)
    specs = [whole(near), whole(far), pick(gain)] + [pick(w) for w in weights]
    return values, specs, scratch


def layer_cost(rows, length):
    dense = 2 * rows * (4 * D * D + 2 * D * FF)
    return pl.CostEstimate(flops=dense + 4 * rows * length * D, transcendentals=rows * length * HEADS,
                           bytes_accessed=4 * rows * D + 4 * D * (2 * D + FF))


PARAMS = pltpu.CompilerParams(dimension_semantics=("arbitrary",))


def intra_layer(mixture, gain, weights, peers, own):
    segs, frames, _ = mixture.shape
    half = frames // 2
    pairs, pitch = segs // 2, half + 8
    values, specs, scratch = layer_consts(frames, 0, gain, weights)

    def kernel(x_ref, *refs):
        n = len(values)
        y_ref, sent_ref = refs[n : n + 2]
        kept = refs[n + 2 : n + 4]
        work = refs[n + 4 :]
        step = pl.program_id(0)

        def emit(sub, y):
            y_ref[sub] = y
            at = pl.multiple_of(jnp.maximum(2 * step - 2 + sub, 0) * pitch, 8)
            for k, part in enumerate(kept):
                part[pl.ds(at, half), :] = y[:half, k * 128 : (k + 1) * 128].astype(F32)

        layer_steps(pairs, lambda: None, lambda sub: x_ref[sub], emit, *refs[:n], *work)

        @pl.when(step == pairs)
        def _():
            for f in range(half):
                p, j = divmod(f, own)
                for k, part in enumerate(kept):
                    sent_ref[p, j * segs : (j + 1) * segs, k * 128 : (k + 1) * 128] = (
                        part[pl.ds(f, segs, stride=pitch), :].astype(BF16))
            tile = stat_rows(work[11], 8)
            for p in range(peers):
                sent_ref[p, own * segs :, :] = tile

    rows = own * segs + 8
    return pl.pallas_call(
        kernel,
        grid=(pairs + 1,),
        in_specs=[pl.BlockSpec((2, frames, D), lambda i: (jnp.minimum(i, pairs - 1), 0, 0))] + specs,
        out_specs=[pl.BlockSpec((2, frames, D), lambda i: (jnp.maximum(i - 1, 0), 0, 0)),
                   pl.BlockSpec((peers, rows, D), lambda i: (0, 0, 0))],
        out_shape=[jax.ShapeDtypeStruct(mixture.shape, BF16), jax.ShapeDtypeStruct((peers, rows, D), BF16)],
        scratch_shapes=[pltpu.VMEM((segs * pitch, 128), F32)] * 2 + scratch,
        compiler_params=PARAMS,
        cost_estimate=layer_cost(segs * frames, frames),
        name="intra",
    )(mixture, *values)


def inter_layer(moved, sent, gln_gain, gln_bias, cells, gain, weights):
    peers, own, segs, _ = moved.shape
    total, pairs, rows = peers * segs, own // 2, own * segs
    values, specs, scratch = layer_consts(total, 1, gain, weights)
    whole = lambda a: pl.BlockSpec(a.shape, lambda i: (0,) * a.ndim)
    pick = lambda i: jnp.minimum(i, pairs - 1)
    extra, extra_specs = (), []
    if sent is not None:
        extra = (sent, sent, gln_gain, gln_bias)
        extra_specs = [pl.BlockSpec((peers, 2 * segs, D), lambda i: (0, pick(i), 0)),
                       pl.BlockSpec((peers, 8, D), lambda i: (0, rows // 8, 0)), whole(gln_gain), whole(gln_bias)]

    def kernel(x_ref, *refs):
        m, n = len(extra), len(extra) + len(values)
        y_ref, affine = refs[n : n + 2]
        work = refs[n + 2 :]
        step = pl.program_id(0)

        def prepare():
            if m:
                sums = jnp.sum(refs[1][...].astype(F32), axis=0)
                slope, offset = global_norm(sums, refs[2][0:1, :], refs[3][0:1, :], cells)
                affine[0:1, :] = slope
                affine[1:2, :] = offset

        def get(sub):
            x = x_ref[:, sub].reshape(total, D)
            if m:
                y = refs[0][:, sub * segs : (sub + 1) * segs].reshape(total, D)
                x = (affine[0:1, :] * y.astype(F32) + affine[1:2, :] + x.astype(F32)).astype(BF16)
            return x

        def emit(sub, y):
            y_ref[:, sub * segs : (sub + 1) * segs] = y.reshape(peers, segs, D)

        layer_steps(pairs, prepare, get, emit, *refs[m:n], *work)

        @pl.when(step == pairs + 1)
        def _():
            y_ref[...] = jnp.broadcast_to(stat_rows(work[11], 2 * segs)[None], y_ref.shape)

    return pl.pallas_call(
        kernel,
        grid=(pairs + 2,),
        in_specs=[pl.BlockSpec((peers, 2, segs, D), lambda i: (0, pick(i), 0, 0))] + extra_specs + specs,
        out_specs=pl.BlockSpec((peers, 2 * segs, D), lambda i: (0, jnp.maximum(i - 1, 0), 0)),
        out_shape=jax.ShapeDtypeStruct((peers, rows + 8, D), BF16),
        scratch_shapes=[pltpu.VMEM((2, D), F32)] + scratch,
        compiler_params=PARAMS,
        cost_estimate=layer_cost(rows * peers, total),
    )(moved, *extra, *values)


def blend_rest(sent, intra, mixture, gln_gain, gln_bias, cells, width):
    segs, frames, _ = mixture.shape
    half, rows = frames // 2, sent.shape[1]
    pitch = width + 8
    whole = lambda a: pl.BlockSpec(a.shape, lambda i: (0,) * a.ndim)
    block = pl.BlockSpec((segs, width, D), lambda i: (0, half // width + i, 0))

    def kernel(stat_ref, y_ref, x_ref, gain_ref, bias_ref, out_ref, *parts):
        sums = jnp.sum(stat_ref[...].astype(F32), axis=0)
        slope, offset = global_norm(sums, gain_ref[0:1, :], bias_ref[0:1, :], cells)
        for s in range(segs):
            mixed = slope * y_ref[s].astype(F32) + offset + x_ref[s].astype(F32)
            for k, part in enumerate(parts):
                part[s * pitch : s * pitch + width, :] = mixed[:, k * 128 : (k + 1) * 128]
        for f in range(width):
            for k, part in enumerate(parts):
                out_ref[f, :, k * 128 : (k + 1) * 128] = part[pl.ds(f, segs, stride=pitch), :].astype(BF16)

    return pl.pallas_call(
        kernel,
        grid=(half // width,),
        in_specs=[pl.BlockSpec((sent.shape[0], 8, D), lambda i: (0, rows // 8 - 1, 0)), block, block,
                  whole(gln_gain), whole(gln_bias)],
        out_specs=pl.BlockSpec((width, segs, D), lambda i: (i, 0, 0)),
        out_shape=jax.ShapeDtypeStruct((half, segs, D), BF16),
        scratch_shapes=[pltpu.VMEM((segs * pitch, 128), F32)] * 2,
        compiler_params=PARAMS,
        name="blend_rest",
    )(sent, intra, mixture, gln_gain, gln_bias)


def blend_final(sent, backs, intra, mixture, gln_gain, gln_bias, cells, width, own):
    segs, frames, _ = mixture.shape
    peers, rows, _ = backs[0].shape
    count, pitch = width // own, segs + 8
    steps = frames // width
    whole = lambda a: pl.BlockSpec(a.shape, lambda i: (0,) * a.ndim)
    stat_spec = pl.BlockSpec((peers, 8, D), lambda i: (0, rows // 8 - 1, 0))
    block = pl.BlockSpec((segs, width, D), lambda i: (0, i, 0))

    def kernel(stat_ref, one_ref, two_ref, first_ref, second_ref, y_ref, x_ref, gain_ref, bias_ref, out_ref, affine, *parts):
        step = pl.program_id(0)

        @pl.when(step == 0)
        def _():
            sums = jnp.sum(stat_ref[...].astype(F32), axis=0)
            affine[0:1, :], affine[1:2, :] = global_norm(sums, gain_ref[0:1, :], bias_ref[0:1, :], cells)
            sums = jnp.sum(one_ref[...].astype(F32) + two_ref[...].astype(F32), axis=0)
            affine[2:3, :], affine[3:4, :] = global_norm(sums, gain_ref[1:2, :], bias_ref[1:2, :], cells)

        def lay(ref):
            for f in range(width):
                p, j = divmod(f, own)
                z = affine[2:3, :] * ref[p, j * segs : (j + 1) * segs, :].astype(F32) + affine[3:4, :]
                for k, part in enumerate(parts):
                    part[f * pitch : f * pitch + segs, :] = z[:, k * 128 : (k + 1) * 128]

        pl.when(step < steps // 2)(lambda: lay(first_ref))
        pl.when(step >= steps // 2)(lambda: lay(second_ref))
        for s in range(segs):
            mixed = (affine[0:1, :] * y_ref[s].astype(F32) + affine[1:2, :] + x_ref[s].astype(F32)).astype(BF16)
            for k, part in enumerate(parts):
                lanes = slice(k * 128, (k + 1) * 128)
                out_ref[s, :, lanes] = (part[pl.ds(s, width, stride=pitch), :] + mixed[:, lanes].astype(F32)).astype(BF16)

    spec = lambda m: pl.BlockSpec((count, rows - 8, D), lambda i: (m(i), 0, 0))
    return pl.pallas_call(
        kernel,
        grid=(steps,),
        in_specs=[stat_spec, stat_spec, stat_spec, spec(lambda i: jnp.minimum(i, steps // 2 - 1)),
                  spec(lambda i: jnp.maximum(i - steps // 2, 0)), block, block, whole(gln_gain), whole(gln_bias)],
        out_specs=block,
        out_shape=jax.ShapeDtypeStruct(mixture.shape, BF16),
        scratch_shapes=[pltpu.VMEM((4, D), F32)] + [pltpu.VMEM((width * pitch, 128), F32)] * 2,
        compiler_params=PARAMS,
        name="blend_final",
    )(sent, backs[0], backs[1], backs[0], backs[1], intra, mixture, gln_gain, gln_bias)


def exchange(blocks):
    return lax.all_to_all(blocks, "span", split_axis=0, concat_axis=0, tiled=True)


def body(mixture, w_query, w_key, w_value, w_out, w_up, w_down, ln_gain, gln_gain, gln_bias):
    peers = lax.axis_size("span")
    segs, frames, _ = mixture.shape
    half, own = frames // 2, frames // 2 // peers
    cells = float(segs * peers * frames * D)
    weights = (w_query, w_key, w_value, w_out, w_up, w_down)

    early = exchange(jnp.swapaxes(mixture[:, :half], 0, 1).reshape(peers, own, segs, D))
    intra, sent = intra_layer(mixture, ln_gain, weights, peers, own)
    sent = exchange(sent)
    rest = blend_rest(sent, intra, mixture, gln_gain, gln_bias, cells, 32)
    rest = exchange(rest.reshape(peers, own, segs, D))
    first = inter_layer(early, sent, gln_gain, gln_bias, cells, ln_gain, weights)
    first = exchange(first)
    second = inter_layer(rest, None, None, None, cells, ln_gain, weights)
    second = exchange(second)
    return blend_final(sent, (first, second), intra, mixture, gln_gain, gln_bias, cells, 32, own)


def solution(mesh):
    in_specs = (P(("mix", "span"), None, None), P(), P(), P(), P(), P(), P(), P(), P(), P())
    out_specs = P(("mix", "span"), None, None)
    return jax.shard_map(body, mesh=mesh, in_specs=in_specs, out_specs=out_specs, check_vma=False)
```

time: 159 us -> 160 us (level)
  the two profiles are of different devices: /device:TPU:70 before, /device:TPU:1 now
where the time goes in v5:
time: 160 us
  Pallas kernels  77.1 us (48%)
  waiting for transfers between devices  29.3 us (18%)
  blocking collectives  26.4 us (16%)
  starting transfers between devices  23.9 us (15%)
  local copies, waits for them, and re-layouts  2.63 us (2%)
    pallas_call x2, Pallas kernels, inter_layer(): pl.pallas_call(kernel, grid=(pairs + 2,), in_specs=[pl.BlockSpec((peers,...  39 us
    all_to_all x4, waiting for transfers between devices, exchange(): lax.all_to_all(blocks, 'span', split_axis=0, concat_axis=0, tiled=True)  29.3 us
    all_to_all x1, blocking collectives, exchange(): lax.all_to_all(blocks, 'span', split_axis=0, concat_axis=0, tiled=True)  26.4 us
    pallas_call x1, Pallas kernels, intra_layer(): pl.pallas_call(kernel, grid=(pairs + 1,), in_specs=[pl.BlockSpec((2, fram...  26.3 us
    all_to_all x4, starting transfers between devices, exchange(): lax.all_to_all(blocks, 'span', split_axis=0, concat_axis=0, tiled=True)  23.9 us
    pallas_call x1, Pallas kernels, blend_final(): pl.pallas_call(kernel, grid=(steps,), in_specs=[stat_spec, stat_spec, sta...  7.59 us
    pallas_call x1, Pallas kernels, blend_rest(): pl.pallas_call(kernel, grid=(half // width,), in_specs=[pl.BlockSpec((sen...  4.25 us
  transfers between devices with their start and end apart: 4, of which 2 were waited for; matrix products, arithmetic and copies ran while one was open for 1% of the time, Pallas kernels for 27%

profile of v5, /device:TPU:1, one launch (start us, length us, event | category | flops | bytes accessed | tf_op | source)
XLA Modules:
  0.0 159.5 jit_solution(9674172376950489034)
XLA Ops:
  0.0 26.3 %intra.1 = (bf16[16,256,256]{2,1,0:T(8,128)(2,1)}, bf16[32,72,256]{2,1,0:T(8,128)(2,1)}) custom-call(bf16[16,256,256]{2,1,0:T(8,128)(2,1)} %x_ref.5, f32[2,256,128]{2,1,0:T(8,128)} %constant.4.clone.refs_0_.refs_4_, f32[8,512]{1,0:T(8,128)} %constant.5.clone.refs_1_.refs_5_, f32[2,2,256]{2,1,0:T(2,128)} %refs_2_.5, bf16[2,256,256]{2,1,0:T(8,128)(2,1)} %refs_3_.5, ...), custom_call_target="tpu_custom_call" | custom-call | flops 7516192768 | bytes 5767168 | tf_op jit(solution)/shard_map/intra/pallas_call | solution.py:272
  26.3 0.0 copy-start
  26.3 8.7 %all-to-all-start = ((bf16[32,72,256]{2,1,0:T(8,128)(2,1)}), bf16[32,72,256]{2,1,0:T(8,128)(2,1)S(1)}, u32[]{:S(2)}, u32[]{:S(2)}) async-start(bf16[32,72,256]{2,1,0:T(8,128)(2,1)} %get-tuple-element.7), calls=%async_computation | async-start | bytes 2359296 | tf_op jit(solution)/shard_map/all_to_all | solution.py:419
  35.1 0.0 copy-done
  35.1 0.1 slice_bitcast_fusion
  35.2 1.6 copy.17
  36.7 16.7 %all-to-all-done.refs_0_.refs_1_.stat_ref = bf16[32,72,256]{2,1,0:T(8,128)(2,1)S(1)} async-done(((bf16[32,72,256]{2,1,0:T(8,128)(2,1)}), bf16[32,72,256]{2,1,0:T(8,128)(2,1)S(1)}, u32[]{:S(2)}, u32[]{:S(2)}) %all-to-all-start) | async-done | bytes 1179680 | tf_op jit(solution)/shard_map/all_to_all | solution.py:419
  53.4 0.0 copy-start.1
  53.4 3.9 %all-to-all-start.1 = ((bf16[32,4,16,256]{3,2,1,0:T(8,128)(2,1)}), bf16[32,4,16,256]{3,2,1,0:T(8,128)(2,1)S(1)}, u32[]{:S(2)}, u32[]{:S(2)}) async-start(bf16[32,4,16,256]{3,2,1,0:T(8,128)(2,1)} %bitcast.1), calls=%async_computation.1 | async-start | bytes 2097152 | tf_op jit(solution)/shard_map/all_to_all | solution.py:419
  57.3 0.0 copy-done.1
  57.3 4.2 %blend_rest.1 = bf16[128,16,256]{2,1,0:T(8,128)(2,1)} custom-call(bf16[32,72,256]{2,1,0:T(8,128)(2,1)} %copy-done.1, bf16[16,256,256]{2,1,0:T(8,128)(2,1)} %get-tuple-element.8.y_ref, bf16[16,256,256]{2,1,0:T(8,128)(2,1)} %x_ref.5, f32[2,256]{1,0:T(2,128)} %gain_ref.3, f32[2,256]{1,0:T(2,128)} %bias_ref.3), custom_call_target="tpu_custom_call" | custom-call | tf_op jit(solution)/shard_map/blend_rest/pallas_call | solution.py:357
  61.6 12.7 %all-to-all-done.1.x_ref = bf16[32,4,16,256]{3,2,1,0:T(8,128)(2,1)S(1)} async-done(((bf16[32,4,16,256]{3,2,1,0:T(8,128)(2,1)}), bf16[32,4,16,256]{3,2,1,0:T(8,128)(2,1)S(1)}, u32[]{:S(2)}, u32[]{:S(2)}) %all-to-all-start.1) | async-done | bytes 1048608 | tf_op jit(solution)/shard_map/all_to_all | solution.py:419
  74.2 0.0 copy-start.4
  74.2 3.9 %all-to-all-start.3 = ((bf16[32,4,16,256]{3,2,1,0:T(8,128)(2,1)}), bf16[32,4,16,256]{3,2,1,0:T(8,128)(2,1)S(1)}, u32[]{:S(2)}, u32[]{:S(2)}) async-start(bf16[32,4,16,256]{3,2,1,0:T(8,128)(2,1)} %bitcast.4), calls=%async_computation.3 | async-start | bytes 2097152 | tf_op jit(solution)/shard_map/all_to_all | solution.py:419
  78.2 0.0 copy-done.4
  78.2 19.8 %shard_map.154 = bf16[32,72,256]{2,1,0:T(8,128)(2,1)} custom-call(bf16[32,4,16,256]{3,2,1,0:T(8,128)(2,1)} %copy-done.4, bf16[32,72,256]{2,1,0:T(8,128)(2,1)} %copy-done.1, bf16[32,72,256]{2,1,0:T(8,128)(2,1)} %copy-done.1, f32[2,256]{1,0:T(2,128)} %gain_ref.3, f32[2,256]{1,0:T(2,128)} %bias_ref.3, f32[2,256,128]{2,1,0:T(8,128)} %constant.4.clone.refs_0_.refs_4_, ...), custom_call_target="tpu_custom_call" | custom-call | flops 4294967296 | bytes 3670016 | tf_op jit(solution)/shard_map/pallas_call | solution.py:327
  98.0 0.0 all-to-all-done.3.x_ref
  98.0 0.0 copy-start.3
  98.0 1.0 copy-done.3
  99.0 7.4 %all-to-all-start.2 = ((bf16[32,72,256]{2,1,0:T(8,128)(2,1)}), bf16[32,72,256]{2,1,0:T(8,128)(2,1)S(1)}, u32[]{:S(2)}, u32[]{:S(2)}) async-start(bf16[32,72,256]{2,1,0:T(8,128)(2,1)} %shard_map.154), calls=%async_computation.2 | async-start | bytes 2359296 | tf_op jit(solution)/shard_map/all_to_all | solution.py:419
  106.4 19.1 %shard_map.155 = bf16[32,72,256]{2,1,0:T(8,128)(2,1)} custom-call(bf16[32,4,16,256]{3,2,1,0:T(8,128)(2,1)} %copy-done.3, f32[2,256,128]{2,1,0:T(8,128)} %constant.4.clone.refs_0_.refs_4_, f32[8,512]{1,0:T(8,128)} %constant.5.clone.refs_1_.refs_5_, f32[2,2,256]{2,1,0:T(2,128)} %refs_2_.5, bf16[2,256,256]{2,1,0:T(8,128)(2,1)} %refs_3_.5, ...), custom_call_target="tpu_custom_call" | custom-call | flops 4294967296 | bytes 3670016 | tf_op jit(solution)/shard_map/pallas_call | solution.py:327
  125.5 0.0 all-to-all-done.2.one_ref.first_ref
  125.5 0.0 copy-start.2
  125.5 26.4 %all_to_all.25.two_ref.second_ref = bf16[32,72,256]{2,1,0:T(8,128)(2,1)} all-to-all(bf16[32,72,256]{2,1,0:T(8,128)(2,1)} %shard_map.155), channel_id=1, replica_groups=mesh['mix'=4,'span'=32] {'span'}, dimensions={0} | all-to-all | bytes 2359296 | tf_op jit(solution)/shard_map/all_to_all | solution.py:419
  151.9 0.0 copy-done.2
  151.9 7.6 %blend_final.1 = bf16[16,256,256]{2,1,0:T(8,128)(2,1)} custom-call(bf16[32,72,256]{2,1,0:T(8,128)(2,1)} %copy-done.1, bf16[32,72,256]{2,1,0:T(8,128)(2,1)} %copy-done.2, bf16[32,72,256]{2,1,0:T(8,128)(2,1)} %all_to_all.25.two_ref.second_ref, bf16[32,72,256]{2,1,0:T(8,128)(2,1)} %copy-done.2, bf16[32,72,256]{2,1,0:T(8,128)(2,1)} %all_to_all.25.two_ref.second_ref, ...), custom_call_target="tpu_custom_call" | custom-call | tf_op jit(solution)/shard_map/blend_final/pallas_call | solution.py:405
Async XLA Ops:
  26.3 8.7 %copy-start = (bf16[16,256,256]{2,1,0:T(8,128)(2,1)S(1)}, bf16[16,256,256]{2,1,0:T(8,128)(2,1)}, u32[]{:S(2)}) copy-start(bf16[16,256,256]{2,1,0:T(8,128)(2,1)} %x_ref.5) | copy-start | bytes 6291460
  26.3 27.1 %all-to-all-start = ((bf16[32,72,256]{2,1,0:T(8,128)(2,1)}), bf16[32,72,256]{2,1,0:T(8,128)(2,1)S(1)}, u32[]{:S(2)}, u32[]{:S(2)}) async-start(bf16[32,72,256]{2,1,0:T(8,128)(2,1)} %get-tuple-element.7), calls=%async_computation | async-start | bytes 2359296 | tf_op jit(solution)/shard_map/all_to_all | solution.py:419
  53.4 3.9 %copy-start.1 = (bf16[32,72,256]{2,1,0:T(8,128)(2,1)}, bf16[32,72,256]{2,1,0:T(8,128)(2,1)S(1)}, u32[]{:S(2)}) copy-start(bf16[32,72,256]{2,1,0:T(8,128)(2,1)S(1)} %all-to-all-done.refs_0_.refs_1_.stat_ref) | copy-start | bytes 3538948
  53.4 20.8 %all-to-all-start.1 = ((bf16[32,4,16,256]{3,2,1,0:T(8,128)(2,1)}), bf16[32,4,16,256]{3,2,1,0:T(8,128)(2,1)S(1)}, u32[]{:S(2)}, u32[]{:S(2)}) async-start(bf16[32,4,16,256]{3,2,1,0:T(8,128)(2,1)} %bitcast.1), calls=%async_computation.1 | async-start | bytes 2097152 | tf_op jit(solution)/shard_map/all_to_all | solution.py:419
  74.2 3.9 %copy-start.4 = (bf16[32,4,16,256]{3,2,1,0:T(8,128)(2,1)}, bf16[32,4,16,256]{3,2,1,0:T(8,128)(2,1)S(1)}, u32[]{:S(2)}) copy-start(bf16[32,4,16,256]{3,2,1,0:T(8,128)(2,1)S(1)} %all-to-all-done.1.x_ref) | copy-start | bytes 3145732
  74.2 23.8 %all-to-all-start.3 = ((bf16[32,4,16,256]{3,2,1,0:T(8,128)(2,1)}), bf16[32,4,16,256]{3,2,1,0:T(8,128)(2,1)S(1)}, u32[]{:S(2)}, u32[]{:S(2)}) async-start(bf16[32,4,16,256]{3,2,1,0:T(8,128)(2,1)} %bitcast.4), calls=%async_computation.3 | async-start | bytes 2097152 | tf_op jit(solution)/shard_map/all_to_all | solution.py:419
  98.0 1.0 copy-start.3
  99.0 26.5 %all-to-all-start.2 = ((bf16[32,72,256]{2,1,0:T(8,128)(2,1)}), bf16[32,72,256]{2,1,0:T(8,128)(2,1)S(1)}, u32[]{:S(2)}, u32[]{:S(2)}) async-start(bf16[32,72,256]{2,1,0:T(8,128)(2,1)} %shard_map.154), calls=%async_computation.2 | async-start | bytes 2359296 | tf_op jit(solution)/shard_map/all_to_all | solution.py:419
  125.5 26.4 %copy-start.2 = (bf16[32,72,256]{2,1,0:T(8,128)(2,1)}, bf16[32,72,256]{2,1,0:T(8,128)(2,1)S(1)}, u32[]{:S(2)}) copy-start(bf16[32,72,256]{2,1,0:T(8,128)(2,1)S(1)} %all-to-all-done.2.one_ref.first_ref) | copy-start | bytes 3538948

commit v6 on v4

--- a/solution.py
+++ b/solution.py
@@ -23,13 +23,12 @@
     column = np.arange(D)
     rates = np.exp(-(2 * (column // 2)) / D * math.log(10000.0))[:, None]
     near = np.arange(128)[None, :] * rates
-    far = 128 * np.arange(length // 128)[None, :] * rates
+    far = 128 * np.arange(8)[None, :] * rates
     even = (column % 2 == 0)[:, None]
     outer = np.where(even, np.sin(far), np.cos(far))
     swap = np.where(even, np.cos(far), -np.sin(far))
-    far_two = np.zeros((2 * D, 128))
-    far_two[:, : length // 128] = np.concatenate([outer, swap], axis=0)
-    return np.stack([np.cos(near), np.sin(near)]).astype(np.float32), far_two.astype(np.float32)
+    return (np.stack([np.cos(near), np.sin(near)]).astype(np.float32),
+            np.concatenate([outer, swap], axis=0).T.astype(np.float32))
 
 
 def dot(a, b):
@@ -180,9 +179,9 @@
         wdn_t[...] = wdn_ref[...].T
         g1[...] = jnp.broadcast_to(gain_ref[0:1, :], (128, D)).T
         g2[...] = jnp.broadcast_to(gain_ref[1:2, :], (128, D)).T
+        far = far_ref[...].T
         for a in range(length // 128):
-            pos[:, a * 128 : (a + 1) * 128] = (
-                far_ref[:D, a : a + 1] * near_ref[0] + far_ref[D:, a : a + 1] * near_ref[1])
+            pos[:, a * 128 : (a + 1) * 128] = far[:D, a : a + 1] * near_ref[0] + far[D:, a : a + 1] * near_ref[1]
         for slot in slots:
             slot[3][...] = jnp.ones_like(slot[3])
         sums[...] = jnp.zeros_like(sums)
@@ -199,9 +198,8 @@
         run(0, False, True, True)
         run(1, False, False, True)
         if stat_ref is not None:
-            rows = [jnp.sum(sums[k], axis=0, keepdims=True) for k in range(2)]
-            tile = jnp.concatenate(rows + [jnp.zeros((6, 128), F32)], axis=0)
-            stat_ref[...] = jnp.broadcast_to(tile[None], stat_ref.shape)
+            row = jnp.concatenate([jnp.sum(sums[k], axis=0, keepdims=True) for k in range(2)], axis=1)
+            stat_ref[...] = jnp.broadcast_to(row[None], stat_ref.shape)
 
     if stat_ref is None:
         @pl.when(step == last + 1)
@@ -211,6 +209,10 @@
             tile = jnp.concatenate(terms + [jnp.zeros((y_ref.shape[1] - 6, 128), F32)], axis=0)
             tile = jnp.concatenate([tile, jnp.zeros_like(tile)], axis=1).astype(BF16)
             y_ref[...] = jnp.broadcast_to(tile[None], y_ref.shape)
+
+
+def in_hbm(arrays):
+    return [pltpu.with_memory_space_constraint(a, pltpu.HBM) for a in arrays]
 
 
 def layer(x, count, x_block, x_map, pair, length, level, gain, weights, joined, peers, name):
@@ -225,8 +227,8 @@
     if joined is None:
         steps = pairs + 1
         out_specs = [pl.BlockSpec(x_block, lambda i: x_map(jnp.maximum(i - 1, 0))),
-                     pl.BlockSpec((peers, 8, 128), lambda i: (0, 0, 0))]
-        out_shape = [jax.ShapeDtypeStruct(x.shape, BF16), jax.ShapeDtypeStruct((peers, 8, 128), F32)]
+                     pl.BlockSpec((peers, 1, 256), lambda i: (0, 0, 0))]
+        out_shape = [jax.ShapeDtypeStruct(x.shape, BF16), jax.ShapeDtypeStruct((peers, 1, 256), F32)]
     else:
         steps = pairs + 2
         out_specs = pl.BlockSpec((peers, (joined[1] - 8) // pairs, D), lambda i: (0, jnp.maximum(i - 1, 0), 0))
@@ -246,9 +248,9 @@
             pltpu.VMEM((2, 8, 128), F32), *slot, *slot, pltpu.VMEM((D, length), BF16),
             *[pltpu.VMEM((length, CHUNK), F32)] * (LEAD + 1), *[pltpu.VMEM((length, CHUNK), BF16)] * (TRAIL + 1),
         ],
-        compiler_params=pltpu.CompilerParams(dimension_semantics=("arbitrary",)),
+        compiler_params=pltpu.CompilerParams(dimension_semantics=("arbitrary",), vmem_limit_bytes=36 << 20),
         name=name,
-    )(x, jnp.asarray(near), jnp.asarray(far), gain, *weights)
+    )(*(in_hbm if joined is None else tuple)((x, jnp.asarray(near), jnp.asarray(far), gain, *weights)))
 
 
 def split_three(x):
@@ -258,58 +260,103 @@
     return high, mid, (rest - mid.astype(F32)).astype(BF16)
 
 
-class ByFrame:
-    def __init__(self, ref, own, segs):
-        self.ref, self.own, self.segs = ref, own, segs
-
-    def __getitem__(self, i):
-        peer, frame = divmod(i, self.own)
-        return self.ref[peer, frame * self.segs : (frame + 1) * self.segs, :]
-
-
-def blend_kernel(cells, level, stat_ref, out_ref, res_ref, gain_ref, bias_ref, final_ref, *halves):
-    if stat_ref.dtype == BF16:
-        rows = jnp.sum(stat_ref[...].astype(F32), axis=0)
-        sums = [jnp.sum(rows[3 * k : 3 * k + 3, :], axis=(0, 1), keepdims=True) for k in range(2)]
-    else:
-        rows = jnp.sum(stat_ref[...], axis=0)
-        sums = [jnp.sum(rows[k : k + 1, :], axis=(0, 1), keepdims=True) for k in range(2)]
-    center = sums[0] / cells
-    spread = sums[1] / cells - center * center
-    slope = gain_ref[level : level + 1, :] * lax.rsqrt(spread + EPS)
-    one, two, _ = res_ref.shape
-    pitch = two + 8
-    for i in range(one):
-        data = out_ref[i].astype(F32) - center
-        final = slope * data + bias_ref[level : level + 1, :] + res_ref[i].astype(F32)
-        for k, half in enumerate(halves):
-            half[i * pitch : i * pitch + two, :] = final[:, k * 128 : (k + 1) * 128]
-    for j in range(two):
-        for k, half in enumerate(halves):
-            final_ref[j, :, k * 128 : (k + 1) * 128] = half[pl.ds(j, one, stride=pitch), :].astype(BF16)
-
-
-def blend(stat, stat_spec, out, out_spec, out_view, residual, res_block, res_map, gain, bias, level, cells, steps, name):
-    first, second, _ = residual.shape
-    whole = lambda a: pl.BlockSpec(a.shape, lambda i: (0,) * a.ndim)
-
-    def final_map(i):
-        one, two, _ = res_map(i)
-        return two, one, 0
-
-    def kernel(stat_ref, out_ref, *rest):
-        blend_kernel(cells, level, stat_ref, out_view(out_ref), *rest)
+def affine_of(stat, gain, bias, cells):
+    center = stat[0] / cells
+    spread = stat[1] / cells - center * center
+    slope = gain * lax.rsqrt(spread + EPS)
+    return slope, bias - slope * center
+
+
+def in_vmem(*arrays):
+    return [pltpu.with_memory_space_constraint(a, pltpu.VMEM) for a in arrays]
+
+
+VMEM_SPEC = pl.BlockSpec(memory_space=pltpu.VMEM)
+
+
+def blend_intra(stat, intra, mixture, gain, bias, cells):
+    segs, frames, _ = mixture.shape
+    width = 64
+    pitch = width + 8
+
+    def kernel(stat_ref, y_ref, x_ref, gain_ref, bias_ref, out_ref, *parts):
+        row = jnp.sum(stat_ref[...], axis=0)
+        sums = [jnp.sum(row[:, 128 * k : 128 * k + 128], axis=(0, 1), keepdims=True) for k in range(2)]
+        slope, offset = affine_of(sums, gain_ref[0:1, :], bias_ref[0:1, :], cells)
+
+        def chunk(i, _):
+            at = pl.multiple_of(i * width, width)
+            for s in range(segs):
+                mixed = slope * y_ref[s, pl.ds(at, width), :].astype(F32) + offset + x_ref[s, pl.ds(at, width), :].astype(F32)
+                for k, part in enumerate(parts):
+                    part[s * pitch : s * pitch + width, :] = mixed[:, k * 128 : (k + 1) * 128]
+            for f in range(width):
+                for k, part in enumerate(parts):
+                    out_ref[at + f, :, k * 128 : (k + 1) * 128] = part[pl.ds(f, segs, stride=pitch), :].astype(BF16)
+            return 0
+
+        lax.fori_loop(0, frames // width, chunk, 0)
 
     return pl.pallas_call(
         kernel,
-        grid=(steps,),
-        in_specs=[stat_spec, out_spec, pl.BlockSpec(res_block, res_map), whole(gain), whole(bias)],
-        out_specs=pl.BlockSpec((res_block[1], res_block[0], D), final_map),
-        out_shape=jax.ShapeDtypeStruct((second, first, D), BF16),
-        scratch_shapes=[pltpu.VMEM((res_block[0] * (res_block[1] + 8), 128), F32)] * 2,
-        compiler_params=pltpu.CompilerParams(dimension_semantics=("arbitrary",)),
-        name=name,
-    )(stat, out, residual, gain, bias)
+        in_specs=[VMEM_SPEC] * 5,
+        out_specs=VMEM_SPEC,
+        out_shape=jax.ShapeDtypeStruct((frames, segs, D), BF16),
+        scratch_shapes=[pltpu.VMEM((segs * pitch, 128), F32)] * 2,
+        compiler_params=pltpu.CompilerParams(vmem_limit_bytes=8 << 20),
+        name="blend_intra",
+    )(*in_vmem(stat, intra, mixture), gain, bias)
+
+
+def blend_inter(back, across, gain, bias, cells, own):
+    frames, segs, _ = across.shape
+    peers, rows, _ = back.shape
+    width = 64
+    pitch, count, steps = segs + 8, width // own, frames // width
+
+    def kernel(back_ref, res_ref, gain_ref, bias_ref, out_ref, stage, sem, *parts):
+        tile = jnp.sum(back_ref[:, rows - 8 :, :].astype(F32), axis=0)
+        sums = [jnp.sum(tile[3 * k : 3 * k + 3, :], axis=(0, 1), keepdims=True) for k in range(2)]
+        slope, offset = affine_of(sums, gain_ref[1:2, :], bias_ref[1:2, :], cells)
+
+        def copy_out(i):
+            at = pl.multiple_of(i * width, width)
+            return pltpu.make_async_copy(stage.at[i], out_ref.at[:, pl.ds(at, width), :], sem.at[i])
+
+        def chunk(i, _):
+            for f in range(width):
+                p, j = divmod(f, own)
+                data = back_ref[i * count + p, j * segs : (j + 1) * segs, :].astype(F32)
+                mixed = slope * data + offset + res_ref[i * width + f].astype(F32)
+                for k, part in enumerate(parts):
+                    part[f * pitch : f * pitch + segs, :] = mixed[:, k * 128 : (k + 1) * 128]
+            for s in range(segs):
+                for k, part in enumerate(parts):
+                    stage[i, s, :, k * 128 : (k + 1) * 128] = part[pl.ds(s, width, stride=pitch), :].astype(BF16)
+            copy_out(i).start()
+            return 0
+
+        lax.fori_loop(0, steps, chunk, 0)
+        for i in range(steps):
+            copy_out(i).wait()
+
+    return pl.pallas_call(
+        kernel,
+        in_specs=[VMEM_SPEC] * 4,
+        out_specs=pl.BlockSpec(memory_space=pl.ANY),
+        out_shape=jax.ShapeDtypeStruct((segs, frames, D), BF16),
+        scratch_shapes=[pltpu.VMEM((steps, segs, width, D), BF16), pltpu.SemaphoreType.DMA((steps,)),
+                        *[pltpu.VMEM((width * pitch, 128), F32)] * 2],
+        compiler_params=pltpu.CompilerParams(vmem_limit_bytes=12 << 20),
+        name="blend_inter",
+    )(*in_vmem(back, across), gain, bias)
+
+
+def split_three(x):
+    high = x.astype(BF16)
+    rest = x - high.astype(F32)
+    mid = rest.astype(BF16)
+    return high, mid, (rest - mid.astype(F32)).astype(BF16)
 
 
 def body(mixture, w_query, w_key, w_value, w_out, w_up, w_down, ln_gain, gln_gain, gln_bias):
@@ -319,25 +366,18 @@
     total = segs * shards
     cells = float(total * frames * D)
     weights = (w_query, w_key, w_value, w_out, w_up, w_down)
-    steps = 4
 
     intra, stat = layer(mixture, segs, (2, frames, D), lambda i: (i, 0, 0), lambda r, k: r.at[k], frames,
                         0, ln_gain, weights, None, shards, name="intra")
     stat = lax.all_to_all(stat, "span", split_axis=0, concat_axis=0, tiled=True)
-    block = (segs, frames // steps, D)
-    spread = lambda i: (0, i, 0)
-    across = blend(stat, pl.BlockSpec(stat.shape, lambda i: (0, 0, 0)), intra, pl.BlockSpec(block, spread), lambda r: r,
-                   mixture, block, spread, gln_gain, gln_bias, 0, cells, steps, "blend_intra")
+    across = blend_intra(stat, intra, mixture, gln_gain, gln_bias, cells)
     moved = lax.all_to_all(across.reshape(shards, own, segs, D), "span", split_axis=0, concat_axis=0, tiled=True)
 
     rows = own * segs
     inter = layer(moved, own, (shards, 2, segs, D), lambda i: (0, i, 0, 0), lambda r, k: r.at[:, k], total,
                   1, ln_gain, weights, (shards, rows + 8, D), shards, name="inter")
     back = lax.all_to_all(inter, "span", split_axis=0, concat_axis=0, tiled=True)
-    peers = shards // steps
-    return blend(back, pl.BlockSpec((shards, 8, D), lambda i: (0, rows // 8, 0)),
-                 back, pl.BlockSpec((peers, rows, D), lambda i: (i, 0, 0)), lambda r: ByFrame(r, own, segs),
-                 across, (frames // steps, segs, D), lambda i: (i, 0, 0), gln_gain, gln_bias, 1, cells, steps, "blend_inter")
+    return blend_inter(back, across, gln_gain, gln_bias, cells, own)
 
 
 def solution(mesh):

time: 149 us -> 137 us (0.919)
  Pallas kernels: 63.8 us -> 54.9 us
  blocking collectives: 84.2 us -> 81.4 us
    pallas_call x2, Pallas kernels: 10.5 us -> 4.13 us  [the longest x1 2.48 us: blend_inter(): pl.pallas_call(kernel, in_specs=[VMEM_SPEC] * 4, out_specs=pl.BlockSpec(m...]
    pallas_call x2, Pallas kernels: 53.3 us -> 50.8 us  [layer(): pl.pallas_call(functools.partial(layer_kernel, pair, pairs, joined is not...]
where the time goes in v6:
time: 137 us
  blocking collectives  81.4 us (59%)
  Pallas kernels  54.9 us (40%)
    pallas_call x2, Pallas kernels, layer(): pl.pallas_call(functools.partial(layer_kernel, pair, pairs, joined is not...  50.8 us
    all_to_all x1, blocking collectives, body(): lax.all_to_all(inter, 'span', split_axis=0, concat_axis=0, tiled=True)  33.9 us
    all_to_all x1, blocking collectives, body(): lax.all_to_all(across.reshape(shards, own, segs, D), 'span', split_axis=0...  31.9 us
    all_to_all x1, blocking collectives, body(): stat = lax.all_to_all(stat, 'span', split_axis=0, concat_axis=0, tiled=True)  15.7 us

profile of v6, /device:TPU:1, one launch (start us, length us, event | category | flops | bytes accessed | tf_op | source)
XLA Modules:
  0.0 136.7 jit_solution(1018608183360728903)
XLA Ops:
  0.0 0.0 copy-start
  0.0 0.0 copy-start.11
  0.0 0.0 copy-start.10
  0.0 23.0 %intra.1 = (bf16[16,256,256]{2,1,0:T(8,128)(2,1)S(1)}, f32[32,1,256]{2,1,0:T(1,128)S(1)}) custom-call(bf16[16,256,256]{2,1,0:T(8,128)(2,1)} %x_ref.3, f32[2,256,128]{2,1,0:T(8,128)} %constant.4.clone.near_ref, f32[8,512]{1,0:T(8,128)} %constant.5.clone.far_ref, f32[2,2,256]{2,1,0:T(2,128)} %gain_ref.6, bf16[2,256,256]{2,1,0:T(8,128)(2,1)} %wq_ref.3, ...), custom_call_target="tpu_custom_call" | custom-call | tf_op jit(solution)/shard_map/intra/pallas_call | solution.py:236
  23.0 15.7 %all_to_all.15.stat_ref = f32[32,1,256]{2,1,0:T(1,128)S(1)} all-to-all(f32[32,1,256]{2,1,0:T(1,128)S(1)} %get-tuple-element.7), channel_id=1, replica_groups=mesh['mix'=4,'span'=32] {'span'}, dimensions={0} | all-to-all | bytes 65536 | tf_op jit(solution)/shard_map/all_to_all | solution.py:372
  38.6 0.0 copy-done
  38.6 0.0 copy-done.11
  38.6 0.0 copy-done.10
  38.6 1.6 %blend_intra.1.res_ref = bf16[256,16,256]{2,1,0:T(8,128)(2,1)S(1)} custom-call(f32[32,1,256]{2,1,0:T(1,128)S(1)} %all_to_all.15.stat_ref, bf16[16,256,256]{2,1,0:T(8,128)(2,1)S(1)} %get-tuple-element.8.y_ref, bf16[16,256,256]{2,1,0:T(8,128)(2,1)S(1)} %copy-done, f32[2,256]{1,0:T(2,128)S(1)} %copy-done.10, f32[2,256]{1,0:T(2,128)S(1)} %copy-done.11), custom_call_target="tpu_custom_call" | custom-call | tf_op jit(solution)/shard_map/blend_intra/pallas_call | solution.py:300
  40.3 0.0 copy-start.1
  40.3 0.0 copy-start.2
  40.3 0.0 copy-start.3
  40.3 0.0 copy-start.4
  40.3 0.0 copy-start.5
  40.4 0.0 copy-start.6
  40.4 0.0 copy-start.7
  40.4 0.0 copy-start.8
  40.4 0.0 copy-start.9
  40.4 31.9 %all_to_all.16.x_ref = bf16[32,8,16,256]{3,2,1,0:T(8,128)(2,1)S(1)} all-to-all(bf16[32,8,16,256]{3,2,1,0:T(8,128)(2,1)S(1)} %bitcast.1), channel_id=1, replica_groups=mesh['mix'=4,'span'=32] {'span'}, dimensions={0} | all-to-all | bytes 4194304 | tf_op jit(solution)/shard_map/all_to_all | solution.py:374
  72.3 0.0 copy-done.1
  72.3 0.0 copy-done.2
  72.3 0.0 copy-done.3
  72.3 0.0 copy-done.4
  72.3 0.0 copy-done.5
  72.3 0.0 copy-done.6
  72.3 0.0 copy-done.7
  72.3 0.0 copy-done.8
  72.3 0.0 copy-done.9
  72.3 27.8 %inter.1 = bf16[32,136,256]{2,1,0:T(8,128)(2,1)S(1)} custom-call(bf16[32,8,16,256]{3,2,1,0:T(8,128)(2,1)S(1)} %all_to_all.16.x_ref, f32[2,256,128]{2,1,0:T(8,128)S(1)} %copy-done.7, f32[8,512]{1,0:T(8,128)S(1)} %copy-done.8, f32[2,2,256]{2,1,0:T(2,128)S(1)} %copy-done.9, bf16[2,256,256]{2,1,0:T(8,128)(2,1)S(1)} %copy-done.3, ...), custom_call_target="tpu_custom_call" | custom-call | tf_op jit(solution)/shard_map/inter/pallas_call | solution.py:236
  100.2 33.9 %all_to_all.17.back_ref = bf16[32,136,256]{2,1,0:T(8,128)(2,1)S(1)} all-to-all(bf16[32,136,256]{2,1,0:T(8,128)(2,1)S(1)} %inter.1), channel_id=1, replica_groups=mesh['mix'=4,'span'=32] {'span'}, dimensions={0} | all-to-all | bytes 4456448 | tf_op jit(solution)/shard_map/all_to_all | solution.py:379
  134.1 2.5 %blend_inter.1 = bf16[16,256,256]{2,1,0:T(8,128)(2,1)} custom-call(bf16[32,136,256]{2,1,0:T(8,128)(2,1)S(1)} %all_to_all.17.back_ref, bf16[256,16,256]{2,1,0:T(8,128)(2,1)S(1)} %blend_intra.1.res_ref, f32[2,256]{1,0:T(2,128)S(1)} %copy-done.10, f32[2,256]{1,0:T(2,128)S(1)} %copy-done.11), custom_call_target="tpu_custom_call" | custom-call | tf_op jit(solution)/shard_map/blend_inter/pallas_call | solution.py:343
Async XLA Ops:
  0.0 38.6 %copy-start = (bf16[16,256,256]{2,1,0:T(8,128)(2,1)S(1)}, bf16[16,256,256]{2,1,0:T(8,128)(2,1)}, u32[]{:S(2)}) copy-start(bf16[16,256,256]{2,1,0:T(8,128)(2,1)} %x_ref.3) | copy-start | bytes 6291460
  0.0 38.6 %copy-start.11 = (f32[2,256]{1,0:T(2,128)S(1)}, f32[2,256]{1,0:T(2,128)}, u32[]{:S(2)}) copy-start(f32[2,256]{1,0:T(2,128)} %bias_ref.3) | copy-start | bytes 6148
  0.0 38.6 %copy-start.10 = (f32[2,256]{1,0:T(2,128)S(1)}, f32[2,256]{1,0:T(2,128)}, u32[]{:S(2)}) copy-start(f32[2,256]{1,0:T(2,128)} %gain_ref.7) | copy-start | bytes 6148
  40.3 32.0 %copy-start.1 = (bf16[2,256,1024]{2,1,0:T(8,128)(2,1)S(1)}, bf16[2,256,1024]{2,1,0:T(8,128)(2,1)}, u32[]{:S(2)}) copy-start(bf16[2,256,1024]{2,1,0:T(8,128)(2,1)} %wup_ref.3) | copy-start | bytes 3145732
  40.3 32.0 %copy-start.2 = (bf16[2,1024,256]{2,1,0:T(8,128)(2,1)S(1)}, bf16[2,1024,256]{2,1,0:T(8,128)(2,1)}, u32[]{:S(2)}) copy-start(bf16[2,1024,256]{2,1,0:T(8,128)(2,1)} %wdn_ref.3) | copy-start | bytes 3145732
  40.3 32.0 %copy-start.3 = (bf16[2,256,256]{2,1,0:T(8,128)(2,1)S(1)}, bf16[2,256,256]{2,1,0:T(8,128)(2,1)}, u32[]{:S(2)}) copy-start(bf16[2,256,256]{2,1,0:T(8,128)(2,1)} %wq_ref.3) | copy-start | bytes 786436
  40.3 32.0 %copy-start.4 = (bf16[2,256,256]{2,1,0:T(8,128)(2,1)S(1)}, bf16[2,256,256]{2,1,0:T(8,128)(2,1)}, u32[]{:S(2)}) copy-start(bf16[2,256,256]{2,1,0:T(8,128)(2,1)} %wk_ref.3) | copy-start | bytes 786436
  40.3 32.0 %copy-start.5 = (bf16[2,256,256]{2,1,0:T(8,128)(2,1)S(1)}, bf16[2,256,256]{2,1,0:T(8,128)(2,1)}, u32[]{:S(2)}) copy-start(bf16[2,256,256]{2,1,0:T(8,128)(2,1)} %wv_ref.3) | copy-start | bytes 786436
  40.4 32.0 %copy-start.6 = (bf16[2,256,256]{2,1,0:T(8,128)(2,1)S(1)}, bf16[2,256,256]{2,1,0:T(8,128)(2,1)}, u32[]{:S(2)}) copy-start(bf16[2,256,256]{2,1,0:T(8,128)(2,1)} %wo_ref.3) | copy-start | bytes 786436
  40.4 32.0 %copy-start.7 = (f32[2,256,128]{2,1,0:T(8,128)S(1)}, f32[2,256,128]{2,1,0:T(8,128)}, u32[]{:S(2)}) copy-start(f32[2,256,128]{2,1,0:T(8,128)} %constant.4.clone.near_ref) | copy-start | bytes 786436
  40.4 32.0 %copy-start.8 = (f32[8,512]{1,0:T(8,128)S(1)}, f32[8,512]{1,0:T(8,128)}, u32[]{:S(2)}) copy-start(f32[8,512]{1,0:T(8,128)} %constant.5.clone.far_ref) | copy-start | bytes 49156
  40.4 32.0 %copy-start.9 = (f32[2,2,256]{2,1,0:T(2,128)S(1)}, f32[2,2,256]{2,1,0:T(2,128)}, u32[]{:S(2)}) copy-start(f32[2,2,256]{2,1,0:T(2,128)} %gain_ref.6) | copy-start | bytes 12292

commit v7 on v6

--- a/solution.py
+++ b/solution.py
@@ -113,7 +113,7 @@
     return [first, get_keys, get_queries, get_values]
 
 
-def pieces_c(after, g2, wup_t, wdn_t, y_ref, sums, n2, hidden):
+def pieces_c(after, g2, wup_t, wdn_t, emit, sums, n2, hidden):
     def first():
         n2[...] = norm_cols(after[...], g2).astype(BF16)
 
@@ -128,42 +128,25 @@
             lanes = slice(k * 128, (k + 1) * 128)
             sums[0] += jnp.sum(part[:, :, lanes], axis=0)
             sums[1] += jnp.sum(part[:, :, lanes] * part[:, :, lanes], axis=0)
-        y_ref[...] = y_t.astype(BF16).T.reshape(y_ref.shape)
+        emit(y_t.astype(BF16).T)
 
     return [first] + [functools.partial(up, j) for j in range(FF // D)] + [down]
 
 
-def layer_kernel(pair, pairs, joined, x_ref, near_ref, far_ref, gain_ref, wq_ref, wk_ref, wv_ref, wo_ref, wup_ref, wdn_ref,
-                 y_ref, *refs):
-    if joined:
-        stat_ref = None
-    else:
-        stat_ref, refs = refs[0], refs[1:]
-    layer_steps(pair, pairs, x_ref, near_ref, far_ref, gain_ref, wq_ref, wk_ref, wv_ref, wo_ref, wup_ref, wdn_ref,
-                y_ref, stat_ref, *refs)
-
-
-def layer_steps(pair, pairs, x_ref, near_ref, far_ref, gain_ref, wq_ref, wk_ref, wv_ref, wo_ref, wup_ref, wdn_ref,
-                y_ref, stat_ref, wq_t, wv_t, wo_t, wup_t, wdn_t, pos, g1, g2, n1, n2, hidden, sums, *bufs):
+def layer_steps(pairs, get, emit, finish, near_ref, far_ref, gain_ref, wq_ref, wk_ref, wv_ref, wo_ref, wup_ref, wdn_ref,
+                wq_t, wv_t, wo_t, wup_t, wdn_t, pos, g1, g2, n1, n2, hidden, sums, *bufs):
     length = pos.shape[1]
     slots = (bufs[0:5], bufs[5:10])
     ctx, scores, weights = bufs[10], bufs[11 : 12 + LEAD], bufs[12 + LEAD :]
     step, last = pl.program_id(0), pairs
 
-    def out_part(sub):
-        if stat_ref is not None:
-            return pair(y_ref, sub)
-        half = y_ref.shape[1] // 2
-        return y_ref.at[:, sub * half : (sub + 1) * half]
-
     def run(sub, a, b, c):
         here, other = slots[sub], slots[1 - sub]
         left, right = [], []
         if c:
-            left = pieces_c(here[4], g2[:, :1], wup_t, wdn_t, out_part(sub), sums, n2, hidden)
+            left = pieces_c(here[4], g2[:, :1], wup_t, wdn_t, functools.partial(emit, sub), sums, n2, hidden)
         if a:
-            get = lambda: pair(x_ref, sub)[...].reshape(length, D)
-            right = pieces_a(get, pos, g1[:, :1], wq_t, wv_t, wk_ref, *here[:4], n1)
+            right = pieces_a(functools.partial(get, sub), pos, g1[:, :1], wq_t, wv_t, wk_ref, *here[:4], n1)
         fills = []
         while left or right:
             fills += left[:1] + right[:1]
@@ -197,60 +180,25 @@
     def _():
         run(0, False, True, True)
         run(1, False, False, True)
-        if stat_ref is not None:
-            row = jnp.concatenate([jnp.sum(sums[k], axis=0, keepdims=True) for k in range(2)], axis=1)
-            stat_ref[...] = jnp.broadcast_to(row[None], stat_ref.shape)
-
-    if stat_ref is None:
-        @pl.when(step == last + 1)
-        def _():
-            rows = [jnp.sum(sums[k], axis=0, keepdims=True) for k in range(2)]
-            terms = [t.astype(F32) for r in rows for t in split_three(r)]
-            tile = jnp.concatenate(terms + [jnp.zeros((y_ref.shape[1] - 6, 128), F32)], axis=0)
-            tile = jnp.concatenate([tile, jnp.zeros_like(tile)], axis=1).astype(BF16)
-            y_ref[...] = jnp.broadcast_to(tile[None], y_ref.shape)
+        finish()
+
+
+def affine_of(stat, gain, bias, cells):
+    center = stat[0] / cells
+    spread = stat[1] / cells - center * center
+    slope = gain * lax.rsqrt(spread + EPS)
+    return slope, bias - slope * center
+
+
+def in_vmem(*arrays):
+    return [pltpu.with_memory_space_constraint(a, pltpu.VMEM) for a in arrays]
+
+
+VMEM_SPEC = pl.BlockSpec(memory_space=pltpu.VMEM)
 
 
 def in_hbm(arrays):
     return [pltpu.with_memory_space_constraint(a, pltpu.HBM) for a in arrays]
-
-
-def layer(x, count, x_block, x_map, pair, length, level, gain, weights, joined, peers, name):
-    near, far = pos_parts(length)
-    pick = lambda a: pl.BlockSpec((None, *a.shape[1:]), lambda i: (level,) + (0,) * (a.ndim - 1))
-    whole = lambda a: pl.BlockSpec(a.shape, lambda i: (0,) * a.ndim)
-    pairs = count // 2
-    slot = [
-        pltpu.VMEM((D, length), F32), pltpu.VMEM((D, length), BF16), pltpu.VMEM((length, D), BF16),
-        pltpu.VMEM((HEADS * AUG, length), BF16), pltpu.VMEM((D, length), F32),
-    ]
-    if joined is None:
-        steps = pairs + 1
-        out_specs = [pl.BlockSpec(x_block, lambda i: x_map(jnp.maximum(i - 1, 0))),
-                     pl.BlockSpec((peers, 1, 256), lambda i: (0, 0, 0))]
-        out_shape = [jax.ShapeDtypeStruct(x.shape, BF16), jax.ShapeDtypeStruct((peers, 1, 256), F32)]
-    else:
-        steps = pairs + 2
-        out_specs = pl.BlockSpec((peers, (joined[1] - 8) // pairs, D), lambda i: (0, jnp.maximum(i - 1, 0), 0))
-        out_shape = jax.ShapeDtypeStruct(joined, BF16)
-    return pl.pallas_call(
-        functools.partial(layer_kernel, pair, pairs, joined is not None),
-        grid=(steps,),
-        in_specs=[pl.BlockSpec(x_block, lambda i: x_map(jnp.minimum(i, pairs - 1))),
-                  whole(near), whole(far), pick(gain)] + [pick(w) for w in weights],
-        out_specs=out_specs,
-        out_shape=out_shape,
-        scratch_shapes=[
-            pltpu.VMEM((D, D), BF16), pltpu.VMEM((D, D), BF16), pltpu.VMEM((D, D), BF16),
-            pltpu.VMEM((FF, D), BF16), pltpu.VMEM((D, FF), BF16),
-            pltpu.VMEM((D, length), F32), pltpu.VMEM((D, 128), F32), pltpu.VMEM((D, 128), F32),
-            pltpu.VMEM((D, length), BF16), pltpu.VMEM((D, length), BF16), pltpu.VMEM((FF, length), BF16),
-            pltpu.VMEM((2, 8, 128), F32), *slot, *slot, pltpu.VMEM((D, length), BF16),
-            *[pltpu.VMEM((length, CHUNK), F32)] * (LEAD + 1), *[pltpu.VMEM((length, CHUNK), BF16)] * (TRAIL + 1),
-        ],
-        compiler_params=pltpu.CompilerParams(dimension_semantics=("arbitrary",), vmem_limit_bytes=36 << 20),
-        name=name,
-    )(*(in_hbm if joined is None else tuple)((x, jnp.asarray(near), jnp.asarray(far), gain, *weights)))
 
 
 def split_three(x):
@@ -260,18 +208,93 @@
     return high, mid, (rest - mid.astype(F32)).astype(BF16)
 
 
-def affine_of(stat, gain, bias, cells):
-    center = stat[0] / cells
-    spread = stat[1] / cells - center * center
-    slope = gain * lax.rsqrt(spread + EPS)
-    return slope, bias - slope * center
-
-
-def in_vmem(*arrays):
-    return [pltpu.with_memory_space_constraint(a, pltpu.VMEM) for a in arrays]
-
-
-VMEM_SPEC = pl.BlockSpec(memory_space=pltpu.VMEM)
+def stat_rows(sums, count):
+    terms = [t.astype(F32) for k in range(2) for t in split_three(jnp.sum(sums[k], axis=0, keepdims=True))]
+    tile = jnp.concatenate(terms + [jnp.zeros((count - 6, 128), F32)], axis=0)
+    return jnp.concatenate([tile, jnp.zeros_like(tile)], axis=1).astype(BF16)
+
+
+def layer_scratch(length):
+    slot = [
+        pltpu.VMEM((D, length), F32), pltpu.VMEM((D, length), BF16), pltpu.VMEM((length, D), BF16),
+        pltpu.VMEM((HEADS * AUG, length), BF16), pltpu.VMEM((D, length), F32),
+    ]
+    return [
+        pltpu.VMEM((D, D), BF16), pltpu.VMEM((D, D), BF16), pltpu.VMEM((D, D), BF16),
+        pltpu.VMEM((FF, D), BF16), pltpu.VMEM((D, FF), BF16),
+        pltpu.VMEM((D, length), F32), pltpu.VMEM((D, 128), F32), pltpu.VMEM((D, 128), F32),
+        pltpu.VMEM((D, length), BF16), pltpu.VMEM((D, length), BF16), pltpu.VMEM((FF, length), BF16),
+        pltpu.VMEM((2, 8, 128), F32), *slot, *slot, pltpu.VMEM((D, length), BF16),
+        *[pltpu.VMEM((length, CHUNK), F32)] * (LEAD + 1), *[pltpu.VMEM((length, CHUNK), BF16)] * (TRAIL + 1),
+    ]
+
+
+LAYER_PARAMS = pltpu.CompilerParams(dimension_semantics=("arbitrary",), vmem_limit_bytes=36 << 20)
+
+
+def intra_layer(mixture, gain, weights, peers):
+    segs, frames, _ = mixture.shape
+    pairs = segs // 2
+    near, far = pos_parts(frames)
+    pick = lambda a: pl.BlockSpec((None, *a.shape[1:]), lambda i: (0,) * a.ndim)
+    whole = lambda a: pl.BlockSpec(a.shape, lambda i: (0,) * a.ndim)
+
+    def kernel(x_ref, *refs):
+        consts, (y_ref, stat_ref), work = refs[:9], refs[9:11], refs[11:]
+
+        def emit(sub, y):
+            y_ref[pl.program_id(0) * 2 - 2 + sub] = y
+
+        def finish():
+            row = jnp.concatenate([jnp.sum(work[11][k], axis=0, keepdims=True) for k in range(2)], axis=1)
+            stat_ref[...] = jnp.broadcast_to(row[None], stat_ref.shape)
+
+        layer_steps(pairs, lambda sub: x_ref[sub], emit, finish, *consts, *work)
+
+    return pl.pallas_call(
+        kernel,
+        grid=(pairs + 1,),
+        in_specs=[pl.BlockSpec((2, frames, D), lambda i: (jnp.minimum(i, pairs - 1), 0, 0)),
+                  whole(near), whole(far), pick(gain)] + [pick(w) for w in weights],
+        out_specs=[VMEM_SPEC, VMEM_SPEC],
+        out_shape=[jax.ShapeDtypeStruct(mixture.shape, BF16), jax.ShapeDtypeStruct((peers, 1, 256), F32)],
+        scratch_shapes=layer_scratch(frames),
+        compiler_params=LAYER_PARAMS,
+        name="intra",
+    )(*in_hbm((mixture, jnp.asarray(near), jnp.asarray(far), gain, *weights)))
+
+
+def inter_layer(moved, gain, weights):
+    peers, own, segs, _ = moved.shape
+    total, pairs, rows = peers * segs, own // 2, own * segs
+    near, far = pos_parts(total)
+
+    def kernel(x_ref, near_ref, far_ref, gain_ref, *refs):
+        weights_refs, y_ref, work = [r.at[1] for r in refs[:6]], refs[6], refs[7:]
+        step = pl.program_id(0)
+
+        def get(sub):
+            return x_ref[:, step * 2 + sub].reshape(total, D)
+
+        def emit(sub, y):
+            at = pl.multiple_of((step * 2 - 2 + sub) * segs, segs)
+            y_ref[:, pl.ds(at, segs), :] = y.reshape(peers, segs, D)
+
+        def finish():
+            y_ref[:, rows:, :] = jnp.broadcast_to(stat_rows(work[11], 8)[None], (peers, 8, D))
+
+        layer_steps(pairs, get, emit, finish, near_ref, far_ref, gain_ref.at[1], *weights_refs, *work)
+
+    return pl.pallas_call(
+        kernel,
+        grid=(pairs + 1,),
+        in_specs=[VMEM_SPEC] * 10,
+        out_specs=VMEM_SPEC,
+        out_shape=jax.ShapeDtypeStruct((peers, rows + 8, D), BF16),
+        scratch_shapes=layer_scratch(total),
+        compiler_params=LAYER_PARAMS,
+        name="inter",
+    )(*in_vmem(moved, jnp.asarray(near), jnp.asarray(far), gain, *weights))
 
 
 def blend_intra(stat, intra, mixture, gain, bias, cells):
@@ -352,13 +375,6 @@
     )(*in_vmem(back, across), gain, bias)
 
 
-def split_three(x):
-    high = x.astype(BF16)
-    rest = x - high.astype(F32)
-    mid = rest.astype(BF16)
-    return high, mid, (rest - mid.astype(F32)).astype(BF16)
-
-
 def body(mixture, w_query, w_key, w_value, w_out, w_up, w_down, ln_gain, gln_gain, gln_bias):
     shards = lax.axis_size("span")
     segs, frames, _ = mixture.shape
@@ -367,15 +383,12 @@
     cells = float(total * frames * D)
     weights = (w_query, w_key, w_value, w_out, w_up, w_down)
 
-    intra, stat = layer(mixture, segs, (2, frames, D), lambda i: (i, 0, 0), lambda r, k: r.at[k], frames,
-                        0, ln_gain, weights, None, shards, name="intra")
+    intra, stat = intra_layer(mixture, ln_gain, weights, shards)
     stat = lax.all_to_all(stat, "span", split_axis=0, concat_axis=0, tiled=True)
     across = blend_intra(stat, intra, mixture, gln_gain, gln_bias, cells)
     moved = lax.all_to_all(across.reshape(shards, own, segs, D), "span", split_axis=0, concat_axis=0, tiled=True)
 
-    rows = own * segs
-    inter = layer(moved, own, (shards, 2, segs, D), lambda i: (0, i, 0, 0), lambda r, k: r.at[:, k], total,
-                  1, ln_gain, weights, (shards, rows + 8, D), shards, name="inter")
+    inter = inter_layer(moved, ln_gain, weights)
     back = lax.all_to_all(inter, "span", split_axis=0, concat_axis=0, tiled=True)
     return blend_inter(back, across, gln_gain, gln_bias, cells, own)
 

time: 137 us -> 136 us (level)
  no operation moved by 1% of the time
where the time goes in v7:
time: 136 us
  blocking collectives  81.4 us (60%)
  Pallas kernels  54.4 us (40%)
    all_to_all x1, blocking collectives, body(): lax.all_to_all(inter, 'span', split_axis=0, concat_axis=0, tiled=True)  33.9 us
    all_to_all x1, blocking collectives, body(): lax.all_to_all(across.reshape(shards, own, segs, D), 'span', split_axis=0...  31.9 us
    pallas_call x1, Pallas kernels, inter_layer(): pl.pallas_call(kernel, grid=(pairs + 1,), in_specs=[VMEM_SPEC] * 10, out_...  27.3 us
    pallas_call x1, Pallas kernels, intra_layer(): pl.pallas_call(kernel, grid=(pairs + 1,), in_specs=[pl.BlockSpec((2, fram...  22.9 us
    all_to_all x1, blocking collectives, body(): stat = lax.all_to_all(stat, 'span', split_axis=0, concat_axis=0, tiled=True)  15.7 us

profile of v7, /device:TPU:1, one launch (start us, length us, event | category | flops | bytes accessed | tf_op | source)
XLA Modules:
  0.0 136.2 jit_solution(16716247127582739987)
XLA Ops:
  0.0 0.0 copy-start
  0.0 0.0 copy-start.11
  0.0 0.0 copy-start.10
  0.0 22.9 %intra.1 = (bf16[16,256,256]{2,1,0:T(8,128)(2,1)S(1)}, f32[32,1,256]{2,1,0:T(1,128)S(1)}) custom-call(bf16[16,256,256]{2,1,0:T(8,128)(2,1)} %x_ref.3, f32[2,256,128]{2,1,0:T(8,128)} %constant.4.clone.refs_0_.near_ref, f32[8,512]{1,0:T(8,128)} %constant.5.clone.refs_1_.far_ref, f32[2,2,256]{2,1,0:T(2,128)} %gain_ref.4, bf16[2,256,256]{2,1,0:T(8,128)(2,1)} %refs_0_.2, ...), custom_call_target="tpu_custom_call" | custom-call | tf_op jit(solution)/shard_map/intra/pallas_call | solution.py:254
  23.0 15.7 %all_to_all.15.stat_ref = f32[32,1,256]{2,1,0:T(1,128)S(1)} all-to-all(f32[32,1,256]{2,1,0:T(1,128)S(1)} %get-tuple-element.7), channel_id=1, replica_groups=mesh['mix'=4,'span'=32] {'span'}, dimensions={0} | all-to-all | bytes 65536 | tf_op jit(solution)/shard_map/all_to_all | solution.py:387
  38.6 0.0 copy-done
  38.6 0.0 copy-done.11
  38.6 0.0 copy-done.10
  38.6 1.6 %blend_intra.1.res_ref = bf16[256,16,256]{2,1,0:T(8,128)(2,1)S(1)} custom-call(f32[32,1,256]{2,1,0:T(1,128)S(1)} %all_to_all.15.stat_ref, bf16[16,256,256]{2,1,0:T(8,128)(2,1)S(1)} %get-tuple-element.8.y_ref, bf16[16,256,256]{2,1,0:T(8,128)(2,1)S(1)} %copy-done, f32[2,256]{1,0:T(2,128)S(1)} %copy-done.10, f32[2,256]{1,0:T(2,128)S(1)} %copy-done.11), custom_call_target="tpu_custom_call" | custom-call | tf_op jit(solution)/shard_map/blend_intra/pallas_call | solution.py:323
  40.3 0.0 copy-start.1
  40.3 0.0 copy-start.2
  40.3 0.0 copy-start.3
  40.3 0.0 copy-start.4
  40.3 0.0 copy-start.5
  40.3 0.0 copy-start.6
  40.4 0.0 copy-start.7
  40.4 0.0 copy-start.8
  40.4 0.0 copy-start.9
  40.4 31.9 %all_to_all.16.x_ref = bf16[32,8,16,256]{3,2,1,0:T(8,128)(2,1)S(1)} all-to-all(bf16[32,8,16,256]{3,2,1,0:T(8,128)(2,1)S(1)} %bitcast.1), channel_id=1, replica_groups=mesh['mix'=4,'span'=32] {'span'}, dimensions={0} | all-to-all | bytes 4194304 | tf_op jit(solution)/shard_map/all_to_all | solution.py:389
  72.3 0.0 copy-done.1
  72.3 0.0 copy-done.2
  72.3 0.0 copy-done.3
  72.3 0.0 copy-done.4
  72.3 0.0 copy-done.5
  72.3 0.0 copy-done.6
  72.3 0.0 copy-done.7
  72.3 0.0 copy-done.8
  72.3 0.0 copy-done.9
  72.3 27.3 %inter.1 = bf16[32,136,256]{2,1,0:T(8,128)(2,1)S(1)} custom-call(bf16[32,8,16,256]{3,2,1,0:T(8,128)(2,1)S(1)} %all_to_all.16.x_ref, f32[2,256,128]{2,1,0:T(8,128)S(1)} %copy-done.7, f32[8,512]{1,0:T(8,128)S(1)} %copy-done.8, f32[2,2,256]{2,1,0:T(2,128)S(1)} %copy-done.9, bf16[2,256,256]{2,1,0:T(8,128)(2,1)S(1)} %copy-done.3, ...), custom_call_target="tpu_custom_call" | custom-call | tf_op jit(solution)/shard_map/inter/pallas_call | solution.py:288
  99.7 33.9 %all_to_all.17.back_ref = bf16[32,136,256]{2,1,0:T(8,128)(2,1)S(1)} all-to-all(bf16[32,136,256]{2,1,0:T(8,128)(2,1)S(1)} %inter.1), channel_id=1, replica_groups=mesh['mix'=4,'span'=32] {'span'}, dimensions={0} | all-to-all | bytes 4456448 | tf_op jit(solution)/shard_map/all_to_all | solution.py:392
  133.5 2.5 %blend_inter.1 = bf16[16,256,256]{2,1,0:T(8,128)(2,1)} custom-call(bf16[32,136,256]{2,1,0:T(8,128)(2,1)S(1)} %all_to_all.17.back_ref, bf16[256,16,256]{2,1,0:T(8,128)(2,1)S(1)} %blend_intra.1.res_ref, f32[2,256]{1,0:T(2,128)S(1)} %copy-done.10, f32[2,256]{1,0:T(2,128)S(1)} %copy-done.11), custom_call_target="tpu_custom_call" | custom-call | tf_op jit(solution)/shard_map/blend_inter/pallas_call | solution.py:366
Async XLA Ops:
  0.0 38.6 %copy-start = (bf16[16,256,256]{2,1,0:T(8,128)(2,1)S(1)}, bf16[16,256,256]{2,1,0:T(8,128)(2,1)}, u32[]{:S(2)}) copy-start(bf16[16,256,256]{2,1,0:T(8,128)(2,1)} %x_ref.3) | copy-start | bytes 6291460
  0.0 38.6 %copy-start.11 = (f32[2,256]{1,0:T(2,128)S(1)}, f32[2,256]{1,0:T(2,128)}, u32[]{:S(2)}) copy-start(f32[2,256]{1,0:T(2,128)} %bias_ref.3) | copy-start | bytes 6148
  0.0 38.6 %copy-start.10 = (f32[2,256]{1,0:T(2,128)S(1)}, f32[2,256]{1,0:T(2,128)}, u32[]{:S(2)}) copy-start(f32[2,256]{1,0:T(2,128)} %gain_ref.5) | copy-start | bytes 6148
  40.3 32.0 %copy-start.1 = (bf16[2,256,1024]{2,1,0:T(8,128)(2,1)S(1)}, bf16[2,256,1024]{2,1,0:T(8,128)(2,1)}, u32[]{:S(2)}) copy-start(bf16[2,256,1024]{2,1,0:T(8,128)(2,1)} %refs_4_.3) | copy-start | bytes 3145732
  40.3 32.0 %copy-start.2 = (bf16[2,1024,256]{2,1,0:T(8,128)(2,1)S(1)}, bf16[2,1024,256]{2,1,0:T(8,128)(2,1)}, u32[]{:S(2)}) copy-start(bf16[2,1024,256]{2,1,0:T(8,128)(2,1)} %refs_5_.3) | copy-start | bytes 3145732
  40.3 32.0 %copy-start.3 = (bf16[2,256,256]{2,1,0:T(8,128)(2,1)S(1)}, bf16[2,256,256]{2,1,0:T(8,128)(2,1)}, u32[]{:S(2)}) copy-start(bf16[2,256,256]{2,1,0:T(8,128)(2,1)} %refs_0_.2) | copy-start | bytes 786436
  40.3 32.0 %copy-start.4 = (bf16[2,256,256]{2,1,0:T(8,128)(2,1)S(1)}, bf16[2,256,256]{2,1,0:T(8,128)(2,1)}, u32[]{:S(2)}) copy-start(bf16[2,256,256]{2,1,0:T(8,128)(2,1)} %refs_1_.2) | copy-start | bytes 786436
  40.3 32.0 %copy-start.5 = (bf16[2,256,256]{2,1,0:T(8,128)(2,1)S(1)}, bf16[2,256,256]{2,1,0:T(8,128)(2,1)}, u32[]{:S(2)}) copy-start(bf16[2,256,256]{2,1,0:T(8,128)(2,1)} %refs_2_.3) | copy-start | bytes 786436
  40.3 32.0 %copy-start.6 = (bf16[2,256,256]{2,1,0:T(8,128)(2,1)S(1)}, bf16[2,256,256]{2,1,0:T(8,128)(2,1)}, u32[]{:S(2)}) copy-start(bf16[2,256,256]{2,1,0:T(8,128)(2,1)} %refs_3_.3) | copy-start | bytes 786436
  40.4 32.0 %copy-start.7 = (f32[2,256,128]{2,1,0:T(8,128)S(1)}, f32[2,256,128]{2,1,0:T(8,128)}, u32[]{:S(2)}) copy-start(f32[2,256,128]{2,1,0:T(8,128)} %constant.4.clone.refs_0_.near_ref) | copy-start | bytes 786436
  40.4 32.0 %copy-start.8 = (f32[8,512]{1,0:T(8,128)S(1)}, f32[8,512]{1,0:T(8,128)}, u32[]{:S(2)}) copy-start(f32[8,512]{1,0:T(8,128)} %constant.5.clone.refs_1_.far_ref) | copy-start | bytes 49156
  40.4 32.0 %copy-start.9 = (f32[2,2,256]{2,1,0:T(2,128)S(1)}, f32[2,2,256]{2,1,0:T(2,128)}, u32[]{:S(2)}) copy-start(f32[2,2,256]{2,1,0:T(2,128)} %gain_ref.4) | copy-start | bytes 12292

commit v8 on v7

--- a/solution.py
+++ b/solution.py
@@ -42,9 +42,9 @@
     return shifted * lax.rsqrt(spread + EPS) * gain
 
 
+INTRA_AHEAD = (4, 2)
+INTER_AHEAD = (6, 3)
 CHUNK = 256
-LEAD = 2
-TRAIL = 1
 
 
 def score_unit(q_t, keys, c, h):
@@ -67,18 +67,19 @@
     units = [(c, h) for c in range(q_t.shape[1] // CHUNK) for h in range(HEADS)]
     tops = {}
     n = len(units)
-    slots = n + LEAD + TRAIL
+    lead, trail = len(scores) - 1, len(weights) - 1
+    slots = n + lead + trail
     done = 0
     for u in range(slots):
         if u < n:
             s = score_unit(q_t, keys, *units[u])
             tops[u] = jnp.max(s, axis=0, keepdims=True)
             scores[u % len(scores)][...] = s
-        v = u - LEAD
+        v = u - lead
         if 0 <= v < n:
             s = scores[v % len(scores)][...]
             weights[v % len(weights)][...] = jnp.exp2(s - tops.pop(v)).astype(BF16)
-        w = v - TRAIL
+        w = v - trail
         if 0 <= w < n:
             c, h = units[w]
             mixed = dot(vaug[h * AUG : (h + 1) * AUG, :], weights[w % len(weights)][...])
@@ -133,11 +134,12 @@
     return [first] + [functools.partial(up, j) for j in range(FF // D)] + [down]
 
 
-def layer_steps(pairs, get, emit, finish, near_ref, far_ref, gain_ref, wq_ref, wk_ref, wv_ref, wo_ref, wup_ref, wdn_ref,
+def layer_steps(pairs, lead, get, emit, finish, near_ref, far_ref, gain_ref, wq_ref, wk_ref, wv_ref, wo_ref, wup_ref, wdn_ref,
                 wq_t, wv_t, wo_t, wup_t, wdn_t, pos, g1, g2, n1, n2, hidden, sums, *bufs):
     length = pos.shape[1]
     slots = (bufs[0:5], bufs[5:10])
-    ctx, scores, weights = bufs[10], bufs[11 : 12 + LEAD], bufs[12 + LEAD :]
+    ctx = bufs[10]
+    scores, weights = bufs[11 : 12 + lead], bufs[12 + lead :]
     step, last = pl.program_id(0), pairs
 
     def run(sub, a, b, c):
@@ -214,7 +216,7 @@
     return jnp.concatenate([tile, jnp.zeros_like(tile)], axis=1).astype(BF16)
 
 
-def layer_scratch(length):
+def layer_scratch(length, lead, trail):
     slot = [
         pltpu.VMEM((D, length), F32), pltpu.VMEM((D, length), BF16), pltpu.VMEM((length, D), BF16),
         pltpu.VMEM((HEADS * AUG, length), BF16), pltpu.VMEM((D, length), F32),
@@ -225,7 +227,7 @@
         pltpu.VMEM((D, length), F32), pltpu.VMEM((D, 128), F32), pltpu.VMEM((D, 128), F32),
         pltpu.VMEM((D, length), BF16), pltpu.VMEM((D, length), BF16), pltpu.VMEM((FF, length), BF16),
         pltpu.VMEM((2, 8, 128), F32), *slot, *slot, pltpu.VMEM((D, length), BF16),
-        *[pltpu.VMEM((length, CHUNK), F32)] * (LEAD + 1), *[pltpu.VMEM((length, CHUNK), BF16)] * (TRAIL + 1),
+        *[pltpu.VMEM((length, CHUNK), F32)] * (lead + 1), *[pltpu.VMEM((length, CHUNK), BF16)] * (trail + 1),
     ]
 
 
@@ -249,7 +251,7 @@
             row = jnp.concatenate([jnp.sum(work[11][k], axis=0, keepdims=True) for k in range(2)], axis=1)
             stat_ref[...] = jnp.broadcast_to(row[None], stat_ref.shape)
 
-        layer_steps(pairs, lambda sub: x_ref[sub], emit, finish, *consts, *work)
+        layer_steps(pairs, INTRA_AHEAD[0], lambda sub: x_ref[sub], emit, finish, *consts, *work)
 
     return pl.pallas_call(
         kernel,
@@ -258,7 +260,7 @@
                   whole(near), whole(far), pick(gain)] + [pick(w) for w in weights],
         out_specs=[VMEM_SPEC, VMEM_SPEC],
         out_shape=[jax.ShapeDtypeStruct(mixture.shape, BF16), jax.ShapeDtypeStruct((peers, 1, 256), F32)],
-        scratch_shapes=layer_scratch(frames),
+        scratch_shapes=layer_scratch(frames, *INTRA_AHEAD),
         compiler_params=LAYER_PARAMS,
         name="intra",
     )(*in_hbm((mixture, jnp.asarray(near), jnp.asarray(far), gain, *weights)))
@@ -283,7 +285,7 @@
         def finish():
             y_ref[:, rows:, :] = jnp.broadcast_to(stat_rows(work[11], 8)[None], (peers, 8, D))
 
-        layer_steps(pairs, get, emit, finish, near_ref, far_ref, gain_ref.at[1], *weights_refs, *work)
+        layer_steps(pairs, INTER_AHEAD[0], get, emit, finish, near_ref, far_ref, gain_ref.at[1], *weights_refs, *work)
 
     return pl.pallas_call(
         kernel,
@@ -291,7 +293,7 @@
         in_specs=[VMEM_SPEC] * 10,
         out_specs=VMEM_SPEC,
         out_shape=jax.ShapeDtypeStruct((peers, rows + 8, D), BF16),
-        scratch_shapes=layer_scratch(total),
+        scratch_shapes=layer_scratch(total, *INTER_AHEAD),
         compiler_params=LAYER_PARAMS,
         name="inter",
     )(*in_vmem(moved, jnp.asarray(near), jnp.asarray(far), gain, *weights))

time: 136 us -> 133 us (0.978)
  Pallas kernels: 54.4 us -> 50.5 us
    pallas_call x1, Pallas kernels: 27.3 us -> 24.3 us  [inter_layer(): pl.pallas_call(kernel, grid=(pairs + 1,), in_specs=[VMEM_SPEC] * 10, out_...]
where the time goes in v8:
time: 133 us; the launch traced here: 132 us
  blocking collectives  81.4 us (61%)
  Pallas kernels  50.5 us (38%)
    all_to_all x1, blocking collectives, body(): lax.all_to_all(inter, 'span', split_axis=0, concat_axis=0, tiled=True)  33.9 us
    all_to_all x1, blocking collectives, body(): lax.all_to_all(across.reshape(shards, own, segs, D), 'span', split_axis=0...  31.9 us
    pallas_call x1, Pallas kernels, inter_layer(): pl.pallas_call(kernel, grid=(pairs + 1,), in_specs=[VMEM_SPEC] * 10, out_...  24.3 us
    pallas_call x1, Pallas kernels, intra_layer(): pl.pallas_call(kernel, grid=(pairs + 1,), in_specs=[pl.BlockSpec((2, fram...  22.1 us
    all_to_all x1, blocking collectives, body(): stat = lax.all_to_all(stat, 'span', split_axis=0, concat_axis=0, tiled=True)  15.7 us

profile of v8, /device:TPU:1, one launch (start us, length us, event | category | flops | bytes accessed | tf_op | source)
XLA Modules:
  0.0 132.3 jit_solution(16379973401112125928)
XLA Ops:
  0.0 0.0 copy-start
  0.0 0.0 copy-start.11
  0.0 0.0 copy-start.10
  0.0 22.1 %intra.1 = (bf16[16,256,256]{2,1,0:T(8,128)(2,1)S(1)}, f32[32,1,256]{2,1,0:T(1,128)S(1)}) custom-call(bf16[16,256,256]{2,1,0:T(8,128)(2,1)} %x_ref.3, f32[2,256,128]{2,1,0:T(8,128)} %constant.4.clone.refs_0_.near_ref, f32[8,512]{1,0:T(8,128)} %constant.5.clone.refs_1_.far_ref, f32[2,2,256]{2,1,0:T(2,128)} %gain_ref.4, bf16[2,256,256]{2,1,0:T(8,128)(2,1)} %refs_0_.2, ...), custom_call_target="tpu_custom_call" | custom-call | tf_op jit(solution)/shard_map/intra/pallas_call | solution.py:256
  22.1 15.7 %all_to_all.15.stat_ref = f32[32,1,256]{2,1,0:T(1,128)S(1)} all-to-all(f32[32,1,256]{2,1,0:T(1,128)S(1)} %get-tuple-element.7), channel_id=1, replica_groups=mesh['mix'=4,'span'=32] {'span'}, dimensions={0} | all-to-all | bytes 65536 | tf_op jit(solution)/shard_map/all_to_all | solution.py:389
  37.8 0.0 copy-done
  37.8 0.0 copy-done.11
  37.8 0.0 copy-done.10
  37.8 1.6 %blend_intra.1.res_ref = bf16[256,16,256]{2,1,0:T(8,128)(2,1)S(1)} custom-call(f32[32,1,256]{2,1,0:T(1,128)S(1)} %all_to_all.15.stat_ref, bf16[16,256,256]{2,1,0:T(8,128)(2,1)S(1)} %get-tuple-element.8.y_ref, bf16[16,256,256]{2,1,0:T(8,128)(2,1)S(1)} %copy-done, f32[2,256]{1,0:T(2,128)S(1)} %copy-done.10, f32[2,256]{1,0:T(2,128)S(1)} %copy-done.11), custom_call_target="tpu_custom_call" | custom-call | tf_op jit(solution)/shard_map/blend_intra/pallas_call | solution.py:325
  39.4 0.0 copy-start.1
  39.5 0.0 copy-start.2
  39.5 0.0 copy-start.3
  39.5 0.0 copy-start.4
  39.5 0.0 copy-start.5
  39.5 0.0 copy-start.6
  39.5 0.0 copy-start.7
  39.5 0.0 copy-start.8
  39.5 0.0 copy-start.9
  39.5 31.9 %all_to_all.16.x_ref = bf16[32,8,16,256]{3,2,1,0:T(8,128)(2,1)S(1)} all-to-all(bf16[32,8,16,256]{3,2,1,0:T(8,128)(2,1)S(1)} %bitcast.1), channel_id=1, replica_groups=mesh['mix'=4,'span'=32] {'span'}, dimensions={0} | all-to-all | bytes 4194304 | tf_op jit(solution)/shard_map/all_to_all | solution.py:391
  71.4 0.0 copy-done.1
  71.4 0.0 copy-done.2
  71.4 0.0 copy-done.3
  71.4 0.0 copy-done.4
  71.4 0.0 copy-done.5
  71.5 0.0 copy-done.6
  71.5 0.0 copy-done.7
  71.5 0.0 copy-done.8
  71.5 0.0 copy-done.9
  71.5 24.3 %inter.1 = bf16[32,136,256]{2,1,0:T(8,128)(2,1)S(1)} custom-call(bf16[32,8,16,256]{3,2,1,0:T(8,128)(2,1)S(1)} %all_to_all.16.x_ref, f32[2,256,128]{2,1,0:T(8,128)S(1)} %copy-done.7, f32[8,512]{1,0:T(8,128)S(1)} %copy-done.8, f32[2,2,256]{2,1,0:T(2,128)S(1)} %copy-done.9, bf16[2,256,256]{2,1,0:T(8,128)(2,1)S(1)} %copy-done.3, ...), custom_call_target="tpu_custom_call" | custom-call | tf_op jit(solution)/shard_map/inter/pallas_call | solution.py:290
  95.8 33.9 %all_to_all.17.back_ref = bf16[32,136,256]{2,1,0:T(8,128)(2,1)S(1)} all-to-all(bf16[32,136,256]{2,1,0:T(8,128)(2,1)S(1)} %inter.1), channel_id=1, replica_groups=mesh['mix'=4,'span'=32] {'span'}, dimensions={0} | all-to-all | bytes 4456448 | tf_op jit(solution)/shard_map/all_to_all | solution.py:394
  129.7 2.5 %blend_inter.1 = bf16[16,256,256]{2,1,0:T(8,128)(2,1)} custom-call(bf16[32,136,256]{2,1,0:T(8,128)(2,1)S(1)} %all_to_all.17.back_ref, bf16[256,16,256]{2,1,0:T(8,128)(2,1)S(1)} %blend_intra.1.res_ref, f32[2,256]{1,0:T(2,128)S(1)} %copy-done.10, f32[2,256]{1,0:T(2,128)S(1)} %copy-done.11), custom_call_target="tpu_custom_call" | custom-call | tf_op jit(solution)/shard_map/blend_inter/pallas_call | solution.py:368
Async XLA Ops:
  0.0 37.8 %copy-start = (bf16[16,256,256]{2,1,0:T(8,128)(2,1)S(1)}, bf16[16,256,256]{2,1,0:T(8,128)(2,1)}, u32[]{:S(2)}) copy-start(bf16[16,256,256]{2,1,0:T(8,128)(2,1)} %x_ref.3) | copy-start | bytes 6291460
  0.0 37.8 %copy-start.11 = (f32[2,256]{1,0:T(2,128)S(1)}, f32[2,256]{1,0:T(2,128)}, u32[]{:S(2)}) copy-start(f32[2,256]{1,0:T(2,128)} %bias_ref.3) | copy-start | bytes 6148
  0.0 37.8 %copy-start.10 = (f32[2,256]{1,0:T(2,128)S(1)}, f32[2,256]{1,0:T(2,128)}, u32[]{:S(2)}) copy-start(f32[2,256]{1,0:T(2,128)} %gain_ref.5) | copy-start | bytes 6148
  39.4 32.0 %copy-start.1 = (bf16[2,256,1024]{2,1,0:T(8,128)(2,1)S(1)}, bf16[2,256,1024]{2,1,0:T(8,128)(2,1)}, u32[]{:S(2)}) copy-start(bf16[2,256,1024]{2,1,0:T(8,128)(2,1)} %refs_4_.3) | copy-start | bytes 3145732
  39.5 32.0 %copy-start.2 = (bf16[2,1024,256]{2,1,0:T(8,128)(2,1)S(1)}, bf16[2,1024,256]{2,1,0:T(8,128)(2,1)}, u32[]{:S(2)}) copy-start(bf16[2,1024,256]{2,1,0:T(8,128)(2,1)} %refs_5_.3) | copy-start | bytes 3145732
  39.5 32.0 %copy-start.3 = (bf16[2,256,256]{2,1,0:T(8,128)(2,1)S(1)}, bf16[2,256,256]{2,1,0:T(8,128)(2,1)}, u32[]{:S(2)}) copy-start(bf16[2,256,256]{2,1,0:T(8,128)(2,1)} %refs_0_.2) | copy-start | bytes 786436
  39.5 32.0 %copy-start.4 = (bf16[2,256,256]{2,1,0:T(8,128)(2,1)S(1)}, bf16[2,256,256]{2,1,0:T(8,128)(2,1)}, u32[]{:S(2)}) copy-start(bf16[2,256,256]{2,1,0:T(8,128)(2,1)} %refs_1_.2) | copy-start | bytes 786436
  39.5 32.0 %copy-start.5 = (bf16[2,256,256]{2,1,0:T(8,128)(2,1)S(1)}, bf16[2,256,256]{2,1,0:T(8,128)(2,1)}, u32[]{:S(2)}) copy-start(bf16[2,256,256]{2,1,0:T(8,128)(2,1)} %refs_2_.3) | copy-start | bytes 786436
  39.5 32.0 %copy-start.6 = (bf16[2,256,256]{2,1,0:T(8,128)(2,1)S(1)}, bf16[2,256,256]{2,1,0:T(8,128)(2,1)}, u32[]{:S(2)}) copy-start(bf16[2,256,256]{2,1,0:T(8,128)(2,1)} %refs_3_.3) | copy-start | bytes 786436
  39.5 32.0 %copy-start.7 = (f32[2,256,128]{2,1,0:T(8,128)S(1)}, f32[2,256,128]{2,1,0:T(8,128)}, u32[]{:S(2)}) copy-start(f32[2,256,128]{2,1,0:T(8,128)} %constant.4.clone.refs_0_.near_ref) | copy-start | bytes 786436
  39.5 32.0 %copy-start.8 = (f32[8,512]{1,0:T(8,128)S(1)}, f32[8,512]{1,0:T(8,128)}, u32[]{:S(2)}) copy-start(f32[8,512]{1,0:T(8,128)} %constant.5.clone.refs_1_.far_ref) | copy-start | bytes 49156
  39.5 32.0 %copy-start.9 = (f32[2,2,256]{2,1,0:T(2,128)S(1)}, f32[2,2,256]{2,1,0:T(2,128)}, u32[]{:S(2)}) copy-start(f32[2,2,256]{2,1,0:T(2,128)} %gain_ref.4) | copy-start | bytes 12292

commit v9 on v8

--- a/solution.py
+++ b/solution.py
@@ -42,8 +42,8 @@
     return shifted * lax.rsqrt(spread + EPS) * gain
 
 
-INTRA_AHEAD = (4, 2)
-INTER_AHEAD = (6, 3)
+INTRA_AHEAD = (5, 2)
+INTER_AHEAD = (7, 3)
 CHUNK = 256
 
 
@@ -120,7 +120,7 @@
 
     def up(j):
         rows = slice(j * D, (j + 1) * D)
-        hidden[rows, :] = jnp.maximum(dot(wup_t[rows, :], n2[...]), 0.0).astype(BF16)
+        hidden[rows, :] = jnp.maximum(dot(wup_t[rows, :], n2[...]).astype(BF16), 0)
 
     def down():
         y_t = after[...] + dot(wdn_t[...], hidden[...])
@@ -134,16 +134,16 @@
     return [first] + [functools.partial(up, j) for j in range(FF // D)] + [down]
 
 
-def layer_steps(pairs, lead, get, emit, finish, near_ref, far_ref, gain_ref, wq_ref, wk_ref, wv_ref, wo_ref, wup_ref, wdn_ref,
+def layer_steps(steps, group, lead, get, emit, finish, near_ref, far_ref, gain_ref, wq_ref, wk_ref, wv_ref, wo_ref, wup_ref, wdn_ref,
                 wq_t, wv_t, wo_t, wup_t, wdn_t, pos, g1, g2, n1, n2, hidden, sums, *bufs):
     length = pos.shape[1]
     slots = (bufs[0:5], bufs[5:10])
     ctx = bufs[10]
     scores, weights = bufs[11 : 12 + lead], bufs[12 + lead :]
-    step, last = pl.program_id(0), pairs
+    step, last = pl.program_id(0), steps
 
     def run(sub, a, b, c):
-        here, other = slots[sub], slots[1 - sub]
+        here, other = slots[sub % 2], slots[1 - sub % 2]
         left, right = [], []
         if c:
             left = pieces_c(here[4], g2[:, :1], wup_t, wdn_t, functools.partial(emit, sub), sums, n2, hidden)
@@ -170,13 +170,13 @@
         for slot in slots:
             slot[3][...] = jnp.ones_like(slot[3])
         sums[...] = jnp.zeros_like(sums)
-        run(0, True, False, False)
-        run(1, True, True, False)
+        for sub in range(group):
+            run(sub, True, sub >= 1, sub >= 2)
 
     @pl.when((step > 0) & (step < last))
     def _():
-        run(0, True, True, True)
-        run(1, True, True, True)
+        for sub in range(group):
+            run(sub, True, True, True)
 
     @pl.when(step == last)
     def _():
@@ -236,7 +236,7 @@
 
 def intra_layer(mixture, gain, weights, peers):
     segs, frames, _ = mixture.shape
-    pairs = segs // 2
+    group = 4
     near, far = pos_parts(frames)
     pick = lambda a: pl.BlockSpec((None, *a.shape[1:]), lambda i: (0,) * a.ndim)
     whole = lambda a: pl.BlockSpec(a.shape, lambda i: (0,) * a.ndim)
@@ -245,18 +245,18 @@
         consts, (y_ref, stat_ref), work = refs[:9], refs[9:11], refs[11:]
 
         def emit(sub, y):
-            y_ref[pl.program_id(0) * 2 - 2 + sub] = y
+            y_ref[pl.program_id(0) * group - 2 + sub] = y
 
         def finish():
             row = jnp.concatenate([jnp.sum(work[11][k], axis=0, keepdims=True) for k in range(2)], axis=1)
             stat_ref[...] = jnp.broadcast_to(row[None], stat_ref.shape)
 
-        layer_steps(pairs, INTRA_AHEAD[0], lambda sub: x_ref[sub], emit, finish, *consts, *work)
+        layer_steps(segs // group, group, INTRA_AHEAD[0], lambda sub: x_ref[sub], emit, finish, *consts, *work)
 
     return pl.pallas_call(
         kernel,
-        grid=(pairs + 1,),
-        in_specs=[pl.BlockSpec((2, frames, D), lambda i: (jnp.minimum(i, pairs - 1), 0, 0)),
+        grid=(segs // group + 1,),
+        in_specs=[pl.BlockSpec((group, frames, D), lambda i: (jnp.minimum(i, segs // group - 1), 0, 0)),
                   whole(near), whole(far), pick(gain)] + [pick(w) for w in weights],
         out_specs=[VMEM_SPEC, VMEM_SPEC],
         out_shape=[jax.ShapeDtypeStruct(mixture.shape, BF16), jax.ShapeDtypeStruct((peers, 1, 256), F32)],
@@ -285,7 +285,7 @@
         def finish():
             y_ref[:, rows:, :] = jnp.broadcast_to(stat_rows(work[11], 8)[None], (peers, 8, D))
 
-        layer_steps(pairs, INTER_AHEAD[0], get, emit, finish, near_ref, far_ref, gain_ref.at[1], *weights_refs, *work)
+        layer_steps(pairs, 2, INTER_AHEAD[0], get, emit, finish, near_ref, far_ref, gain_ref.at[1], *weights_refs, *work)
 
     return pl.pallas_call(
         kernel,

time: 133 us -> 131 us (0.985)
    pallas_call x1, Pallas kernels: 22.1 us -> 20.7 us  [intra_layer(): pl.pallas_call(kernel, grid=(segs // group + 1,), in_specs=[pl.BlockSpec(...]
where the time goes in v9:
time: 131 us
  blocking collectives  81.4 us (62%)
  Pallas kernels  49.2 us (38%)
    all_to_all x1, blocking collectives, body(): lax.all_to_all(inter, 'span', split_axis=0, concat_axis=0, tiled=True)  33.9 us
    all_to_all x1, blocking collectives, body(): lax.all_to_all(across.reshape(shards, own, segs, D), 'span', split_axis=0...  31.9 us
    pallas_call x1, Pallas kernels, inter_layer(): pl.pallas_call(kernel, grid=(pairs + 1,), in_specs=[VMEM_SPEC] * 10, out_...  24.4 us
    pallas_call x1, Pallas kernels, intra_layer(): pl.pallas_call(kernel, grid=(segs // group + 1,), in_specs=[pl.BlockSpec(...  20.7 us
    all_to_all x1, blocking collectives, body(): stat = lax.all_to_all(stat, 'span', split_axis=0, concat_axis=0, tiled=True)  15.7 us

profile of v9, /device:TPU:1, one launch (start us, length us, event | category | flops | bytes accessed | tf_op | source)
XLA Modules:
  0.0 131.0 jit_solution(4852987204406178942)
XLA Ops:
  0.0 0.0 copy-start
  0.0 0.0 copy-start.11
  0.0 0.0 copy-start.10
  0.0 20.7 %intra.1 = (bf16[16,256,256]{2,1,0:T(8,128)(2,1)S(1)}, f32[32,1,256]{2,1,0:T(1,128)S(1)}) custom-call(bf16[16,256,256]{2,1,0:T(8,128)(2,1)} %x_ref.3, f32[2,256,128]{2,1,0:T(8,128)} %constant.4.clone.refs_0_.near_ref, f32[8,512]{1,0:T(8,128)} %constant.5.clone.refs_1_.far_ref, f32[2,2,256]{2,1,0:T(2,128)} %gain_ref.4, bf16[2,256,256]{2,1,0:T(8,128)(2,1)} %refs_0_.2, ...), custom_call_target="tpu_custom_call" | custom-call | tf_op jit(solution)/shard_map/intra/pallas_call | solution.py:256
  20.7 15.7 %all_to_all.15.stat_ref = f32[32,1,256]{2,1,0:T(1,128)S(1)} all-to-all(f32[32,1,256]{2,1,0:T(1,128)S(1)} %get-tuple-element.7), channel_id=1, replica_groups=mesh['mix'=4,'span'=32] {'span'}, dimensions={0} | all-to-all | bytes 65536 | tf_op jit(solution)/shard_map/all_to_all | solution.py:389
  36.4 0.0 copy-done
  36.4 0.0 copy-done.11
  36.4 0.0 copy-done.10
  36.4 1.6 %blend_intra.1.res_ref = bf16[256,16,256]{2,1,0:T(8,128)(2,1)S(1)} custom-call(f32[32,1,256]{2,1,0:T(1,128)S(1)} %all_to_all.15.stat_ref, bf16[16,256,256]{2,1,0:T(8,128)(2,1)S(1)} %get-tuple-element.8.y_ref, bf16[16,256,256]{2,1,0:T(8,128)(2,1)S(1)} %copy-done, f32[2,256]{1,0:T(2,128)S(1)} %copy-done.10, f32[2,256]{1,0:T(2,128)S(1)} %copy-done.11), custom_call_target="tpu_custom_call" | custom-call | tf_op jit(solution)/shard_map/blend_intra/pallas_call | solution.py:325
  38.0 0.0 copy-start.1
  38.0 0.0 copy-start.2
  38.1 0.0 copy-start.3
  38.1 0.0 copy-start.4
  38.1 0.0 copy-start.5
  38.1 0.0 copy-start.6
  38.1 0.0 copy-start.7
  38.1 0.0 copy-start.8
  38.1 0.0 copy-start.9
  38.1 31.9 %all_to_all.16.x_ref = bf16[32,8,16,256]{3,2,1,0:T(8,128)(2,1)S(1)} all-to-all(bf16[32,8,16,256]{3,2,1,0:T(8,128)(2,1)S(1)} %bitcast.1), channel_id=1, replica_groups=mesh['mix'=4,'span'=32] {'span'}, dimensions={0} | all-to-all | bytes 4194304 | tf_op jit(solution)/shard_map/all_to_all | solution.py:391
  70.0 0.0 copy-done.1
  70.0 0.0 copy-done.2
  70.0 0.0 copy-done.3
  70.0 0.0 copy-done.4
  70.0 0.0 copy-done.5
  70.0 0.0 copy-done.6
  70.1 0.0 copy-done.7
  70.1 0.0 copy-done.8
  70.1 0.0 copy-done.9
  70.1 24.4 %inter.1 = bf16[32,136,256]{2,1,0:T(8,128)(2,1)S(1)} custom-call(bf16[32,8,16,256]{3,2,1,0:T(8,128)(2,1)S(1)} %all_to_all.16.x_ref, f32[2,256,128]{2,1,0:T(8,128)S(1)} %copy-done.7, f32[8,512]{1,0:T(8,128)S(1)} %copy-done.8, f32[2,2,256]{2,1,0:T(2,128)S(1)} %copy-done.9, bf16[2,256,256]{2,1,0:T(8,128)(2,1)S(1)} %copy-done.3, ...), custom_call_target="tpu_custom_call" | custom-call | tf_op jit(solution)/shard_map/inter/pallas_call | solution.py:290
  94.5 33.9 %all_to_all.17.back_ref = bf16[32,136,256]{2,1,0:T(8,128)(2,1)S(1)} all-to-all(bf16[32,136,256]{2,1,0:T(8,128)(2,1)S(1)} %inter.1), channel_id=1, replica_groups=mesh['mix'=4,'span'=32] {'span'}, dimensions={0} | all-to-all | bytes 4456448 | tf_op jit(solution)/shard_map/all_to_all | solution.py:394
  128.4 2.5 %blend_inter.1 = bf16[16,256,256]{2,1,0:T(8,128)(2,1)} custom-call(bf16[32,136,256]{2,1,0:T(8,128)(2,1)S(1)} %all_to_all.17.back_ref, bf16[256,16,256]{2,1,0:T(8,128)(2,1)S(1)} %blend_intra.1.res_ref, f32[2,256]{1,0:T(2,128)S(1)} %copy-done.10, f32[2,256]{1,0:T(2,128)S(1)} %copy-done.11), custom_call_target="tpu_custom_call" | custom-call | tf_op jit(solution)/shard_map/blend_inter/pallas_call | solution.py:368
Async XLA Ops:
  0.0 36.4 %copy-start = (bf16[16,256,256]{2,1,0:T(8,128)(2,1)S(1)}, bf16[16,256,256]{2,1,0:T(8,128)(2,1)}, u32[]{:S(2)}) copy-start(bf16[16,256,256]{2,1,0:T(8,128)(2,1)} %x_ref.3) | copy-start | bytes 6291460
  0.0 36.4 %copy-start.11 = (f32[2,256]{1,0:T(2,128)S(1)}, f32[2,256]{1,0:T(2,128)}, u32[]{:S(2)}) copy-start(f32[2,256]{1,0:T(2,128)} %bias_ref.3) | copy-start | bytes 6148
  0.0 36.4 %copy-start.10 = (f32[2,256]{1,0:T(2,128)S(1)}, f32[2,256]{1,0:T(2,128)}, u32[]{:S(2)}) copy-start(f32[2,256]{1,0:T(2,128)} %gain_ref.5) | copy-start | bytes 6148
  38.0 32.0 %copy-start.1 = (bf16[2,256,1024]{2,1,0:T(8,128)(2,1)S(1)}, bf16[2,256,1024]{2,1,0:T(8,128)(2,1)}, u32[]{:S(2)}) copy-start(bf16[2,256,1024]{2,1,0:T(8,128)(2,1)} %refs_4_.3) | copy-start | bytes 3145732
  38.0 32.0 %copy-start.2 = (bf16[2,1024,256]{2,1,0:T(8,128)(2,1)S(1)}, bf16[2,1024,256]{2,1,0:T(8,128)(2,1)}, u32[]{:S(2)}) copy-start(bf16[2,1024,256]{2,1,0:T(8,128)(2,1)} %refs_5_.3) | copy-start | bytes 3145732
  38.1 32.0 %copy-start.3 = (bf16[2,256,256]{2,1,0:T(8,128)(2,1)S(1)}, bf16[2,256,256]{2,1,0:T(8,128)(2,1)}, u32[]{:S(2)}) copy-start(bf16[2,256,256]{2,1,0:T(8,128)(2,1)} %refs_0_.2) | copy-start | bytes 786436
  38.1 32.0 %copy-start.4 = (bf16[2,256,256]{2,1,0:T(8,128)(2,1)S(1)}, bf16[2,256,256]{2,1,0:T(8,128)(2,1)}, u32[]{:S(2)}) copy-start(bf16[2,256,256]{2,1,0:T(8,128)(2,1)} %refs_1_.2) | copy-start | bytes 786436
  38.1 32.0 %copy-start.5 = (bf16[2,256,256]{2,1,0:T(8,128)(2,1)S(1)}, bf16[2,256,256]{2,1,0:T(8,128)(2,1)}, u32[]{:S(2)}) copy-start(bf16[2,256,256]{2,1,0:T(8,128)(2,1)} %refs_2_.3) | copy-start | bytes 786436
  38.1 32.0 %copy-start.6 = (bf16[2,256,256]{2,1,0:T(8,128)(2,1)S(1)}, bf16[2,256,256]{2,1,0:T(8,128)(2,1)}, u32[]{:S(2)}) copy-start(bf16[2,256,256]{2,1,0:T(8,128)(2,1)} %refs_3_.3) | copy-start | bytes 786436
  38.1 32.0 %copy-start.7 = (f32[2,256,128]{2,1,0:T(8,128)S(1)}, f32[2,256,128]{2,1,0:T(8,128)}, u32[]{:S(2)}) copy-start(f32[2,256,128]{2,1,0:T(8,128)} %constant.4.clone.refs_0_.near_ref) | copy-start | bytes 786436
  38.1 32.0 %copy-start.8 = (f32[8,512]{1,0:T(8,128)S(1)}, f32[8,512]{1,0:T(8,128)}, u32[]{:S(2)}) copy-start(f32[8,512]{1,0:T(8,128)} %constant.5.clone.refs_1_.far_ref) | copy-start | bytes 49156
  38.1 32.0 %copy-start.9 = (f32[2,2,256]{2,1,0:T(2,128)S(1)}, f32[2,2,256]{2,1,0:T(2,128)}, u32[]{:S(2)}) copy-start(f32[2,2,256]{2,1,0:T(2,128)} %gain_ref.4) | copy-start | bytes 12292

commit v10 on v9

--- a/solution.py
+++ b/solution.py
@@ -336,7 +336,7 @@
 def blend_inter(back, across, gain, bias, cells, own):
     frames, segs, _ = across.shape
     peers, rows, _ = back.shape
-    width = 64
+    width = 32
     pitch, count, steps = segs + 8, width // own, frames // width
 
     def kernel(back_ref, res_ref, gain_ref, bias_ref, out_ref, stage, sem, *parts):

time: 131 us -> 131 us (level)
  no operation moved by 1% of the time
where the time goes in v10:
time: 131 us
  blocking collectives  81.4 us (62%)
  Pallas kernels  49.1 us (37%)
    all_to_all x1, blocking collectives, body(): lax.all_to_all(inter, 'span', split_axis=0, concat_axis=0, tiled=True)  33.9 us
    all_to_all x1, blocking collectives, body(): lax.all_to_all(across.reshape(shards, own, segs, D), 'span', split_axis=0...  31.9 us
    pallas_call x1, Pallas kernels, inter_layer(): pl.pallas_call(kernel, grid=(pairs + 1,), in_specs=[VMEM_SPEC] * 10, out_...  24.4 us
    pallas_call x1, Pallas kernels, intra_layer(): pl.pallas_call(kernel, grid=(segs // group + 1,), in_specs=[pl.BlockSpec(...  20.7 us
    all_to_all x1, blocking collectives, body(): stat = lax.all_to_all(stat, 'span', split_axis=0, concat_axis=0, tiled=True)  15.7 us

profile of v10, /device:TPU:1, one launch (start us, length us, event | category | flops | bytes accessed | tf_op | source)
XLA Modules:
  0.0 130.9 jit_solution(13463925718180537361)
XLA Ops:
  0.0 0.0 copy-start
  0.0 0.0 copy-start.11
  0.0 0.0 copy-start.10
  0.0 20.7 %intra.1 = (bf16[16,256,256]{2,1,0:T(8,128)(2,1)S(1)}, f32[32,1,256]{2,1,0:T(1,128)S(1)}) custom-call(bf16[16,256,256]{2,1,0:T(8,128)(2,1)} %x_ref.3, f32[2,256,128]{2,1,0:T(8,128)} %constant.4.clone.refs_0_.near_ref, f32[8,512]{1,0:T(8,128)} %constant.5.clone.refs_1_.far_ref, f32[2,2,256]{2,1,0:T(2,128)} %gain_ref.4, bf16[2,256,256]{2,1,0:T(8,128)(2,1)} %refs_0_.2, ...), custom_call_target="tpu_custom_call" | custom-call | tf_op jit(solution)/shard_map/intra/pallas_call | solution.py:256
  20.7 15.7 %all_to_all.15.stat_ref = f32[32,1,256]{2,1,0:T(1,128)S(1)} all-to-all(f32[32,1,256]{2,1,0:T(1,128)S(1)} %get-tuple-element.7), channel_id=1, replica_groups=mesh['mix'=4,'span'=32] {'span'}, dimensions={0} | all-to-all | bytes 65536 | tf_op jit(solution)/shard_map/all_to_all | solution.py:389
  36.4 0.0 copy-done
  36.4 0.0 copy-done.11
  36.4 0.0 copy-done.10
  36.4 1.6 %blend_intra.1.res_ref = bf16[256,16,256]{2,1,0:T(8,128)(2,1)S(1)} custom-call(f32[32,1,256]{2,1,0:T(1,128)S(1)} %all_to_all.15.stat_ref, bf16[16,256,256]{2,1,0:T(8,128)(2,1)S(1)} %get-tuple-element.8.y_ref, bf16[16,256,256]{2,1,0:T(8,128)(2,1)S(1)} %copy-done, f32[2,256]{1,0:T(2,128)S(1)} %copy-done.10, f32[2,256]{1,0:T(2,128)S(1)} %copy-done.11), custom_call_target="tpu_custom_call" | custom-call | tf_op jit(solution)/shard_map/blend_intra/pallas_call | solution.py:325
  38.0 0.0 copy-start.1
  38.0 0.0 copy-start.2
  38.1 0.0 copy-start.3
  38.1 0.0 copy-start.4
  38.1 0.0 copy-start.5
  38.1 0.0 copy-start.6
  38.1 0.0 copy-start.7
  38.1 0.0 copy-start.8
  38.1 0.0 copy-start.9
  38.1 31.9 %all_to_all.16.x_ref = bf16[32,8,16,256]{3,2,1,0:T(8,128)(2,1)S(1)} all-to-all(bf16[32,8,16,256]{3,2,1,0:T(8,128)(2,1)S(1)} %bitcast.1), channel_id=1, replica_groups=mesh['mix'=4,'span'=32] {'span'}, dimensions={0} | all-to-all | bytes 4194304 | tf_op jit(solution)/shard_map/all_to_all | solution.py:391
  70.0 0.0 copy-done.1
  70.0 0.0 copy-done.2
  70.0 0.0 copy-done.3
  70.0 0.0 copy-done.4
  70.0 0.0 copy-done.5
  70.0 0.0 copy-done.6
  70.1 0.0 copy-done.7
  70.1 0.0 copy-done.8
  70.1 0.0 copy-done.9
  70.1 24.4 %inter.1 = bf16[32,136,256]{2,1,0:T(8,128)(2,1)S(1)} custom-call(bf16[32,8,16,256]{3,2,1,0:T(8,128)(2,1)S(1)} %all_to_all.16.x_ref, f32[2,256,128]{2,1,0:T(8,128)S(1)} %copy-done.7, f32[8,512]{1,0:T(8,128)S(1)} %copy-done.8, f32[2,2,256]{2,1,0:T(2,128)S(1)} %copy-done.9, bf16[2,256,256]{2,1,0:T(8,128)(2,1)S(1)} %copy-done.3, ...), custom_call_target="tpu_custom_call" | custom-call | tf_op jit(solution)/shard_map/inter/pallas_call | solution.py:290
  94.5 33.9 %all_to_all.17.back_ref = bf16[32,136,256]{2,1,0:T(8,128)(2,1)S(1)} all-to-all(bf16[32,136,256]{2,1,0:T(8,128)(2,1)S(1)} %inter.1), channel_id=1, replica_groups=mesh['mix'=4,'span'=32] {'span'}, dimensions={0} | all-to-all | bytes 4456448 | tf_op jit(solution)/shard_map/all_to_all | solution.py:394
  128.4 2.4 %blend_inter.1 = bf16[16,256,256]{2,1,0:T(8,128)(2,1)} custom-call(bf16[32,136,256]{2,1,0:T(8,128)(2,1)S(1)} %all_to_all.17.back_ref, bf16[256,16,256]{2,1,0:T(8,128)(2,1)S(1)} %blend_intra.1.res_ref, f32[2,256]{1,0:T(2,128)S(1)} %copy-done.10, f32[2,256]{1,0:T(2,128)S(1)} %copy-done.11), custom_call_target="tpu_custom_call" | custom-call | tf_op jit(solution)/shard_map/blend_inter/pallas_call | solution.py:368
Async XLA Ops:
  0.0 36.4 %copy-start = (bf16[16,256,256]{2,1,0:T(8,128)(2,1)S(1)}, bf16[16,256,256]{2,1,0:T(8,128)(2,1)}, u32[]{:S(2)}) copy-start(bf16[16,256,256]{2,1,0:T(8,128)(2,1)} %x_ref.3) | copy-start | bytes 6291460
  0.0 36.4 %copy-start.11 = (f32[2,256]{1,0:T(2,128)S(1)}, f32[2,256]{1,0:T(2,128)}, u32[]{:S(2)}) copy-start(f32[2,256]{1,0:T(2,128)} %bias_ref.3) | copy-start | bytes 6148
  0.0 36.4 %copy-start.10 = (f32[2,256]{1,0:T(2,128)S(1)}, f32[2,256]{1,0:T(2,128)}, u32[]{:S(2)}) copy-start(f32[2,256]{1,0:T(2,128)} %gain_ref.5) | copy-start | bytes 6148
  38.0 32.0 %copy-start.1 = (bf16[2,256,1024]{2,1,0:T(8,128)(2,1)S(1)}, bf16[2,256,1024]{2,1,0:T(8,128)(2,1)}, u32[]{:S(2)}) copy-start(bf16[2,256,1024]{2,1,0:T(8,128)(2,1)} %refs_4_.3) | copy-start | bytes 3145732
  38.0 32.0 %copy-start.2 = (bf16[2,1024,256]{2,1,0:T(8,128)(2,1)S(1)}, bf16[2,1024,256]{2,1,0:T(8,128)(2,1)}, u32[]{:S(2)}) copy-start(bf16[2,1024,256]{2,1,0:T(8,128)(2,1)} %refs_5_.3) | copy-start | bytes 3145732
  38.1 32.0 %copy-start.3 = (bf16[2,256,256]{2,1,0:T(8,128)(2,1)S(1)}, bf16[2,256,256]{2,1,0:T(8,128)(2,1)}, u32[]{:S(2)}) copy-start(bf16[2,256,256]{2,1,0:T(8,128)(2,1)} %refs_0_.2) | copy-start | bytes 786436
  38.1 32.0 %copy-start.4 = (bf16[2,256,256]{2,1,0:T(8,128)(2,1)S(1)}, bf16[2,256,256]{2,1,0:T(8,128)(2,1)}, u32[]{:S(2)}) copy-start(bf16[2,256,256]{2,1,0:T(8,128)(2,1)} %refs_1_.2) | copy-start | bytes 786436
  38.1 32.0 %copy-start.5 = (bf16[2,256,256]{2,1,0:T(8,128)(2,1)S(1)}, bf16[2,256,256]{2,1,0:T(8,128)(2,1)}, u32[]{:S(2)}) copy-start(bf16[2,256,256]{2,1,0:T(8,128)(2,1)} %refs_2_.3) | copy-start | bytes 786436
  38.1 32.0 %copy-start.6 = (bf16[2,256,256]{2,1,0:T(8,128)(2,1)S(1)}, bf16[2,256,256]{2,1,0:T(8,128)(2,1)}, u32[]{:S(2)}) copy-start(bf16[2,256,256]{2,1,0:T(8,128)(2,1)} %refs_3_.3) | copy-start | bytes 786436
  38.1 32.0 %copy-start.7 = (f32[2,256,128]{2,1,0:T(8,128)S(1)}, f32[2,256,128]{2,1,0:T(8,128)}, u32[]{:S(2)}) copy-start(f32[2,256,128]{2,1,0:T(8,128)} %constant.4.clone.refs_0_.near_ref) | copy-start | bytes 786436
  38.1 32.0 %copy-start.8 = (f32[8,512]{1,0:T(8,128)S(1)}, f32[8,512]{1,0:T(8,128)}, u32[]{:S(2)}) copy-start(f32[8,512]{1,0:T(8,128)} %constant.5.clone.refs_1_.far_ref) | copy-start | bytes 49156
  38.1 32.0 %copy-start.9 = (f32[2,2,256]{2,1,0:T(2,128)S(1)}, f32[2,2,256]{2,1,0:T(2,128)}, u32[]{:S(2)}) copy-start(f32[2,2,256]{2,1,0:T(2,128)} %gain_ref.4) | copy-start | bytes 12292
